TPU v7x, 32 devices: a whole 2x2x4 slice. The times are simulated.
32 devices in a mesh: expert: 4 (over z), context: 8 (over y, x, core).
Axes of the slice: x: 2, y: 2, z: 4, core: 2. Of those that a mesh axis runs over, the one named last changes fastest.
Arguments:
- hidden_in: bfloat16 [4, 3072, 768], P('expert', 'context'), may hold values from -6 to 6
- prior_logits: float32 [4, 3072, 12], P('expert', 'context'), may hold values from -6 to 6
- routes: int32 [4, 3072, 2], P('expert', 'context'), may hold values from 0 to 11, all different within a row; in each aligned block of 384 rows (0 to 383, 384 to 767, ..., all dimensions but the last counted through in order) at most 96 rows name the same one
- block_ids: int32 [4, 3072], P('expert', 'context'), may hold values from 0 to 23, never falling along the last dimension, each value on 1 to 256 neighbouring positions
- grad_out: bfloat16 [4, 3072, 768], P('expert', 'context'), may hold values from -6 to 6
- attn_gain: float32 [768], replicated, may hold values from 0.25 to 1.75
- query_weight: bfloat16 [768, 768], P('context'), may hold values from -0.21875 to 0.21875
- key_weight: bfloat16 [768, 768], P('context'), may hold values from -0.21875 to 0.21875
- value_weight: bfloat16 [768, 768], P('context'), may hold values from -0.21875 to 0.21875
- output_weight: bfloat16 [768, 768], P('context'), may hold values from -0.875 to 0.875
- moe_gain: float32 [768], replicated, may hold values from 0.25 to 1.75
- router_weight: float32 [768, 12], replicated, may hold values from -0.109375 to 0.109375
- prior_weight: float32 [12, 12], replicated, may hold values from -0.875 to 0.875
- const_mix: float32 [2, 2, 768], replicated, may hold values from -0.21875 to 0.21875
- const_vector: float32 [2, 768], replicated, may hold values from -6 to 6
- gate_weight: bfloat16 [8, 768, 2048], P('expert', 'context'), may hold values from -0.21875 to 0.21875
- up_weight: bfloat16 [8, 768, 2048], P('expert', 'context'), may hold values from -0.21875 to 0.21875
- down_weight: bfloat16 [8, 2048, 768], P('expert', 'context'), may hold values from -1 to 1
Outputs:
- layer_out: bfloat16 [4, 3072, 768], P('expert', 'context')
- grad_input: float32 [4, 3072, 768], P('expert', 'context')
- grad_prior: float32 [4, 3072, 12], P('expert', 'context')
- grad_attn_gain: float32 [768], P('context')
- grad_query: float32 [768, 768], P('context')
- grad_key: float32 [768, 768], P('context')
- grad_value: float32 [768, 768], P('context')
- grad_output_weight: float32 [768, 768], P('context')
- grad_moe_gain: float32 [768], P('context')
- grad_router: float32 [768, 12], P('context')
- grad_prior_weight: float32 [12, 12], replicated
- grad_const_mix: float32 [2, 2, 768], P(None, None, 'context')
- grad_const_vector: float32 [2, 768], P(None, 'context')
- grad_gate: float32 [8, 768, 2048], P('expert', 'context')
- grad_up: float32 [8, 768, 2048], P('expert', 'context')
- grad_down: float32 [8, 2048, 768], P('expert', 'context')
Inputs may be any that keep to these rules, and one draw needn't show every extreme that they name: `routes`: each token names two different experts; experts 0 to 7 are feed-forward, 8 the zero expert, 9 the copy expert, the rest constant experts. Among the 384 positions of one device (aligned blocks of 384 positions of a sequence), no expert is named by more than 96 tokens, and in some block one is named by exactly 96. `block_ids`: along a sequence the block id never falls; each id covers 1 to 256 consecutive positions, and some id covers exactly 256.
All inputs are finite; a program needn't handle non-finite values.
Results may differ from a plain program's by a relative error of at most 0.017.
Values may be sent and summed in bfloat16 or wider, within the bound.
A program may use at most 384 MiB of HBM per device.

v0:
```python
import jax
import jax.numpy as jnp
from jax import lax
from jax.sharding import PartitionSpec as P

HEADS = 12
FFN_E = 8
CAP = 96


EPS = 1e-06
THETA = 10000.0
NEGATIVE = -1e30
HIGH = lax.Precision.HIGHEST


def rope_tables(positions, head_size):
    half = head_size // 2
    freq = jnp.power(THETA, -2.0 * jnp.arange(half, dtype=jnp.float32) / head_size)
    angle = positions.astype(jnp.float32)[:, None] * freq[None, :]
    return (jnp.cos(angle)[:, None, :], jnp.sin(angle)[:, None, :])


def rotate(field, cos_table, sin_table):
    half = field.shape[-1] // 2
    first = field[..., :half]
    second = field[..., half:]
    return jnp.concatenate(
        [first * cos_table - second * sin_table, second * cos_table + first * sin_table], axis=-1
    )


def rotate_back(grads, cos_table, sin_table):
    half = grads.shape[-1] // 2
    first = grads[..., :half]
    second = grads[..., half:]
    return jnp.concatenate(
        [first * cos_table + second * sin_table, second * cos_table - first * sin_table], axis=-1
    )


def when_live(live, update, carry):
    return lax.cond(live, update, lambda kept: kept, carry)


def shards(
    hidden_in,
    prior_logits,
    routes,
    block_ids,
    grad_out,
    attn_gain,
    query_weight,
    key_weight,
    value_weight,
    output_weight,
    moe_gain,
    router_weight,
    prior_weight,
    const_mix,
    const_vector,
    gate_weight,
    up_weight,
    down_weight,
):
    token_rows = hidden_in.shape[1]
    model_width = hidden_in.shape[2]
    head_count = HEADS
    head_size = model_width // head_count
    score_scale = head_size ** (-0.5)
    owners = lax.axis_size("expert")
    per_owner = gate_weight.shape[0]
    slot_count = per_owner * owners * CAP
    residual = hidden_in[0].astype(jnp.float32)
    prior_rows = prior_logits[0]
    route_rows = routes[0]
    own_ids = block_ids[0]
    own_low = jnp.min(own_ids)
    own_high = jnp.max(own_ids)
    cotangent = grad_out[0].astype(jnp.float32)
    query_full, key_full, value_full, output_full = (
        lax.all_gather(query_weight, "context", axis=0, tiled=True),
        lax.all_gather(key_weight, "context", axis=0, tiled=True),
        lax.all_gather(value_weight, "context", axis=0, tiled=True),
        lax.all_gather(output_weight, "context", axis=0, tiled=True),
    )
    inv_rms1 = lax.rsqrt(jnp.mean(residual * residual, axis=1, keepdims=True) + EPS)
    normed_one = residual * inv_rms1
    attn_input = (normed_one * attn_gain).astype(jnp.bfloat16)
    query_pre = jnp.dot(attn_input, query_full, preferred_element_type=jnp.float32)
    key_pre = jnp.dot(attn_input, key_full, preferred_element_type=jnp.float32)
    value_low = jnp.dot(attn_input, value_full, preferred_element_type=jnp.float32).astype(
        jnp.bfloat16
    )
    positions = lax.axis_index("context") * token_rows + jnp.arange(token_rows, dtype=jnp.int32)
    cos_table, sin_table = rope_tables(positions, head_size)
    query_rot = rotate(
        query_pre.reshape(token_rows, head_count, head_size), cos_table, sin_table
    ).astype(jnp.bfloat16)
    key_rot = rotate(
        key_pre.reshape(token_rows, head_count, head_size), cos_table, sin_table
    ).astype(jnp.bfloat16)
    key_flat = key_rot.reshape(token_rows, model_width)
    value_heads = value_low.reshape(token_rows, head_count, head_size)

    def piece_scores(queries, key_rows, query_ids, key_ids):
        scores = (
            jnp.einsum("qhd,khd->hqk", queries, key_rows, preferred_element_type=jnp.float32)
            * score_scale
        )
        allowed = key_ids[None, None, :] <= query_ids[None, :, None]
        return (scores, allowed)

    start_stats = (
        jnp.full((head_count, token_rows), NEGATIVE, jnp.float32),
        jnp.zeros((head_count, token_rows), jnp.float32),
    )
    key_rows = lax.all_gather(key_flat, "context", axis=0, tiled=True)
    key_ids = lax.all_gather(own_ids, "context", axis=0, tiled=True)

    def update(state):
        run_max, run_sum = state
        scores, allowed = piece_scores(
            query_rot, key_rows.reshape(-1, head_count, head_size), own_ids, key_ids
        )
        new_max = jnp.maximum(run_max, jnp.max(jnp.where(allowed, scores, NEGATIVE), axis=2))
        weights = jnp.exp(jnp.where(allowed, scores - new_max[:, :, None], NEGATIVE))
        return (new_max, jnp.sum(weights, axis=2))

    run_max, run_sum = when_live(jnp.min(key_ids) <= own_high, update, start_stats)
    log_total = run_max + jnp.log(run_sum)
    zero_heads = jnp.zeros((token_rows, head_count, head_size), jnp.float32)
    value_key_rows = lax.all_gather(key_flat, "context", axis=0, tiled=True)
    value_rows = lax.all_gather(value_low, "context", axis=0, tiled=True)
    value_key_ids = lax.all_gather(own_ids, "context", axis=0, tiled=True)

    def update(state):
        scores, allowed = piece_scores(
            query_rot, value_key_rows.reshape(-1, head_count, head_size), own_ids, value_key_ids
        )
        probs_low = jnp.exp(jnp.where(allowed, scores - log_total[:, :, None], NEGATIVE)).astype(
            jnp.bfloat16
        )
        return jnp.einsum(
            "hqk,khd->qhd",
            probs_low,
            value_rows.reshape(-1, head_count, head_size),
            preferred_element_type=jnp.float32,
        )

    attn_heads = when_live(jnp.min(value_key_ids) <= own_high, update, zero_heads)
    mix_low = attn_heads.reshape(token_rows, model_width).astype(jnp.bfloat16)
    after_attn = residual + jnp.dot(mix_low, output_full, preferred_element_type=jnp.float32)
    inv_rms2 = lax.rsqrt(jnp.mean(after_attn * after_attn, axis=1, keepdims=True) + EPS)
    normed_two = after_attn * inv_rms2
    moe_input = normed_two * moe_gain
    logits = jnp.dot(
        moe_input, router_weight, precision=HIGH, preferred_element_type=jnp.float32
    ) + jnp.dot(prior_rows, prior_weight, precision=HIGH, preferred_element_type=jnp.float32)
    probs = jax.nn.softmax(logits, axis=1)
    expert_ids = jnp.arange(logits.shape[1], dtype=jnp.int32)
    first_hot = (route_rows[:, 0:1] == expert_ids[None, :]).astype(jnp.float32)
    second_hot = (route_rows[:, 1:2] == expert_ids[None, :]).astype(jnp.float32)
    chosen = first_hot + second_hot
    gated = probs * chosen
    const_soft = jax.nn.softmax(
        jnp.einsum(
            "td,cjd->tcj", moe_input, const_mix, precision=HIGH, preferred_element_type=jnp.float32
        ),
        axis=2,
    )
    const_out = (
        const_soft[:, :, 0:1] * moe_input[:, None, :]
        + const_soft[:, :, 1:2] * const_vector[None, :, :]
    )
    copy_gate = gated[:, FFN_E + 1 : FFN_E + 2]
    const_gate = gated[:, FFN_E + 2 :]
    local_moe = copy_gate * moe_input + jnp.einsum(
        "tc,tcd->td", const_gate, const_out, precision=HIGH, preferred_element_type=jnp.float32
    )
    flat_route = route_rows.reshape(-1)
    ffn_hot = (flat_route[:, None] == jnp.arange(FFN_E, dtype=jnp.int32)[None, :]).astype(jnp.int32)
    before = jnp.sum((jnp.cumsum(ffn_hot, axis=0) - ffn_hot) * ffn_hot, axis=1)
    slot_index = jnp.where(
        flat_route < FFN_E,
        flat_route % per_owner * (owners * CAP) + flat_route // per_owner * CAP + before,
        -1,
    ).reshape(token_rows, 2)
    slot_ids = jnp.arange(slot_count, dtype=jnp.int32)[:, None]
    pick_first = (slot_ids == slot_index[None, :, 0]).astype(jnp.bfloat16)
    pick_second = (slot_ids == slot_index[None, :, 1]).astype(jnp.bfloat16)
    pick_either = pick_first + pick_second
    moe_low = moe_input.astype(jnp.bfloat16)
    send_rows = jnp.dot(pick_either, moe_low, preferred_element_type=jnp.float32).astype(
        jnp.bfloat16
    )
    arrived = lax.all_to_all(
        send_rows.reshape(per_owner, owners, CAP, model_width),
        "expert",
        split_axis=1,
        concat_axis=1,
        tiled=True,
    ).reshape(per_owner, owners * CAP, model_width)
    gate_full, up_full, down_full = (
        lax.all_gather(gate_weight, "context", axis=1, tiled=True),
        lax.all_gather(up_weight, "context", axis=1, tiled=True),
        lax.all_gather(down_weight, "context", axis=1, tiled=True),
    )
    gate_pre = jnp.einsum("erd,edh->erh", arrived, gate_full, preferred_element_type=jnp.float32)
    up_pre = jnp.einsum("erd,edh->erh", arrived, up_full, preferred_element_type=jnp.float32)
    hidden_low = (jax.nn.silu(gate_pre) * up_pre).astype(jnp.bfloat16)
    expert_out = jnp.einsum(
        "erh,ehd->erd", hidden_low, down_full, preferred_element_type=jnp.float32
    ).astype(jnp.bfloat16)
    returned = lax.all_to_all(
        expert_out.reshape(per_owner, owners, CAP, model_width),
        "expert",
        split_axis=1,
        concat_axis=1,
        tiled=True,
    ).reshape(slot_count, model_width)
    first_out = jnp.einsum("st,sd->td", pick_first, returned, preferred_element_type=jnp.float32)
    second_out = jnp.einsum("st,sd->td", pick_second, returned, preferred_element_type=jnp.float32)
    first_gate = jnp.sum(probs * first_hot, axis=1, keepdims=True)
    second_gate = jnp.sum(probs * second_hot, axis=1, keepdims=True)
    layer_out = after_attn + local_moe + first_gate * first_out + second_gate * second_out
    first_low = (first_gate * cotangent).astype(jnp.bfloat16)
    second_low = (second_gate * cotangent).astype(jnp.bfloat16)
    grad_send = jnp.dot(
        jnp.concatenate([pick_first, pick_second], axis=1),
        jnp.concatenate([first_low, second_low], axis=0),
        preferred_element_type=jnp.float32,
    ).astype(jnp.bfloat16)
    grad_arrived = lax.all_to_all(
        grad_send.reshape(per_owner, owners, CAP, model_width),
        "expert",
        split_axis=1,
        concat_axis=1,
        tiled=True,
    ).reshape(per_owner, owners * CAP, model_width)
    gate_back, up_back, down_back = (
        lax.all_gather(gate_weight, "context", axis=1, tiled=True),
        lax.all_gather(up_weight, "context", axis=1, tiled=True),
        lax.all_gather(down_weight, "context", axis=1, tiled=True),
    )
    grad_hidden = jnp.einsum(
        "erd,ehd->erh", grad_arrived, down_back, preferred_element_type=jnp.float32
    ).astype(jnp.bfloat16)
    grad_down_local = jnp.einsum(
        "erh,erd->ehd", hidden_low, grad_arrived, preferred_element_type=jnp.float32
    )
    sigmoid_gate = jax.nn.sigmoid(gate_pre)
    hidden_grad_wide = grad_hidden.astype(jnp.float32)
    grad_gate_low = (
        hidden_grad_wide * up_pre * sigmoid_gate * (1.0 + gate_pre * (1.0 - sigmoid_gate))
    ).astype(jnp.bfloat16)
    grad_up_low = (hidden_grad_wide * gate_pre * sigmoid_gate).astype(jnp.bfloat16)
    grad_gate_local = jnp.einsum(
        "erd,erh->edh", arrived, grad_gate_low, preferred_element_type=jnp.float32
    )
    grad_up_local = jnp.einsum(
        "erd,erh->edh", arrived, grad_up_low, preferred_element_type=jnp.float32
    )
    grad_rows = (
        jnp.einsum("erh,edh->erd", grad_gate_low, gate_back, preferred_element_type=jnp.float32)
        + jnp.einsum("erh,edh->erd", grad_up_low, up_back, preferred_element_type=jnp.float32)
    ).astype(jnp.bfloat16)
    grad_back = lax.all_to_all(
        grad_rows.reshape(per_owner, owners, CAP, model_width),
        "expert",
        split_axis=1,
        concat_axis=1,
        tiled=True,
    ).reshape(slot_count, model_width)
    grad_moe_ffn = jnp.einsum(
        "st,sd->td", pick_either, grad_back, preferred_element_type=jnp.float32
    )
    first_dot = jnp.sum(cotangent * first_out, axis=1, keepdims=True)
    second_dot = jnp.sum(cotangent * second_out, axis=1, keepdims=True)
    copy_dot = jnp.sum(cotangent * moe_input, axis=1, keepdims=True)
    const_dot = jnp.sum(cotangent[:, None, :] * const_out, axis=2)
    extra = jnp.concatenate(
        [jnp.zeros((token_rows, FFN_E + 1), jnp.float32), copy_dot, const_dot], axis=1
    )
    grad_probs = first_hot * first_dot + second_hot * second_dot + chosen * extra
    grad_logits = probs * (grad_probs - jnp.sum(probs * grad_probs, axis=1, keepdims=True))
    grad_router_local = jnp.einsum(
        "td,tj->dj", moe_input, grad_logits, precision=HIGH, preferred_element_type=jnp.float32
    )
    grad_prior_local = jnp.einsum(
        "ti,tj->ij", prior_rows, grad_logits, precision=HIGH, preferred_element_type=jnp.float32
    )
    grad_prior_rows = jnp.einsum(
        "tj,ij->ti", grad_logits, prior_weight, precision=HIGH, preferred_element_type=jnp.float32
    )
    grad_const_out = const_gate[:, :, None] * cotangent[:, None, :]
    grad_soft = jnp.stack(
        [
            jnp.sum(grad_const_out * moe_input[:, None, :], axis=2),
            jnp.sum(grad_const_out * const_vector[None, :, :], axis=2),
        ],
        axis=2,
    )
    grad_mix = const_soft * (grad_soft - jnp.sum(const_soft * grad_soft, axis=2, keepdims=True))
    grad_const_mix_local = jnp.einsum(
        "tcj,td->cjd", grad_mix, moe_input, precision=HIGH, preferred_element_type=jnp.float32
    )
    grad_const_vector_local = jnp.einsum(
        "tc,tcd->cd",
        const_soft[:, :, 1],
        grad_const_out,
        precision=HIGH,
        preferred_element_type=jnp.float32,
    )
    grad_moe_input = (
        grad_moe_ffn
        + jnp.einsum(
            "tj,dj->td",
            grad_logits,
            router_weight,
            precision=HIGH,
            preferred_element_type=jnp.float32,
        )
        + copy_gate * cotangent
        + jnp.einsum(
            "tc,tcd->td",
            const_soft[:, :, 0],
            grad_const_out,
            precision=HIGH,
            preferred_element_type=jnp.float32,
        )
        + jnp.einsum(
            "tcj,cjd->td", grad_mix, const_mix, precision=HIGH, preferred_element_type=jnp.float32
        )
    )
    grad_moe_gain_local = jnp.sum(grad_moe_input * normed_two, axis=0)
    grad_normed_two = grad_moe_input * moe_gain
    grad_after = cotangent + inv_rms2 * (
        grad_normed_two - normed_two * jnp.mean(grad_normed_two * normed_two, axis=1, keepdims=True)
    )
    grad_attn_low = grad_after.astype(jnp.bfloat16)
    grad_output_local = jnp.einsum(
        "ti,tj->ij", mix_low, grad_attn_low, preferred_element_type=jnp.float32
    )
    grad_mix_low = jnp.einsum(
        "tj,ij->ti", grad_attn_low, output_full, preferred_element_type=jnp.float32
    ).astype(jnp.bfloat16)
    grad_mix_heads = grad_mix_low.reshape(token_rows, head_count, head_size)
    delta_rows = jnp.sum(grad_mix_heads.astype(jnp.float32) * attn_heads, axis=2)
    row_delta = jnp.transpose(delta_rows)
    query_key_rows = lax.all_gather(key_flat, "context", axis=0, tiled=True)
    query_value_rows = lax.all_gather(value_low, "context", axis=0, tiled=True)
    query_key_ids = lax.all_gather(own_ids, "context", axis=0, tiled=True)

    def update(state):
        key_part = query_key_rows.reshape(-1, head_count, head_size)
        scores, allowed = piece_scores(query_rot, key_part, own_ids, query_key_ids)
        probs_part = jnp.exp(jnp.where(allowed, scores - log_total[:, :, None], NEGATIVE))
        grad_probs_part = jnp.einsum(
            "qhd,khd->hqk",
            grad_mix_heads,
            query_value_rows.reshape(-1, head_count, head_size),
            preferred_element_type=jnp.float32,
        )
        grad_scores = (probs_part * (grad_probs_part - row_delta[:, :, None])).astype(jnp.bfloat16)
        return jnp.einsum("hqk,khd->qhd", grad_scores, key_part, preferred_element_type=jnp.float32)

    grad_query_rot = when_live(jnp.min(query_key_ids) <= own_high, update, zero_heads) * score_scale
    query_rows = lax.all_gather(
        query_rot.reshape(token_rows, model_width).astype(jnp.float32),
        "context",
        axis=0,
        tiled=True,
    ).astype(jnp.bfloat16)
    grad_rows_part = lax.all_gather(
        grad_mix_low.astype(jnp.float32), "context", axis=0, tiled=True
    ).astype(jnp.bfloat16)
    total_rows = lax.all_gather(jnp.transpose(log_total), "context", axis=0, tiled=True)
    delta_part = lax.all_gather(delta_rows, "context", axis=0, tiled=True)
    query_ids = lax.all_gather(own_ids, "context", axis=0, tiled=True)

    def update(state):
        query_part = query_rows.reshape(-1, head_count, head_size)
        grad_part = grad_rows_part.reshape(-1, head_count, head_size)
        scores, allowed = piece_scores(query_part, key_rot, query_ids, own_ids)
        probs_part = jnp.exp(
            jnp.where(allowed, scores - jnp.transpose(total_rows)[:, :, None], NEGATIVE)
        )
        grad_probs_part = jnp.einsum(
            "qhd,khd->hqk", grad_part, value_heads, preferred_element_type=jnp.float32
        )
        grad_scores = (
            probs_part * (grad_probs_part - jnp.transpose(delta_part)[:, :, None])
        ).astype(jnp.bfloat16)
        grad_values = jnp.einsum(
            "hqk,qhd->khd",
            probs_part.astype(jnp.bfloat16),
            grad_part,
            preferred_element_type=jnp.float32,
        )
        grad_keys = jnp.einsum(
            "hqk,qhd->khd", grad_scores, query_part, preferred_element_type=jnp.float32
        )
        return (grad_keys, grad_values)

    grad_key_rot, grad_value_heads = when_live(
        own_low <= jnp.max(query_ids), update, (zero_heads, zero_heads)
    )
    grad_query_pre = (
        rotate_back(grad_query_rot, cos_table, sin_table)
        .reshape(token_rows, model_width)
        .astype(jnp.bfloat16)
    )
    grad_key_pre = (
        rotate_back(grad_key_rot * score_scale, cos_table, sin_table)
        .reshape(token_rows, model_width)
        .astype(jnp.bfloat16)
    )
    grad_value_low = grad_value_heads.reshape(token_rows, model_width).astype(jnp.bfloat16)
    grad_query_local = jnp.einsum(
        "ti,tj->ij", attn_input, grad_query_pre, preferred_element_type=jnp.float32
    )
    grad_key_local = jnp.einsum(
        "ti,tj->ij", attn_input, grad_key_pre, preferred_element_type=jnp.float32
    )
    grad_value_local = jnp.einsum(
        "ti,tj->ij", attn_input, grad_value_low, preferred_element_type=jnp.float32
    )
    grad_attn_input = (
        jnp.einsum("tj,ij->ti", grad_query_pre, query_full, preferred_element_type=jnp.float32)
        + jnp.einsum("tj,ij->ti", grad_key_pre, key_full, preferred_element_type=jnp.float32)
        + jnp.einsum("tj,ij->ti", grad_value_low, value_full, preferred_element_type=jnp.float32)
    )
    grad_attn_gain_local = jnp.sum(grad_attn_input * normed_one, axis=0)
    grad_normed_one = grad_attn_input * attn_gain
    grad_input = grad_after + inv_rms1 * (
        grad_normed_one - normed_one * jnp.mean(grad_normed_one * normed_one, axis=1, keepdims=True)
    )
    shares = (
        lax.psum_scatter(grad_query_local, "context", scatter_dimension=0, tiled=True),
        lax.psum_scatter(grad_key_local, "context", scatter_dimension=0, tiled=True),
        lax.psum_scatter(grad_value_local, "context", scatter_dimension=0, tiled=True),
        lax.psum_scatter(grad_output_local, "context", scatter_dimension=0, tiled=True),
        lax.psum_scatter(grad_gate_local, "context", scatter_dimension=1, tiled=True),
        lax.psum_scatter(grad_up_local, "context", scatter_dimension=1, tiled=True),
        lax.psum_scatter(grad_down_local, "context", scatter_dimension=1, tiled=True),
        lax.psum_scatter(grad_attn_gain_local, "context", scatter_dimension=0, tiled=True),
        lax.psum_scatter(grad_moe_gain_local, "context", scatter_dimension=0, tiled=True),
        lax.psum_scatter(grad_router_local, "context", scatter_dimension=0, tiled=True),
        lax.psum_scatter(grad_const_mix_local, "context", scatter_dimension=2, tiled=True),
        lax.psum_scatter(grad_const_vector_local, "context", scatter_dimension=1, tiled=True),
    )
    summed = lax.psum(
        (
            shares[0],
            shares[1],
            shares[2],
            shares[3],
            shares[7],
            shares[8],
            shares[9],
            shares[10],
            shares[11],
        ),
        "expert",
    )
    grad_prior_weight = lax.psum(grad_prior_local, ("expert", "context"))
    return (
        layer_out.astype(jnp.bfloat16)[None],
        grad_input[None],
        grad_prior_rows[None],
        summed[4],
        summed[0],
        summed[1],
        summed[2],
        summed[3],
        summed[5],
        summed[6],
        grad_prior_weight,
        summed[7],
        summed[8],
        shares[4],
        shares[5],
        shares[6],
    )


def solution(mesh):
    return jax.shard_map(
        shards,
        mesh=mesh,
        in_specs=(
            P("expert", "context", None),
            P("expert", "context", None),
            P("expert", "context", None),
            P("expert", "context"),
            P("expert", "context", None),
            P(),
            P("context", None),
            P("context", None),
            P("context", None),
            P("context", None),
            P(),
            P(),
            P(),
            P(),
            P(),
            P("expert", "context", None),
            P("expert", "context", None),
            P("expert", "context", None),
        ),
        out_specs=(
            P("expert", "context", None),
            P("expert", "context", None),
            P("expert", "context", None),
            P("context"),
            P("context", None),
            P("context", None),
            P("context", None),
            P("context", None),
            P("context"),
            P("context", None),
            P(),
            P(None, None, "context"),
            P(None, "context"),
            P("expert", "context", None),
            P("expert", "context", None),
            P("expert", "context", None),
        ),
        check_vma=False,
    )
```

profile of v0, /device:TPU:0, one launch (start us, length us, event | category | flops | bytes accessed | tf_op | source)
XLA Modules:
  0.0 1292.2 jit_solution(18350824987109720943)
XLA Ops:
  11.1 25.5 %all-gather.17.cloned.1.call-done = bf16[768,768]{1,0:T(8,128)(2,1)} async-done(((bf16[96,768]{1,0:T(8,128)(2,1)}), bf16[768,768]{1,0:T(8,128)(2,1)}) %all-gather.17.cloned.1.call-update) | async-done | bytes 1179664 | tf_op jit(solution)/shard_map/all_gather | solution.py:82
  38.1 24.3 %all-gather.13.cloned.1.call-done = bf16[768,768]{1,0:T(8,128)(2,1)} async-done(((bf16[96,768]{1,0:T(8,128)(2,1)}), bf16[768,768]{1,0:T(8,128)(2,1)}) %all-gather.13.cloned.1.call-update) | async-done | bytes 1179664 | tf_op jit(solution)/shard_map/all_gather | solution.py:83
  67.2 21.1 %all-gather.19.cloned.1.call-done = bf16[768,768]{1,0:T(8,128)(2,1)} async-done(((bf16[96,768]{1,0:T(8,128)(2,1)}), bf16[768,768]{1,0:T(8,128)(2,1)}) %all-gather.19.cloned.1.call-update) | async-done | bytes 1179664 | tf_op jit(solution)/shard_map/all_gather | solution.py:84
  88.2 2.8 convolution_convert_fusion.5
  94.4 9.0 all-gather
  109.0 20.6 %all-gather.15.cloned.1.call-done = bf16[3072,768]{0,1:T(8,128)(2,1)} async-done(((bf16[384,768]{0,1:T(8,128)(2,1)}), bf16[3072,768]{0,1:T(8,128)(2,1)}) %all-gather.15.cloned.1.call-update) | async-done | bytes 4718608 | tf_op jit(solution)/shard_map/all_gather | solution.py:133
  129.7 45.2 %conditional.4 = (f32[12,384]{1,0:T(8,128)}, f32[12,384]{1,0:T(8,128)S(1)}) conditional(s32[]{:T(128)} %convert_element_type.203, () %tuple.43, (s32[3072]{0:T(1024)S(1)}, s32[1,384]{1,0:T(1,128)S(1)}, bf16[3072,768]{0,1:T(8,128)(2,1)}, bf16[384,12,64]{0,2,1:T(8,128)(2,1)S(1)}) %tuple.182), branch_computations={%region_3.0_spmd, %region_4.7_spmd} | conditional | flops 1912204800 | bytes 122239504 | solution.py:43
  130.4 24.8 %select_reduce_fusion = (f32[12,384]{1,0:T(8,128)S(1)}, f32[12,384,3072]{2,1,0:T(8,128)}) fusion(pred[384,3072]{1,0:T(8,128)(4,1)S(1)} %broadcast_compare_fusion, bf16[384,12,64]{0,2,1:T(8,128)(2,1)S(1)} %get-tuple-element.61, bf16[3072,12,64]{0,2,1:T(8,128)(2,1)} %bitcast.240), kind=kOutput, calls=%fused_computation.1 | convolution fusion | flops 1854402048 | bytes 63129600 | tf_op jit(solution)/shard_map/cond/branch_1_fun/qhd,khd->hqk/dot_general | solution.py:108
  155.8 19.1 %exponential_reduce_fusion = f32[12,384]{1,0:T(8,128)S(1)} fusion(f32[12,384,3072]{2,1,0:T(8,128)} %get-tuple-element.375, f32[12,384]{1,0:T(8,128)} %broadcast_maximum_fusion, pred[384,3072]{1,0:T(8,128)(4,1)S(1)} %broadcast_compare_fusion), kind=kLoop, calls=%fused_computation | loop fusion | flops 56618496 | bytes 57839616 | tf_op jit(solution)/shard_map/cond/branch_1_fun/reduce_sum | solution.py:128
  175.6 31.7 %conditional.5 = (f32[384,12,64]{0,2,1:T(8,128)S(1)}, bf16[384,768]{0,1:T(8,128)(2,1)S(1)}) conditional(s32[]{:T(128)} %convert_element_type.203, () %tuple.42, (s32[3072]{0:T(1024)S(1)}, s32[1,384]{1,0:T(1,128)S(1)}, bf16[3072,768]{0,1:T(8,128)(2,1)}, bf16[384,12,64]{0,2,1:T(8,128)(2,1)S(1)}, f32[12,384]{1,0:T(8,128)S(1)}, ...), branch_computations={%region_7.0_spmd, %region_8.9_spmd} | conditional | flops 3681976320 | bytes 23628308 | solution.py:43
  175.8 6.7 copy.151
  184.2 23.0 %fusion.150 = (bf16[384,12,64]{0,2,1:T(8,128)(2,1)S(1)}, f32[384,12,64]{0,2,1:T(8,128)S(1)}) fusion(bf16[3072,12,64]{0,2,1:T(8,128)(2,1)} %bitcast.264, f32[12,384]{1,0:T(8,128)S(1)} %get-tuple-element.67, pred[384,3072]{1,0:T(8,128)(4,1)} %broadcast_compare_fusion.1, bf16[384,12,64]{0,2,1:T(8,128)(2,1)S(1)} %get-tuple-element.65, ...), kind=kOutput, calls=%fused_computation.238 | convolution fusion | flops 3680796672 | bytes 12994560 | tf_op jit(solution)/shard_map/cond/branch_1_fun/hqk,khd->qhd/dot_general | solution.py:144
  212.4 5.0 all-to-all-start
  220.5 26.0 %all-to-all-done = bf16[2,4,96,768]{3,2,0,1:T(8,128)(2,1)} async-done(((bf16[2,4,96,768]{3,2,0,1:T(8,128)(2,1)}), bf16[2,4,96,768]{3,2,0,1:T(8,128)(2,1)}, u32[]{:S(2)}, u32[]{:S(2)}) %all-to-all-start) | async-done | bytes 1179680 | tf_op jit(solution)/shard_map/all_to_all | solution.py:197
  246.5 2.4 copy.158
  248.9 8.5 fusion.157
  257.4 33.2 %all-gather.27.cloned.1.call-done = bf16[2,768,2048]{2,1,0:T(8,128)(2,1)} async-done(((bf16[2,96,2048]{2,1,0:T(8,128)(2,1)}), bf16[2,768,2048]{2,1,0:T(8,128)(2,1)}) %all-gather.27.cloned.1.call-update) | async-done | bytes 6291472 | tf_op jit(solution)/shard_map/all_gather | solution.py:206
  290.6 11.6 multiply_convert_fusion.8
  302.1 35.8 %all-gather.29.cloned.1.call-done = bf16[2,2048,768]{2,1,0:T(8,128)(2,1)} async-done(((bf16[2,256,768]{2,1,0:T(8,128)(2,1)}), bf16[2,2048,768]{2,1,0:T(8,128)(2,1)}) %all-gather.29.cloned.1.call-update) | async-done | bytes 6291472 | tf_op jit(solution)/shard_map/all_gather | solution.py:207
  337.9 6.3 convolution_convert_fusion.2
  345.3 4.9 all-to-all-start.1
  352.0 27.3 %all-to-all-done.1 = bf16[2,4,96,768]{3,2,0,1:T(8,128)(2,1)} async-done(((bf16[2,4,96,768]{3,2,0,1:T(8,128)(2,1)}), bf16[2,4,96,768]{3,2,0,1:T(8,128)(2,1)}, u32[]{:S(2)}, u32[]{:S(2)}) %all-to-all-start.1) | async-done | bytes 1179680 | tf_op jit(solution)/shard_map/all_to_all | solution.py:215
  383.4 3.0 multiply_reduce_fusion
  389.9 4.3 all-to-all-start.2
  394.8 27.6 %all-to-all-done.2 = bf16[2,4,96,768]{3,2,0,1:T(8,128)(2,1)} async-done(((bf16[2,4,96,768]{3,2,0,1:T(8,128)(2,1)}), bf16[2,4,96,768]{3,2,0,1:T(8,128)(2,1)}, u32[]{:S(2)}, u32[]{:S(2)}) %all-to-all-start.2) | async-done | bytes 1179680 | tf_op jit(solution)/shard_map/all_to_all | solution.py:234
  423.7 10.9 fusion.33
  434.6 5.9 fusion.158
  440.6 8.3 add_convert_fusion
  450.0 3.5 all-to-all-start.3
  459.3 10.6 fusion.42
  469.9 11.0 fusion.40
  483.2 3.2 multiply_reduce_fusion.1
  489.6 2.2 fusion.108
  493.3 11.0 all_gather.62
  505.7 65.7 %conditional.6 = (f32[384,12,64]{0,2,1:T(8,128)S(1)}) conditional(s32[]{:T(128)} %convert_element_type.203, () %tuple.46, (s32[3072]{0:T(1024)S(1)}, s32[1,384]{1,0:T(1,128)S(1)}, bf16[3072,768]{0,1:T(8,128)(2,1)}, bf16[384,12,64]{0,2,1:T(8,128)(2,1)S(1)}, f32[12,384]{1,0:T(8,128)S(1)}, /*index=5*/bf16[3072,768]{1,0:T(8,128)(2,1)}, ...), branch_computations={%region_29.30_spmd, %region_30.31_spmd} | conditional | flops 5521932288 | bytes 141611520 | solution.py:43
  505.7 23.7 %fusion.155 = f32[12,384,3072]{2,1,0:T(8,128)} fusion(bf16[384,12,64]{0,2,1:T(8,128)(2,1)S(1)} %get-tuple-element.71, bf16[3072,12,64]{0,2,1:T(8,128)(2,1)} %bitcast.242), kind=kOutput, calls=%fused_computation.243 | convolution fusion | flops 1811939328 | bytes 61931520 | tf_op jit(solution)/shard_map/cond/branch_1_fun/qhd,khd->hqk/dot_general | solution.py:108
  529.4 6.6 copy.166
  537.8 33.5 %fusion.11 = f32[384,12,64]{0,2,1:T(8,128)S(1)} fusion(bf16[3072,12,64]{0,2,1:T(8,128)(2,1)} %bitcast.243, f32[12,384,3072]{2,1,0:T(8,128)} %fusion.155, f32[12,384]{1,0:T(8,128)S(1)} %get-tuple-element.76, f32[12,384]{1,0:T(8,128)S(1)} %get-tuple-element.73, pred[384,3072]{1,0:T(8,128)(4,1)} %broadcast_compare_fusion.2, ...), kind=kOutput, calls=%fused_computation.17 | convolution fusion | flops 3708813312 | bytes 69046272 | tf_op jit(solution)/shard_map/cond/branch_1_fun/hqk,khd->qhd/dot_general | solution.py:366
  571.4 8.1 all_gather.64
  581.3 101.9 %conditional.7 = (f32[384,12,64]{0,2,1:T(8,128)}, bf16[384,768]{0,1:T(8,128)(2,1)S(1)}) conditional(s32[]{:T(128)} %convert_element_type.239, () %tuple.48, (s32[1,384]{1,0:T(1,128)S(1)}, s32[3072]{0:T(1024)S(1)}, bf16[3072,768]{0,1:T(8,128)(2,1)}, bf16[384,12,64]{0,2,1:T(8,128)(2,1)S(1)}, f32[3072,12]{0,1:T(8,128)S(1)}, ...), branch_computations={%region_33.34_spmd, %region_34.35_spmd} | conditional | flops 7390789632 | bytes 277086784 | solution.py:43
  581.3 22.2 %fusion.156 = f32[12,3072,384]{2,1,0:T(8,128)} fusion(bf16[3072,12,64]{0,2,1:T(8,128)(2,1)} %bitcast.244, bf16[384,12,64]{0,2,1:T(8,128)(2,1)S(1)} %get-tuple-element.80), kind=kOutput, calls=%fused_computation.244 | convolution fusion | flops 1811939328 | bytes 61931520 | tf_op jit(solution)/shard_map/cond/branch_1_fun/qhd,khd->hqk/dot_general | solution.py:108
  603.5 6.7 copy.167
  611.9 35.8 %multiply_convert_fusion.11 = bf16[12,3072,384]{2,1,0:T(8,128)(2,1)} fusion(f32[12,3072,384]{2,1,0:T(8,128)} %fusion.156, f32[12,3072]{1,0:T(8,128)S(1)} %bitcast.290, f32[12,3072]{1,0:T(8,128)S(1)} %bitcast.288, pred[3072,384]{1,0:T(8,128)(4,1)S(1)} %broadcast_compare_fusion.3, bf16[3072,12,64]{0,2,1:T(8,128)(2,1)} %bitcast.262, ...), kind=kOutput, calls=%fused_computation.20.clone.clone.clone.clone.1 | convolution fusion | flops 1896873984 | bytes 91717632 | tf_op jit(solution)/shard_map/cond/branch_1_fun/qhd,khd->hqk/dot_general | solution.py:389
  647.8 12.4 fusion.22
  660.2 22.8 %fusion.23 = bf16[12,384,64]{1,2,0:T(8,128)(2,1)S(1)} fusion(bf16[3072,12,64]{0,2,1:T(8,128)(2,1)} %bitcast.263, f32[12,3072,384]{2,1,0:T(8,128)} %fusion.156, f32[12,3072]{1,0:T(8,128)S(1)} %bitcast.289, pred[3072,384]{1,0:T(8,128)(4,1)S(1)} %broadcast_compare_fusion.3), kind=kOutput, calls=%fused_computation.30 | convolution fusion | flops 1868857344 | bytes 63258624 | tf_op jit(solution)/shard_map/cond/branch_1_fun/hqk,qhd->khd/dot_general | solution.py:395
  686.5 2.4 fusion.101
  689.9 2.3 fusion.97
  692.3 2.4 fusion.99
  701.1 2.9 fusion.143
  704.1 27.2 %reduce-scatter.19.cloned.1.call-done = f32[96,768]{1,0:T(8,128)} async-done(((f32[768,768]{1,0:T(8,128)}), f32[96,768]{1,0:T(8,128)}) %reduce-scatter.19.cloned.1.call-update) | async-done | bytes 294928 | tf_op jit(solution)/shard_map/reduce_scatter | solution.py:441
  731.3 45.6 %reduce-scatter.17.cloned.1.call-done = f32[96,768]{1,0:T(8,128)} async-done(((f32[768,768]{1,0:T(8,128)}), f32[96,768]{1,0:T(8,128)}) %reduce-scatter.17.cloned.1.call-update) | async-done | bytes 294928 | tf_op jit(solution)/shard_map/reduce_scatter | solution.py:440
  776.9 45.6 %reduce-scatter.21.cloned.1.call-done = f32[96,768]{1,0:T(8,128)} async-done(((f32[768,768]{1,0:T(8,128)}), f32[96,768]{1,0:T(8,128)}) %reduce-scatter.21.cloned.1.call-update) | async-done | bytes 294928 | tf_op jit(solution)/shard_map/reduce_scatter | solution.py:442
  822.6 11.1 fusion.145
  834.9 9.9 fusion.162
  845.0 8.3 fusion.161
  855.1 4.3 reduce-scatter.35.cloned.1.call-done
  861.2 39.3 %psum.77 = f32[12,12]{0,1:T(8,128)S(1)} all-reduce(f32[12,12]{0,1:T(8,128)S(1)} %convolution_bitcast_fusion.2), channel_id=1, replica_groups=mesh['expert'=4,'context'=8] {'expert','context'}, use_global_device_ids=true, to_apply=%region_52.53 | all-reduce | flops 144 | bytes 1152 | tf_op jit(solution)/shard_map/psum | solution.py:467
  902.2 30.8 %reduce-scatter.31.cloned.1.call-done = f32[96,12]{1,0:T(8,128)} async-done(((f32[768,12]{1,0:T(8,128)}), f32[96,12]{1,0:T(8,128)}) %reduce-scatter.31.cloned.1.call-update) | async-done | bytes 4624
  937.8 12.8 all-reduce.2
  950.8 19.9 %all-reduce.3 = (f32[96]{0:T(128)}, f32[96]{0:T(128)}, f32[96,12]{0,1:T(8,128)}, f32[2,2,96]{2,1,0:T(2,128)}, f32[2,96]{1,0:T(2,128)}) all-reduce(f32[96]{0:T(128)S(1)} %dynamic-slice.1, f32[96]{0:T(128)S(1)} %dynamic-slice.3, f32[96,12]{0,1:T(8,128)S(1)} %copy.187, ...), channel_id=1, replica_groups=mesh['expert'=4,'context'=8] {'expert'}, use_global_device_ids=true, to_apply=%region_38.39 | all-reduce | flops 1920 | bytes 15360 | tf_op jit(solution)/shard_map/psum | solution.py:453
  972.0 20.2 %all-reduce.7.cloned.1.call-done = (f32[96,768]{1,0:T(8,128)}, f32[96,768]{1,0:T(8,128)}, f32[96,768]{1,0:T(8,128)}, f32[96,768]{1,0:T(8,128)}) async-done(((f32[96,768]{1,0:T(8,128)}, f32[96,768]{1,0:T(8,128)}, f32[96,768]{1,0:T(8,128)}, f32[96,768]{1,0:T(8,128)}), (f32[96,768]{1,0:T(8,128)}, f32[96,768]{1,0:T(8,128)}, f32[96,768]{1,0:T(8,128)}, f32[96,768]{1,0:T(8,128)})) %all-reduce.7.cloned.1.call-update) | async-done | bytes 1179664 | tf_op jit(solution)/shard_map/psum | solution.py:453
  992.2 95.5 %reduce-scatter.27.cloned.1.call-done = f32[2,96,2048]{2,1,0:T(8,128)} async-done(((f32[2,768,2048]{2,1,0:T(8,128)}), f32[2,96,2048]{2,1,0:T(8,128)}) %reduce-scatter.27.cloned.1.call-update) | async-done | bytes 1572880 | tf_op jit(solution)/shard_map/reduce_scatter | solution.py:445
  1087.6 96.2 %reduce-scatter.29.cloned.1.call-done = f32[2,256,768]{2,1,0:T(8,128)} async-done(((f32[2,2048,768]{2,1,0:T(8,128)}), f32[2,256,768]{2,1,0:T(8,128)}) %reduce-scatter.29.cloned.1.call-update) | async-done | bytes 1572880 | tf_op jit(solution)/shard_map/reduce_scatter | solution.py:446
  1183.8 96.2 %reduce-scatter.25.cloned.1.call-done = f32[2,96,2048]{2,1,0:T(8,128)} async-done(((f32[2,768,2048]{2,1,0:T(8,128)}), f32[2,96,2048]{2,1,0:T(8,128)}) %reduce-scatter.25.cloned.1.call-update) | async-done | bytes 1572880 | tf_op jit(solution)/shard_map/reduce_scatter | solution.py:444
  (342 shorter events, 88.2 us)
Async XLA Ops:
  7.2 212.0 %copy-start = (f32[768,12]{0,1:T(8,128)S(1)}, f32[768,12]{0,1:T(8,128)}, u32[]{:S(2)}) copy-start(f32[768,12]{0,1:T(8,128)} %param.37) | copy-start | bytes 110596
  7.2 29.4 %all-gather.17.cloned.1.call-start = ((), (), s32[]{:S(2)}) async-start(), calls=%async_computation.16 | async-start | bytes 1327104 | tf_op jit(solution)/shard_map/all_gather | solution.py:82
  7.9 54.5 %all-gather.13.cloned.1.call-start = ((), (), s32[]{:S(2)}) async-start(), calls=%async_computation.14 | async-start | bytes 1327104 | tf_op jit(solution)/shard_map/all_gather | solution.py:83
  8.7 79.6 %all-gather.19.cloned.1.call-start = ((), (), s32[]{:S(2)}) async-start(), calls=%async_computation.17 | async-start | bytes 1327104 | tf_op jit(solution)/shard_map/all_gather | solution.py:84
  9.4 120.3 %all-gather.15.cloned.1.call-start = ((), (), s32[]{:S(2)}) async-start(), calls=%async_computation.15 | async-start | bytes 5308416 | tf_op jit(solution)/shard_map/all_gather | solution.py:133
  10.8 77.5 %copy-start.67 = (f32[384]{0:T(512)}, f32[384]{0:T(512)S(1)}, u32[]{:S(2)}) copy-start(f32[384]{0:T(512)S(1)} %add_rsqrt_fusion.1) | copy-start | bytes 4612
  11.0 54.8 %copy-start.47 = (f32[384,32]{0,1:T(8,128)}, f32[384,32]{0,1:T(8,128)S(1)}, u32[]{:S(2)}) copy-start(f32[384,32]{0,1:T(8,128)S(1)} %get-tuple-element.401) | copy-start | bytes 147460
  11.0 54.8 %copy-start.49 = (f32[384,32]{0,1:T(8,128)}, f32[384,32]{0,1:T(8,128)S(1)}, u32[]{:S(2)}) copy-start(f32[384,32]{0,1:T(8,128)S(1)} %get-tuple-element.402) | copy-start | bytes 147460
  67.1 108.5 %all-gather.21.cloned.1.call-start = ((), (), s32[]{:S(2)}) async-start(), calls=%async_computation.18 | async-start | bytes 5308416 | tf_op jit(solution)/shard_map/all_gather | solution.py:134
  91.1 116.3 %all-gather.23.cloned.1.call-start = ((), (), s32[]{:S(2)}) async-start(), calls=%async_computation.19 | async-start | bytes 1327104 | tf_op jit(solution)/shard_map/all_gather | solution.py:85
  91.6 157.2 %all-gather.25.cloned.1.call-start = ((), (), s32[]{:S(2)}) async-start(), calls=%async_computation.20 | async-start | bytes 7077888 | tf_op jit(solution)/shard_map/all_gather | solution.py:205
  92.4 198.1 %all-gather.27.cloned.1.call-start = ((), (), s32[]{:S(2)}) async-start(), calls=%async_computation.21 | async-start | bytes 7077888 | tf_op jit(solution)/shard_map/all_gather | solution.py:206
  93.2 244.7 %all-gather.29.cloned.1.call-start = ((), (), s32[]{:S(2)}) async-start(), calls=%async_computation.22 | async-start | bytes 7077888 | tf_op jit(solution)/shard_map/all_gather | solution.py:207
  109.0 66.6 %copy-start.9 = (bf16[384,12,64]{0,2,1:T(8,128)(2,1)}, bf16[384,12,64]{0,2,1:T(8,128)(2,1)S(1)}, u32[]{:S(2)}) copy-start(bf16[384,12,64]{0,2,1:T(8,128)(2,1)S(1)} %maximum_convert_fusion.1) | copy-start | bytes 1769476
  175.6 317.7 %copy-start.65 = (f32[12,384]{1,0:T(8,128)}, f32[12,384]{1,0:T(8,128)S(1)}, u32[]{:S(2)}) copy-start(f32[12,384]{1,0:T(8,128)S(1)} %add.175) | copy-start | bytes 55300
  210.4 276.1 %copy-start.2 = (f32[384,768]{1,0:T(8,128)}, f32[384,768]{1,0:T(8,128)S(1)}, u32[]{:S(2)}) copy-start(f32[384,768]{1,0:T(8,128)S(1)} %get-tuple-element.404) | copy-start | bytes 3538948
  210.4 276.1 %copy-start.59 = (f32[384]{0:T(512)}, f32[384]{0:T(512)S(1)}, u32[]{:S(2)}) copy-start(f32[384]{0:T(512)S(1)} %add_rsqrt_fusion) | copy-start | bytes 4612
  212.4 34.1 %all-to-all-start = ((bf16[2,4,96,768]{3,2,0,1:T(8,128)(2,1)}), bf16[2,4,96,768]{3,2,0,1:T(8,128)(2,1)}, u32[]{:S(2)}, u32[]{:S(2)}) async-start(bf16[2,4,96,768]{3,2,0,1:T(8,128)(2,1)} %copy.157), calls=%async_computation | async-start | bytes 2359296 | tf_op jit(solution)/shard_map/all_to_all | solution.py:197
  219.2 164.2 %copy-start.11 = (f32[384,768]{1,0:T(8,128)}, f32[384,768]{1,0:T(8,128)S(1)}, u32[]{:S(2)}) copy-start(f32[384,768]{1,0:T(8,128)S(1)} %bitcast_convert_fusion.1) | copy-start | bytes 3538948
  345.3 4.9 copy-start.61
  345.3 4.9 copy-start.75
  345.3 5.2 copy-start.70
  345.3 34.0 %all-to-all-start.1 = ((bf16[2,4,96,768]{3,2,0,1:T(8,128)(2,1)}), bf16[2,4,96,768]{3,2,0,1:T(8,128)(2,1)}, u32[]{:S(2)}, u32[]{:S(2)}) async-start(bf16[2,4,96,768]{3,2,0,1:T(8,128)(2,1)} %copy.159), calls=%async_computation.1 | async-start | bytes 2359296 | tf_op jit(solution)/shard_map/all_to_all | solution.py:215
  351.9 103.0 %copy-start.57 = (f32[384,2,2]{0,2,1:T(2,128)}, f32[384,2,2]{0,2,1:T(2,128)S(1)}, u32[]{:S(2)}) copy-start(f32[384,2,2]{0,2,1:T(2,128)S(1)} %broadcast_divide_fusion) | copy-start | bytes 18436
  352.0 31.5 %copy-start.77 = (f32[384,2]{0,1:T(2,128)}, f32[384,2]{0,1:T(2,128)S(1)}, u32[]{:S(2)}) copy-start(f32[384,2]{0,1:T(2,128)S(1)} %get-tuple-element.397) | copy-start | bytes 9220
  389.9 32.4 %all-to-all-start.2 = ((bf16[2,4,96,768]{3,2,0,1:T(8,128)(2,1)}), bf16[2,4,96,768]{3,2,0,1:T(8,128)(2,1)}, u32[]{:S(2)}, u32[]{:S(2)}) async-start(bf16[2,4,96,768]{3,2,0,1:T(8,128)(2,1)} %copy.161), calls=%async_computation.2 | async-start | bytes 2359296 | tf_op jit(solution)/shard_map/all_to_all | solution.py:234
  394.2 186.5 %all-gather.31.cloned.1.call-start = ((), (), s32[]{:S(2)}) async-start(), calls=%async_computation.23 | async-start | bytes 5308416 | tf_op jit(solution)/shard_map/all_gather | solution.py:369
  423.7 10.9 copy-start.22
  434.6 5.9 copy-start.34
  450.0 31.6 %all-to-all-start.3 = ((bf16[2,4,96,768]{3,2,0,1:T(8,128)(2,1)}), bf16[2,4,96,768]{3,2,0,1:T(8,128)(2,1)S(1)}, u32[]{:S(2)}, u32[]{:S(2)}) async-start(bf16[2,4,96,768]{3,2,0,1:T(8,128)(2,1)} %copy.163), calls=%async_computation.3 | async-start | bytes 2359296 | tf_op jit(solution)/shard_map/all_to_all | solution.py:268
  453.5 127.2 %all-gather.33.cloned.1.call-start = ((), (), s32[]{:S(2)}) async-start(), calls=%async_computation.24 | async-start | bytes 5308416 | tf_op jit(solution)/shard_map/all_gather | solution.py:375
  454.8 4.5 copy-start.71
  454.8 4.5 copy-start.56
  454.8 4.5 copy-start.73
  454.8 4.4 copy-start.79
  454.9 4.4 copy-start.39
  459.3 10.6 copy-start.38
  489.5 214.6 %reduce-scatter.23.cloned.1.call-start = ((), (), s32[]{:S(2)}) async-start(), calls=%async_computation.28 | async-start | bytes 2654208 | tf_op jit(solution)/shard_map/reduce_scatter | solution.py:443
  491.8 12.6 copy-start.14
  491.8 12.9 copy-start.29
  491.8 239.5 %reduce-scatter.19.cloned.1.call-start = ((), (), s32[]{:S(2)}) async-start(), calls=%async_computation.26 | async-start | bytes 2654208 | tf_op jit(solution)/shard_map/reduce_scatter | solution.py:441
  610.2 37.6 %slice-start = ((s8[4718592]{0:T(1024)(128)(4,1)}), s8[524288]{0:T(1024)(128)(4,1)S(1)}, s32[]{:S(2)}) async-start(s8[4718592]{0:T(1024)(128)(4,1)} %bitcast.245), calls=%async_computation.36 | async-start | bytes 1048576 | tf_op jit(solution)/shard_map/cond
  611.9 35.9 %slice-start.1 = ((s8[4718592]{0:T(1024)(128)(4,1)}), s8[4194304]{0:T(1024)(128)(4,1)S(1)}, s32[]{:S(2)}) async-start(s8[4718592]{0:T(1024)(128)(4,1)} %bitcast.245), calls=%async_computation.37 | async-start | bytes 8388608 | tf_op jit(solution)/shard_map/cond
  683.1 9.2 copy-start.19
  688.9 88.0 %reduce-scatter.17.cloned.1.call-start = ((), (), s32[]{:S(2)}) async-start(), calls=%async_computation.25 | async-start | bytes 2654208 | tf_op jit(solution)/shard_map/reduce_scatter | solution.py:440
  692.3 130.2 %reduce-scatter.21.cloned.1.call-start = ((), (), s32[]{:S(2)}) async-start(), calls=%async_computation.27 | async-start | bytes 2654208 | tf_op jit(solution)/shard_map/reduce_scatter | solution.py:442
  694.8 3.7 copy-start.3
  694.8 3.7 copy-start.54
  694.8 164.5 %reduce-scatter.35.cloned.1.call-start = ((), (), s32[]{:S(2)}) async-start(), calls=%async_computation.34 | async-start | bytes 442368
  698.4 202.8 %reduce-scatter.33.cloned.1.call-start = ((), (), s32[]{:S(2)}) async-start(), calls=%async_computation.33 | async-start | bytes 442368
  701.1 231.9 %reduce-scatter.31.cloned.1.call-start = ((), (), s32[]{:S(2)}) async-start(), calls=%async_computation.32 | async-start | bytes 442368
  704.0 118.5 %copy-start.21 = (bf16[2,4,96,768]{3,2,1,0:T(8,128)(2,1)S(1)}, bf16[2,4,96,768]{3,2,1,0:T(8,128)(2,1)}, u32[]{:S(2)}) copy-start(bf16[2,4,96,768]{3,2,1,0:T(8,128)(2,1)} %copy.158) | copy-start | bytes 3538948
  704.1 288.1 %all-reduce.7.cloned.1.call-start = ((), (), s32[]{:S(2)}) async-start(), calls=%async_computation.35 | async-start | bytes 2359296 | tf_op jit(solution)/shard_map/psum | solution.py:453
  822.5 265.1 %reduce-scatter.27.cloned.1.call-start = ((), (), s32[]{:S(2)}) async-start(), calls=%async_computation.30 | async-start | bytes 14155776 | tf_op jit(solution)/shard_map/reduce_scatter | solution.py:445
  833.7 350.2 %reduce-scatter.29.cloned.1.call-start = ((), (), s32[]{:S(2)}) async-start(), calls=%async_computation.31 | async-start | bytes 14155776 | tf_op jit(solution)/shard_map/reduce_scatter | solution.py:446
  844.9 435.2 %reduce-scatter.25.cloned.1.call-start = ((), (), s32[]{:S(2)}) async-start(), calls=%async_computation.29 | async-start | bytes 14155776 | tf_op jit(solution)/shard_map/reduce_scatter | solution.py:444
  853.2 7.0 copy-start.76
  853.2 7.8 copy-start.62
  853.2 80.6 %copy-start.18 = (bf16[384,12,64]{0,2,1:T(8,128)(2,1)S(1)}, bf16[384,12,64]{0,2,1:T(8,128)(2,1)}, u32[]{:S(2)}) copy-start(bf16[384,12,64]{0,2,1:T(8,128)(2,1)} %copy-done.17) | copy-start | bytes 1769476
  853.2 80.6 %copy-start.30 = (bf16[768,768]{1,0:T(8,128)(2,1)S(1)}, bf16[768,768]{1,0:T(8,128)(2,1)}, u32[]{:S(2)}) copy-start(bf16[768,768]{1,0:T(8,128)(2,1)} %all-gather.17.cloned.1.call-done) | copy-start | bytes 3538948
  936.8 33.9 %copy-start.7 = (f32[384,768]{1,0:T(8,128)S(1)}, f32[384,768]{1,0:T(8,128)}, u32[]{:S(2)}) copy-start(f32[384,768]{1,0:T(8,128)} %copy-done.6) | copy-start | bytes 3538948
  992.1 291.3 %copy-start.52 = (f32[96,768]{1,0:T(8,128)S(1)}, f32[96,768]{1,0:T(8,128)}, u32[]{:S(2)}) copy-start(f32[96,768]{1,0:T(8,128)} %get-tuple-element.438) | copy-start | bytes 884740
  992.1 292.0 %copy-start.51 = (f32[96,768]{1,0:T(8,128)S(1)}, f32[96,768]{1,0:T(8,128)}, u32[]{:S(2)}) copy-start(f32[96,768]{1,0:T(8,128)} %get-tuple-element.439) | copy-start | bytes 884740
  1280.1 4.8 copy-start.1
  (49 other events, 86.7 us)
Sparse Core Ops, SparseCore 0:
  9.9 26.6 all-gather.16
  38.4 23.9 all-gather.12
  64.3 23.9 all-gather.18
  90.0 39.6 all-gather.14
  131.4 38.7 all-gather.20
  172.0 23.9 all-gather.22
  197.8 45.3 all-gather.24
  245.1 45.3 all-gather.26
  292.5 45.3 all-gather.28
  396.6 40.0 all-gather.30
  489.6 38.7 all-gather.32
  531.6 42.3 reduce-scatter.22
  689.0 42.2 reduce-scatter.18
  734.5 42.3 reduce-scatter.16
  780.1 42.3 reduce-scatter.20
  825.4 33.8 reduce-scatter.34
  862.3 33.8 reduce-scatter.32
  899.0 33.8 reduce-scatter.30
  935.6 56.5 all-reduce.6
  996.1 91.4 reduce-scatter.26
  1091.7 92.1 reduce-scatter.28
  1187.9 92.1 reduce-scatter.24
where the time goes:
time: 1300 us; the launch traced here: 1290 us
  waiting for transfers between devices  709 us (55%)
  matrix products  341 us (26%)
  blocking collectives  100 us (8%)
  local copies, waits for them, and re-layouts  59.5 us (5%)
  other arithmetic  43.6 us (3%)
  between operations  19.3 us (1%)
  starting transfers between devices  19.1 us (1%)
    reduce_scatter x1, waiting for transfers between devices, shards(): lax.psum_scatter(grad_down_local, 'context', scatter_dimension=1, tiled=T...  96.2 us
    reduce_scatter x1, waiting for transfers between devices, shards(): lax.psum_scatter(grad_gate_local, 'context', scatter_dimension=1, tiled=T...  96.2 us
    reduce_scatter x1, waiting for transfers between devices, shards(): lax.psum_scatter(grad_up_local, 'context', scatter_dimension=1, tiled=True)  95.5 us
    dot_general x3, matrix products, piece_scores(): jnp.einsum('qhd,khd->hqk', queries, key_rows, preferred_element_type=jnp....  70.7 us
    reduce_scatter x1, waiting for transfers between devices, shards(): lax.psum_scatter(grad_value_local, 'context', scatter_dimension=0, tiled=...  45.6 us
    reduce_scatter x1, waiting for transfers between devices, shards(): lax.psum_scatter(grad_query_local, 'context', scatter_dimension=0, tiled=...  45.6 us
    unnamed x25, waiting for transfers between devices  40.4 us
    psum x1, blocking collectives, shards(): grad_prior_weight = lax.psum(grad_prior_local, ('expert', 'context'))  39.3 us
  transfers between devices with their start and end apart: 26, of which 19 were waited for; matrix products, arithmetic and copies ran while one was open for 32% of the time, Pallas kernels for 0%

commit v1 on v0

v1 whole, which is shorter than its diff:
```python
import functools
import math

import jax
import jax.numpy as jnp
from jax import lax
from jax.experimental import pallas as pl
from jax.experimental.pallas import tpu as pltpu
from jax.sharding import PartitionSpec as P

HEADS = 12
FFN_E = 8
CAP = 96
TILE = 256
EXTRA = 16
HIDDEN_TILE = 256

EPS = 1e-06
THETA = 10000.0
NEGATIVE = -1e30
HIGH = lax.Precision.HIGHEST
F32 = jnp.float32
BF16 = jnp.bfloat16


def dot(left, right, left_dim=1, right_dim=0):
    return lax.dot_general(
        left, right, (((left_dim,), (right_dim,)), ((), ())), preferred_element_type=F32
    )


def turn(rows, cos_rows, sin_rows, heads, size, back=False):
    half = size // 2
    parts = []
    for head in range(heads):
        first = rows[head * size : head * size + half]
        second = rows[head * size + half : (head + 1) * size]
        if back:
            parts.append(first * cos_rows + second * sin_rows)
            parts.append(second * cos_rows - first * sin_rows)
        else:
            parts.append(first * cos_rows - second * sin_rows)
            parts.append(second * cos_rows + first * sin_rows)
    return jnp.concatenate(parts, axis=0)


def own_tile(index, ranks):
    rank = lax.rem(lax.axis_index("context"), ranks)
    place = lax.rem(index, 2)
    return (index // 2) * (2 * ranks) + jnp.where(place == 0, rank, 2 * ranks - 1 - rank)


def lanes(start):
    return pl.ds(pl.multiple_of(start * TILE, TILE), TILE)


def attn_forward_kernel(
    heads, size, ranks, scale,
    a_ref, wt_ref, cos_ref, sin_ref, ids_col_ref, ids_row_ref,
    out_ref, out_t_ref, lse_ref, query_t_ref, key_ref, key_t_ref, value_ref,
    value_t_ref, scores_ref, acc_ref,
):
    length = a_ref.shape[0]
    width = heads * size
    tiles = length // TILE
    own_tiles = tiles // ranks
    ext = size + EXTRA
    tail = (lax.broadcasted_iota(jnp.int32, (EXTRA, TILE), 0) == 0).astype(BF16)

    def project(step, carry):
        at = lanes(step)
        both = dot(wt_ref[width:, :], a_ref[at, :], 1, 1)
        key_t = turn(both[:width], cos_ref[:, at], sin_ref[:, at], heads, size)
        key_t_ref[:, at] = key_t.astype(BF16)
        value_t = both[width:]
        for head in range(heads):
            rows = slice(head * size, (head + 1) * size)
            key_ref[head, at, :] = key_t[rows].T.astype(BF16)
            value_ref[head, at, :] = value_t[rows].T.astype(BF16)
            value_t_ref[head * ext : head * ext + size, at] = value_t[rows].astype(BF16)
            value_t_ref[head * ext + size : (head + 1) * ext, at] = tail
        return carry

    lax.fori_loop(0, tiles, project, 0)

    def attend(index, carry):
        tile = own_tile(index, ranks)
        at = lanes(tile)
        query_t = dot(wt_ref[:width, :], a_ref[at, :], 1, 1)
        query_t = turn(query_t, cos_ref[:, at], sin_ref[:, at], heads, size)
        query_t = query_t.astype(BF16) * jnp.asarray(scale, BF16)
        query_t_ref[:, lanes(index)] = query_t
        query_ids = ids_row_ref[:, at]

        def score(step, tops, masked):
            here = lanes(step)
            fresh = []
            if masked:
                allowed = ids_col_ref[here, :] <= query_ids
            for head in range(heads):
                part = dot(key_ref[head, here, :], query_t[head * size : (head + 1) * size])
                if masked:
                    part = jnp.where(allowed, part, NEGATIVE)
                scores_ref[head, here, :] = part
                fresh.append(
                    jnp.maximum(tops[head], jnp.max(part.reshape(TILE // 8, 8, TILE), axis=0))
                )
            return tuple(fresh)

        tops = tuple(jnp.full((8, TILE), NEGATIVE, F32) for _ in range(heads))
        stop = jnp.minimum(tile + 2, tiles)
        tops = lax.fori_loop(0, tile, lambda s, c: score(s, c, False), tops)
        tops = lax.fori_loop(tile, stop, lambda s, c: score(s, c, True), tops)
        peaks = [jnp.max(top, axis=0, keepdims=True) for top in tops]
        acc_ref[...] = jnp.zeros_like(acc_ref)

        def combine(step, carry):
            here = lanes(step)
            for head in range(heads):
                weights = jnp.exp(scores_ref[head, here, :] - peaks[head]).astype(BF16)
                acc_ref[head] += dot(value_t_ref[head * ext : (head + 1) * ext, here], weights)
            return carry

        lax.fori_loop(0, stop, combine, 0)
        parts = []
        for head in range(heads):
            total = acc_ref[head, size : size + 1, :]
            part = acc_ref[head, :size, :] * (1.0 / total)
            lse_ref[head : head + 1, lanes(index)] = peaks[head] + jnp.log(total)
            parts.append(part)
        joined = jnp.concatenate(parts, axis=0)
        out_t_ref[:, lanes(index)] = joined
        out_ref[lanes(index), :] = joined.T.astype(BF16)
        return carry

    lax.fori_loop(0, own_tiles, attend, 0)


def attn_backward_kernel(
    heads, size, ranks, scale,
    grad_ref, a_ref, wt_ref, cos_ref, sin_ref, ids_col_ref, ids_row_ref,
    out_t_ref, lse_ref, query_t_ref, key_ref, key_t_ref, value_ref,
    da_ref, grad_w_ref,
    query_ref, own_grad_ref, dq_ref, dk_ref, dv_ref,
):
    length = a_ref.shape[0]
    width = heads * size
    tiles = length // TILE
    own_tiles = tiles // ranks
    dk_ref[...] = jnp.zeros_like(dk_ref)
    dv_ref[...] = jnp.zeros_like(dv_ref)
    da_ref[...] = jnp.zeros_like(da_ref)
    grad_w_ref[...] = jnp.zeros_like(grad_w_ref)

    def attend(index, carry):
        tile = own_tile(index, ranks)
        at = lanes(tile)
        query_t = query_t_ref[:, lanes(index)]
        grad_rows = grad_ref[lanes(index), :]
        grad_t = grad_rows.astype(F32).T
        query_rows = query_t.astype(F32).T.astype(BF16)
        query_ids = ids_row_ref[:, at]
        deltas, tops, grads_low = [], [], []
        for head in range(heads):
            rows = slice(head * size, (head + 1) * size)
            query_ref[head] = query_rows[:, rows]
            own_grad_ref[head] = grad_rows[:, rows]
            deltas.append(
                jnp.sum(grad_t[rows] * out_t_ref[rows, lanes(index)], axis=0, keepdims=True)
            )
            tops.append(lse_ref[head : head + 1, lanes(index)])
        grad_t_low = grad_t.astype(BF16)
        dq_ref[...] = jnp.zeros_like(dq_ref)

        def chunk(step, carry, masked):
            here = lanes(step)
            if masked:
                allowed = ids_col_ref[here, :] <= query_ids
            for head in range(heads):
                rows = slice(head * size, (head + 1) * size)
                scores = dot(key_ref[head, here, :], query_t[rows]) - tops[head]
                if masked:
                    scores = jnp.where(allowed, scores, NEGATIVE)
                probs = jnp.exp(scores)
                grad_probs = dot(value_ref[head, here, :], grad_t_low[rows])
                grad_scores = (probs * (grad_probs - deltas[head])).astype(BF16)
                dv_ref[head, here, :] += dot(probs.astype(BF16), own_grad_ref[head])
                dk_ref[head, here, :] += dot(grad_scores, query_ref[head])
                dq_ref[rows, :] += dot(key_t_ref[rows, here], grad_scores)
            return carry

        stop = jnp.minimum(tile + 2, tiles)
        lax.fori_loop(0, tile, lambda s, c: chunk(s, c, False), 0)
        lax.fori_loop(tile, stop, lambda s, c: chunk(s, c, True), 0)
        grad_query = turn(
            dq_ref[...] * scale, cos_ref[:, at], sin_ref[:, at], heads, size, back=True
        )
        grad_w_ref[:width, :] += dot(grad_query.astype(BF16), a_ref[at, :])
        da_ref[at, :] = dot(grad_query.T.astype(BF16), wt_ref[:width, :]).astype(BF16)
        return carry

    lax.fori_loop(0, own_tiles, attend, 0)

    def finish(step, carry):
        at = lanes(step)
        key_grad = jnp.concatenate([dk_ref[head, at, :].T for head in range(heads)], axis=0)
        key_grad = turn(key_grad, cos_ref[:, at], sin_ref[:, at], heads, size, back=True)
        value_grad = jnp.concatenate([dv_ref[head, at, :].T for head in range(heads)], axis=0)
        both = jnp.concatenate([key_grad, value_grad], axis=0)
        grad_w_ref[width:, :] += dot(both.astype(BF16), a_ref[at, :])
        total = da_ref[at, :].astype(F32) + dot(both.T.astype(BF16), wt_ref[width:, :])
        da_ref[at, :] = total.astype(BF16)
        return carry

    lax.fori_loop(0, tiles, finish, 0)


def expert_kernel(
    rows_ref, grad_ref, prob_ref, gate_ref, up_ref, down_ref,
    out_ref, grad_rows_ref, dot_ref, grad_gate_ref, grad_up_ref, grad_down_ref,
    rows_t_ref, dye_ref, out_acc_ref, grad_acc_ref,
):
    step = pl.program_id(1)

    @pl.when(step == 0)
    def _():
        rows_t_ref[...] = rows_ref[:, 0].reshape(dye_ref.shape).astype(F32).T.astype(BF16)
        grads = grad_ref[:, 0].reshape(dye_ref.shape).astype(F32)
        dye_ref[...] = (grads * prob_ref[0]).astype(BF16)
        out_acc_ref[...] = jnp.zeros_like(out_acc_ref)
        grad_acc_ref[...] = jnp.zeros_like(grad_acc_ref)

    rows = rows_ref[:, 0].reshape(dye_ref.shape)
    dye = dye_ref[...]
    gate = gate_ref[0]
    up = up_ref[0]
    down = down_ref[0]
    gate_pre = dot(rows, gate)
    up_pre = dot(rows, up)
    sigmoid = jax.nn.sigmoid(gate_pre)
    silu = gate_pre * sigmoid
    hidden = silu * up_pre
    hidden_low = hidden.astype(BF16)
    out_acc_ref[...] += dot(hidden_low, down)
    grad_hidden = dot(dye, down, 1, 1).astype(BF16).astype(F32)
    grad_down_ref[0] = dot(hidden.T.astype(BF16), dye).astype(BF16)
    grad_gate = (grad_hidden * up_pre * sigmoid * (1.0 + gate_pre * (1.0 - sigmoid))).astype(BF16)
    grad_up = (grad_hidden * silu).astype(BF16)
    grad_gate_ref[0] = dot(rows_t_ref[...], grad_gate).astype(BF16)
    grad_up_ref[0] = dot(rows_t_ref[...], grad_up).astype(BF16)
    grad_acc_ref[...] += dot(grad_gate, gate, 1, 1) + dot(grad_up, up, 1, 1)

    @pl.when(step == pl.num_programs(1) - 1)
    def _():
        out_low = out_acc_ref[...].astype(BF16)
        blocks = out_ref.shape[:1] + out_ref.shape[2:]
        out_ref[:, 0] = out_low.reshape(blocks)
        grad_rows_ref[:, 0] = grad_acc_ref[...].astype(BF16).reshape(blocks)
        grads = grad_ref[:, 0].reshape(dye_ref.shape).astype(F32)
        dot_ref[0] = jnp.sum(out_low.astype(F32) * grads, axis=1, keepdims=True)


def vmem(count):
    return [pl.BlockSpec(memory_space=pltpu.VMEM)] * count


def attn_forward(a_full, weights_t, cos_t, sin_t, ids, heads, size, ranks):
    length = a_full.shape[0]
    own = length // ranks
    width = heads * size
    ext = size + EXTRA
    shapes = (
        jax.ShapeDtypeStruct((own, width), BF16),
        jax.ShapeDtypeStruct((width, own), F32),
        jax.ShapeDtypeStruct((heads, own), F32),
        jax.ShapeDtypeStruct((width, own), BF16),
        jax.ShapeDtypeStruct((heads, length, size), BF16),
        jax.ShapeDtypeStruct((width, length), BF16),
        jax.ShapeDtypeStruct((heads, length, size), BF16),
    )
    return pl.pallas_call(
        functools.partial(attn_forward_kernel, heads, size, ranks, size ** (-0.5)),
        out_shape=shapes,
        in_specs=vmem(6),
        out_specs=vmem(7),
        scratch_shapes=[
            pltpu.VMEM((heads * ext, length), BF16),
            pltpu.VMEM((heads, length, TILE), F32),
            pltpu.VMEM((heads, ext, TILE), F32),
        ],
        compiler_params=pltpu.CompilerParams(vmem_limit_bytes=60 << 20),
        cost_estimate=cost(37),
        name="attn_forward",
    )(a_full, weights_t, cos_t, sin_t, ids[:, None], ids[None, :])


def attn_backward(grad_full, a_full, weights_t, cos_t, sin_t, ids, kept, heads, size, ranks):
    length = a_full.shape[0]
    width = heads * size
    shapes = (
        jax.ShapeDtypeStruct(a_full.shape, BF16),
        jax.ShapeDtypeStruct(weights_t.shape, F32),
    )
    return pl.pallas_call(
        functools.partial(attn_backward_kernel, heads, size, ranks, size ** (-0.5)),
        out_shape=shapes,
        in_specs=vmem(13),
        out_specs=vmem(2),
        scratch_shapes=[
            pltpu.VMEM((heads, TILE, size), BF16),
            pltpu.VMEM((heads, TILE, size), BF16),
            pltpu.VMEM((width, TILE), F32),
            pltpu.VMEM((heads, length, size), F32),
            pltpu.VMEM((heads, length, size), F32),
        ],
        compiler_params=pltpu.CompilerParams(vmem_limit_bytes=63 << 20),
        cost_estimate=cost(58),
        name="attn_backward",
    )(grad_full, a_full, weights_t, cos_t, sin_t, ids[:, None], ids[None, :], *kept)


def experts(rows, grads, gates, gate_full, up_full, down_full):
    owners, count, cap, width = rows.shape
    slots = owners * cap
    hidden = gate_full.shape[2]
    per_row = pl.BlockSpec((owners, 1, cap, width), lambda e, t: (0, e, 0, 0))
    column = pl.BlockSpec((1, slots, 1), lambda e, t: (e, 0, 0))
    wide = pl.BlockSpec((1, width, HIDDEN_TILE), lambda e, t: (e, 0, t))
    tall = pl.BlockSpec((1, HIDDEN_TILE, width), lambda e, t: (e, t, 0))
    return pl.pallas_call(
        expert_kernel,
        grid=(count, hidden // HIDDEN_TILE),
        out_shape=(
            jax.ShapeDtypeStruct(rows.shape, BF16),
            jax.ShapeDtypeStruct(rows.shape, BF16),
            jax.ShapeDtypeStruct((count, slots, 1), F32),
            jax.ShapeDtypeStruct(gate_full.shape, BF16),
            jax.ShapeDtypeStruct(up_full.shape, BF16),
            jax.ShapeDtypeStruct(down_full.shape, BF16),
        ),
        in_specs=[per_row, per_row, column, wide, wide, tall],
        out_specs=(per_row, per_row, column, wide, wide, tall),
        scratch_shapes=[
            pltpu.VMEM((width, slots), BF16),
            pltpu.VMEM((slots, width), BF16),
            pltpu.VMEM((slots, width), F32),
            pltpu.VMEM((slots, width), F32),
        ],
        compiler_params=pltpu.CompilerParams(vmem_limit_bytes=60 << 20),
        cost_estimate=cost(37),
        name="experts",
    )(rows, grads, gates, gate_full, up_full, down_full)


def cost(micros):
    return pl.CostEstimate(flops=micros * 1_150_000_000, bytes_accessed=0, transcendentals=0)


def swap_kernel(axis, stride, count, same, *refs):
    total = len(same)
    sources, targets = refs[:total], refs[total : 2 * total]
    local_sem, send_sem, recv_sem = refs[2 * total :]
    place = lax.axis_index(axis)
    mine = lax.rem(place // stride, count)
    barrier = pltpu.get_barrier_semaphore()
    for far in range(1, count):
        peer = lax.rem(mine + far, count)
        pl.semaphore_signal(
            barrier, inc=1, device_id={axis: place + (peer - mine) * stride},
            device_id_type=pl.DeviceIdType.MESH,
        )
    pl.semaphore_wait(barrier, count - 1)
    copies = []
    for item in range(total):
        for far in range(1, count):
            peer = lax.rem(mine + far, count)
            copies.append(
                pltpu.make_async_remote_copy(
                    src_ref=sources[item] if same[item] else sources[item].at[peer],
                    dst_ref=targets[item].at[mine],
                    send_sem=send_sem.at[item, far],
                    recv_sem=recv_sem.at[item, far],
                    device_id={axis: place + (peer - mine) * stride},
                    device_id_type=pl.DeviceIdType.MESH,
                )
            )
            copies[-1].start()
    for item in range(total):
        copies.append(
            pltpu.make_async_copy(
                sources[item] if same[item] else sources[item].at[mine],
                targets[item].at[mine],
                local_sem.at[item],
            )
        )
        copies[-1].start()
    for copy in copies:
        copy.wait()


def swap(arrays, axis, stride, count, number, same=None):
    same = same or (False,) * len(arrays)
    shapes = tuple(
        jax.ShapeDtypeStruct(((count,) if own else ()) + array.shape, array.dtype)
        for array, own in zip(arrays, same)
    )
    return pl.pallas_call(
        functools.partial(swap_kernel, axis, stride, count, same),
        out_shape=shapes,
        in_specs=vmem(len(arrays)),
        out_specs=vmem(len(arrays)),
        scratch_shapes=[
            pltpu.SemaphoreType.DMA((len(arrays),)),
            pltpu.SemaphoreType.DMA((len(arrays), count)),
            pltpu.SemaphoreType.DMA((len(arrays), count)),
        ],
        compiler_params=pltpu.CompilerParams(
            collective_id=number, has_side_effects=True, vmem_limit_bytes=60 << 20
        ),
        name="swap",
    )(*arrays)


def gather_kernel(chips, ranks, split, *refs):
    total = len(split)
    sources, targets = refs[:total], refs[total : 2 * total]
    local_sem, send_sem, recv_sem, pass_sem, land_sem = refs[2 * total :]
    place = lax.axis_index("context")
    chip, core = place // 2, lax.rem(place, 2)
    partner = 2 * chip + 1 - core

    def piece(item, device):
        return sources[item].at[device // ranks] if split[item] else sources[item]

    def remote(source, target, send, recv, device):
        return pltpu.make_async_remote_copy(
            src_ref=source, dst_ref=target, send_sem=send, recv_sem=recv,
            device_id={"context": device}, device_id_type=pl.DeviceIdType.MESH,
        )

    barrier = pltpu.get_barrier_semaphore()
    for far in range(1, chips):
        pl.semaphore_signal(
            barrier, inc=1, device_id={"context": 2 * lax.rem(chip + far, chips) + core},
            device_id_type=pl.DeviceIdType.MESH,
        )
    pl.semaphore_signal(
        barrier, inc=1, device_id={"context": partner}, device_id_type=pl.DeviceIdType.MESH
    )
    pl.semaphore_wait(barrier, chips)
    sent = {}
    for item in range(total):
        for far in range(chips):
            peer = partner if far == 0 else 2 * lax.rem(chip + far, chips) + core
            sent[item, far] = remote(
                piece(item, peer), targets[item].at[place],
                send_sem.at[item, far], recv_sem.at[item, far], peer,
            )
            sent[item, far].start()
    local = []
    for item in range(total):
        local.append(
            pltpu.make_async_copy(
                piece(item, place), targets[item].at[place], local_sem.at[item]
            )
        )
        local[-1].start()
    passed = []
    for item in range(total):
        for far in range(1, chips):
            sent[item, far].wait_recv()
            block = targets[item].at[2 * lax.rem(chip + chips - far, chips) + core]
            passed.append(
                remote(block, block, pass_sem.at[item, far], land_sem.at[item, far], partner)
            )
            passed[-1].start()
    for item in range(total):
        sent[item, 0].wait_recv()
        for far in range(chips):
            sent[item, far].wait_send()
    for copy in local + passed:
        copy.wait()


def gather(arrays, split, context, ranks, number):
    chips = context // 2
    total = len(arrays)
    shapes = tuple(
        jax.ShapeDtypeStruct((context,) + (array.shape[1:] if cut else array.shape), array.dtype)
        for array, cut in zip(arrays, split)
    )
    return pl.pallas_call(
        functools.partial(gather_kernel, chips, ranks, split),
        out_shape=shapes,
        in_specs=vmem(total),
        out_specs=vmem(total),
        scratch_shapes=[pltpu.SemaphoreType.DMA((total,))]
        + [pltpu.SemaphoreType.DMA((total, chips))] * 4,
        compiler_params=pltpu.CompilerParams(
            collective_id=number, has_side_effects=True, vmem_limit_bytes=60 << 20
        ),
        name="gather",
    )(*arrays)


def granule_kernel(ranks, shard_granules, outward, source_ref, target_ref, send_sem, recv_sem):
    place = lax.axis_index("context")
    context = lax.axis_size("context")
    group, rank = place // ranks, lax.rem(place, ranks)
    groups = context // ranks
    owned = context * shard_granules // ranks
    barrier = pltpu.get_barrier_semaphore()
    for far in range(1, context):
        pl.semaphore_signal(
            barrier, inc=1, device_id={"context": lax.rem(place + far, context)},
            device_id_type=pl.DeviceIdType.MESH,
        )
    pl.semaphore_wait(barrier, context - 1)

    def owner_rank(granule):
        spot = lax.rem(granule // 2, 2 * ranks)
        return jnp.minimum(spot, 2 * ranks - 1 - spot)

    def owner_slot(granule):
        tile = granule // 2
        spot = lax.rem(tile, 2 * ranks)
        upper = jnp.where(spot >= ranks, 1, 0)
        return (tile // (2 * ranks) * 2 + upper) * 2 + lax.rem(granule, 2)

    def granule_of(slot):
        return own_tile(slot // 2, ranks) * 2 + lax.rem(slot, 2)

    def remote(source, target, index, device):
        return pltpu.make_async_remote_copy(
            src_ref=source, dst_ref=target, send_sem=send_sem.at[index],
            recv_sem=recv_sem.at[index], device_id={"context": device},
            device_id_type=pl.DeviceIdType.MESH,
        )

    def outgoing(step):
        if outward:
            granule = granule_of(step)
            home = granule // shard_granules
            slot = group * shard_granules + lax.rem(granule, shard_granules)
            return home, source_ref.at[step], slot
        other, spot = step // shard_granules, step % shard_granules
        granule = place * shard_granules + spot
        return other * ranks + owner_rank(granule), source_ref.at[step], owner_slot(granule)

    def incoming(step):
        if outward:
            other, spot = step // shard_granules, step % shard_granules
            return other * ranks + owner_rank(place * shard_granules + spot)
        return granule_of(step) // shard_granules

    for step in range(owned):
        device, source, slot = outgoing(step)

        @pl.when(device == place)
        def _():
            pltpu.make_async_copy(source, target_ref.at[slot], recv_sem.at[slot]).start()

        @pl.when(device != place)
        def _():
            pltpu.make_async_remote_copy(
                src_ref=source, dst_ref=target_ref.at[slot], send_sem=send_sem.at[step],
                recv_sem=recv_sem.at[slot], device_id={"context": device},
                device_id_type=pl.DeviceIdType.MESH,
            ).start()

    for step in range(owned):
        device, source, slot = outgoing(step)

        @pl.when(device != place)
        def _():
            remote(source, target_ref.at[slot], step, device).wait_send()

        sender = incoming(step)

        @pl.when(sender == place)
        def _():
            pltpu.make_async_copy(source_ref.at[0], target_ref.at[step], recv_sem.at[step]).wait()

        @pl.when(sender != place)
        def _():
            remote(source_ref.at[0], target_ref.at[step], step, sender).wait_recv()


def granules(rows, ranks, shard_granules, outward, number):
    owned = rows.shape[0]
    return pl.pallas_call(
        functools.partial(granule_kernel, ranks, shard_granules, outward),
        out_shape=jax.ShapeDtypeStruct(rows.shape, rows.dtype),
        in_specs=vmem(1),
        out_specs=vmem(1)[0],
        scratch_shapes=[
            pltpu.SemaphoreType.DMA((owned,)),
            pltpu.SemaphoreType.DMA((owned,)),
        ],
        compiler_params=pltpu.CompilerParams(
            collective_id=number, has_side_effects=True, vmem_limit_bytes=60 << 20
        ),
        name="granules",
    )(rows)


def exchange(value, axis_name, axis):
    return lax.all_to_all(value, axis_name, split_axis=axis, concat_axis=axis, tiled=True)


def shards(
    hidden_in,
    prior_logits,
    routes,
    block_ids,
    grad_out,
    attn_gain,
    query_weight,
    key_weight,
    value_weight,
    output_weight,
    moe_gain,
    router_weight,
    prior_weight,
    const_mix,
    const_vector,
    gate_weight,
    up_weight,
    down_weight,
):
    token_rows = hidden_in.shape[1]
    model_width = hidden_in.shape[2]
    head_size = model_width // HEADS
    context = lax.axis_size("context")
    owners = lax.axis_size("expert")
    groups = math.gcd(HEADS, context)
    ranks = context // groups
    heads = HEADS // groups
    width = heads * head_size
    length = context * token_rows
    per_owner = gate_weight.shape[0]
    slot_count = per_owner * owners * CAP
    shard_width = model_width // context
    residual = hidden_in[0].astype(F32)
    prior_rows = prior_logits[0]
    route_rows = routes[0]
    cotangent_low = grad_out[0]
    cotangent = cotangent_low.astype(F32)

    inv_rms1 = lax.rsqrt(jnp.mean(residual * residual, axis=1, keepdims=True) + EPS)
    normed_one = residual * inv_rms1
    attn_input = (normed_one * attn_gain).astype(BF16)
    ids_wide = jnp.broadcast_to(block_ids.astype(F32), (8, token_rows))
    stacked = jnp.stack([query_weight, key_weight, value_weight])
    stacked = stacked.reshape(3, shard_width, groups, width)
    pieces = jnp.transpose(stacked, (2, 0, 3, 1)).reshape(groups, 3 * width, shard_width)
    ids_all, w_all, a_all, output_all = gather(
        (ids_wide, pieces, attn_input, output_weight),
        (False, True, False, False), context, ranks, 0,
    )
    a_full = a_all.reshape(length, model_width)
    output_full = output_all.reshape(model_width, model_width)
    ids = ids_all[:, 0, :].reshape(length)
    weights_t = jnp.transpose(w_all, (1, 0, 2)).reshape(3 * width, model_width)
    half = head_size // 2
    freq = jnp.power(THETA, -2.0 * jnp.arange(half, dtype=F32) / head_size)
    angle = freq[:, None] * jnp.arange(length, dtype=jnp.int32).astype(F32)[None, :]
    cos_t, sin_t = jnp.cos(angle), jnp.sin(angle)

    flat_route = route_rows.reshape(-1)
    ffn_hot = (flat_route[:, None] == jnp.arange(FFN_E, dtype=jnp.int32)[None, :]).astype(jnp.int32)
    before = jnp.sum((jnp.cumsum(ffn_hot, axis=0) - ffn_hot) * ffn_hot, axis=1)
    slot_index = jnp.where(
        flat_route < FFN_E,
        flat_route * CAP + before,
        -1,
    ).reshape(token_rows, 2)
    slot_ids = jnp.arange(slot_count, dtype=jnp.int32)[:, None]
    hit_first = slot_ids == slot_index[None, :, 0]
    hit_second = slot_ids == slot_index[None, :, 1]
    pick_first = hit_first.astype(BF16)
    pick_second = hit_second.astype(BF16)
    pick_either = pick_first + pick_second

    blocks = (owners, per_owner, CAP, model_width)

    def pick(rows):
        return jnp.dot(pick_either, rows, preferred_element_type=F32).astype(BF16).reshape(blocks)

    grad_arrived = exchange(pick(cotangent_low), "expert", 0)

    (
        attn_out, out_t, log_total, query_t, key_heads, key_t, value_heads,
    ) = attn_forward(a_full, weights_t, cos_t, sin_t, ids, heads, head_size, ranks)
    kept = (out_t, log_total, query_t, key_heads, key_t, value_heads)
    gate_full = lax.all_gather(gate_weight, "context", axis=1, tiled=True)
    up_full = lax.all_gather(up_weight, "context", axis=1, tiled=True)
    down_full = lax.all_gather(down_weight, "context", axis=1, tiled=True)
    granule = TILE // 2
    shard_granules = token_rows // granule
    out_blocks = granules(
        attn_out.reshape(-1, granule, width), ranks, shard_granules, True, 1
    ).reshape(groups, token_rows, width)
    mix_low = jnp.transpose(out_blocks, (1, 0, 2)).reshape(token_rows, model_width)

    after_attn = residual + jnp.dot(mix_low, output_full, preferred_element_type=F32)
    inv_rms2 = lax.rsqrt(jnp.mean(after_attn * after_attn, axis=1, keepdims=True) + EPS)
    normed_two = after_attn * inv_rms2
    moe_input = normed_two * moe_gain
    narrow = jnp.concatenate(
        [router_weight, jnp.transpose(const_mix.reshape(-1, model_width))], axis=1
    )
    narrow_out = jnp.dot(moe_input, narrow, precision=HIGH, preferred_element_type=F32)
    expert_count = router_weight.shape[1]
    consts = const_mix.shape[0]
    logits = narrow_out[:, :expert_count] + jnp.dot(
        prior_rows, prior_weight, precision=HIGH, preferred_element_type=F32
    )
    probs = jax.nn.softmax(logits, axis=1)
    expert_ids = jnp.arange(expert_count, dtype=jnp.int32)
    first_hot = (route_rows[:, 0:1] == expert_ids[None, :]).astype(F32)
    second_hot = (route_rows[:, 1:2] == expert_ids[None, :]).astype(F32)
    chosen = first_hot + second_hot
    gated = probs * chosen
    first_gate = jnp.sum(probs * first_hot, axis=1, keepdims=True)
    second_gate = jnp.sum(probs * second_hot, axis=1, keepdims=True)
    slot_gate = jnp.sum(
        jnp.where(hit_first, first_gate[None, :, 0], 0.0)
        + jnp.where(hit_second, second_gate[None, :, 0], 0.0),
        axis=1,
    )
    def spread(values):
        values = values.reshape(owners, per_owner, CAP)
        return jnp.pad(values, ((0, 0), (0, 8 - per_owner), (0, 128 - CAP)))

    gates, arrived = swap(
        (spread(slot_gate), pick(moe_input.astype(BF16))), "expert", 1, owners, 2
    )
    gates = jnp.transpose(gates[:, :per_owner, :CAP], (1, 0, 2)).reshape(per_owner, -1, 1)

    expert_out, grad_rows, owner_dot, grad_gate, grad_up, grad_down = experts(
        arrived, grad_arrived, gates, gate_full, up_full, down_full
    )
    share_gate = lax.psum_scatter(grad_gate, "context", scatter_dimension=1, tiled=True)
    share_up = lax.psum_scatter(grad_up, "context", scatter_dimension=1, tiled=True)
    share_down = lax.psum_scatter(grad_down, "context", scatter_dimension=1, tiled=True)

    owner_dot = jnp.transpose(owner_dot.reshape(per_owner, owners, CAP), (1, 0, 2))
    slot_dot, grad_back = swap((spread(owner_dot), grad_rows), "expert", 1, owners, 3)
    slot_dot = slot_dot[:, :per_owner, :CAP].reshape(slot_count)
    grad_back = grad_back.reshape(slot_count, model_width)
    returned = exchange(expert_out, "expert", 0).reshape(slot_count, model_width)

    const_soft = jax.nn.softmax(narrow_out[:, expert_count:].reshape(token_rows, consts, 2), axis=2)
    const_gate = gated[:, FFN_E + 2 :]
    copy_gate = gated[:, FFN_E + 1 : FFN_E + 2]
    const_out = [
        const_soft[:, c, 0:1] * moe_input + const_soft[:, c, 1:2] * const_vector[c][None, :]
        for c in range(consts)
    ]
    local_moe = copy_gate * moe_input
    for c in range(consts):
        local_moe = local_moe + const_gate[:, c : c + 1] * const_out[c]
    grad_moe_ffn = lax.dot_general(
        pick_either, grad_back, (((0,), (0,)), ((), ())), preferred_element_type=F32
    )
    first_dot = jnp.sum(jnp.where(hit_first, slot_dot[:, None], 0.0), axis=0)[:, None]
    second_dot = jnp.sum(jnp.where(hit_second, slot_dot[:, None], 0.0), axis=0)[:, None]
    copy_dot = jnp.sum(cotangent * moe_input, axis=1, keepdims=True)
    const_dot = [jnp.sum(cotangent * const_out[c], axis=1, keepdims=True) for c in range(consts)]
    extra = jnp.concatenate(
        [jnp.zeros((token_rows, FFN_E + 1), F32), copy_dot, *const_dot], axis=1
    )
    grad_probs = first_hot * first_dot + second_hot * second_dot + chosen * extra
    grad_logits = probs * (grad_probs - jnp.sum(probs * grad_probs, axis=1, keepdims=True))
    grad_prior_rows = lax.dot_general(
        grad_logits, prior_weight, (((1,), (1,)), ((), ())),
        precision=HIGH, preferred_element_type=F32,
    )
    vector_dot = jnp.dot(
        cotangent, jnp.transpose(const_vector), precision=HIGH, preferred_element_type=F32
    )
    grad_soft = jnp.stack(
        [const_gate * copy_dot, const_gate * vector_dot], axis=2
    )
    grad_mix = const_soft * (grad_soft - jnp.sum(const_soft * grad_soft, axis=2, keepdims=True))
    narrow_grad = jnp.concatenate([grad_logits, grad_mix.reshape(token_rows, -1)], axis=1)
    local_scale = copy_gate + jnp.sum(const_soft[:, :, 0] * const_gate, axis=1, keepdims=True)
    grad_moe_input = (
        grad_moe_ffn
        + lax.dot_general(
            narrow_grad, narrow, (((1,), (1,)), ((), ())),
            precision=HIGH, preferred_element_type=F32,
        )
        + local_scale * cotangent
    )
    small_moe = lax.dot_general(
        narrow_grad, moe_input, (((0,), (0,)), ((), ())),
        precision=HIGH, preferred_element_type=F32,
    )
    small_vector = lax.dot_general(
        const_soft[:, :, 1] * const_gate, cotangent, (((0,), (0,)), ((), ())),
        precision=HIGH, preferred_element_type=F32,
    )
    grad_prior_local = lax.dot_general(
        prior_rows, grad_logits, (((0,), (0,)), ((), ())),
        precision=HIGH, preferred_element_type=F32,
    )
    small_gain = jnp.sum(grad_moe_input * normed_two, axis=0, keepdims=True)
    prior_values = jnp.pad(
        grad_prior_local.reshape(-1), (0, -(expert_count * expert_count) % shard_width)
    ).reshape(-1, 1, shard_width)
    prior_lines = prior_values.shape[0]
    small = jnp.concatenate([small_moe, small_vector, small_gain], axis=0)
    small_lines = small.shape[0]
    small = jnp.concatenate(
        [
            small.reshape(small_lines, context, shard_width),
            jnp.broadcast_to(prior_values, (prior_lines, context, shard_width)),
        ],
        axis=0,
    )
    small = jnp.pad(small, ((0, -small.shape[0] % 8), (0, 0), (0, 0)))

    grad_normed_two = grad_moe_input * moe_gain
    grad_after = cotangent + inv_rms2 * (
        grad_normed_two - normed_two * jnp.mean(grad_normed_two * normed_two, axis=1, keepdims=True)
    )
    grad_attn_low = grad_after.astype(BF16)
    grad_mix_low = lax.dot_general(
        grad_attn_low, output_full, (((1,), (1,)), ((), ())), preferred_element_type=F32
    ).astype(BF16)
    grad_pieces = jnp.transpose(grad_mix_low.reshape(token_rows, groups, width), (1, 0, 2))
    grad_own = granules(
        grad_pieces.reshape(-1, granule, width), ranks, shard_granules, False, 4
    ).reshape(-1, width)
    grad_output_local = lax.dot_general(
        mix_low, grad_attn_low, (((0,), (0,)), ((), ())), preferred_element_type=F32
    ).astype(BF16)
    output_parts = exchange(
        grad_output_local.reshape(context, shard_width, model_width), "context", 0
    )

    da_part, grad_w = attn_backward(
        grad_own, a_full, weights_t, cos_t, sin_t, ids, kept, heads, head_size, ranks
    )
    chips = context // 2
    core = lax.rem(lax.axis_index("context"), 2)
    both_parts = jnp.concatenate(
        [grad_w.reshape(3 * width, context, shard_width), small], axis=0
    )
    both_lines = both_parts.shape[0]
    both_parts = jnp.transpose(both_parts, (1, 0, 2)).reshape(chips, 2, both_lines, shard_width)
    da_part = da_part.reshape(chips, 2, token_rows, model_width)
    da_twin, both_twin = swap(
        (jnp.swapaxes(da_part, 0, 1), jnp.swapaxes(both_parts, 0, 1)), "context", 1, 2, 5
    )
    da_chip = (da_twin[0].astype(F32) + da_twin[1].astype(F32)).astype(BF16)
    both_chip = both_twin[0] + both_twin[1]
    da_all, both_all = swap((da_chip, both_chip), "context", 2, chips, 6)
    grad_attn_input = jnp.sum(da_all.astype(F32), axis=0)
    grad_normed_one = grad_attn_input * attn_gain
    grad_input = grad_after + inv_rms1 * (
        grad_normed_one - normed_one * jnp.mean(grad_normed_one * normed_one, axis=1, keepdims=True)
    )

    per_group = ranks // 2
    w_blocks = both_all[:, : 3 * width].reshape(groups, per_group, 3, width, shard_width)
    w_blocks = jnp.sum(w_blocks, axis=1)
    w_share = jnp.transpose(w_blocks, (1, 3, 0, 2)).reshape(3, shard_width, model_width)
    output_share = jnp.sum(output_parts.astype(F32), axis=0)
    shares = jnp.concatenate([w_share, output_share[None]], axis=0).reshape(
        4, owners, shard_width // owners, model_width
    )
    shares = jnp.transpose(shares.astype(BF16), (1, 0, 2, 3))
    small_ctx = jnp.sum(both_all[:, 3 * width :], axis=0)
    shares_all, small_all = swap((shares, small_ctx), "expert", 1, owners, 7, (False, True))
    share_sum = jnp.sum(shares_all.astype(F32), axis=0).astype(BF16)
    (sums,) = swap((share_sum,), "expert", 1, owners, 8, (True,))
    sums = jnp.transpose(sums.astype(F32), (1, 0, 2, 3)).reshape(4, shard_width, model_width)
    w_sum, output_sum = sums[:3], sums[3]
    small_own = jnp.sum(small_all, axis=0)
    grad_attn_gain = jnp.sum(
        w_sum[0] * query_weight.astype(F32)
        + w_sum[1] * key_weight.astype(F32)
        + w_sum[2] * value_weight.astype(F32),
        axis=1,
    )
    column = lax.axis_index("context") * shard_width
    grad_attn_gain = grad_attn_gain / lax.dynamic_slice_in_dim(attn_gain, column, shard_width)
    mixes = expert_count + 2 * consts
    grad_prior_weight = small_own[small_lines : small_lines + prior_lines].reshape(-1)
    grad_prior_weight = grad_prior_weight[: expert_count * expert_count].reshape(
        expert_count, expert_count
    )
    layer_out = after_attn + local_moe
    layer_out = layer_out + first_gate * lax.dot_general(
        pick_first, returned, (((0,), (0,)), ((), ())), preferred_element_type=F32
    )
    layer_out = layer_out + second_gate * lax.dot_general(
        pick_second, returned, (((0,), (0,)), ((), ())), preferred_element_type=F32
    )
    return (
        layer_out.astype(BF16)[None],
        grad_input[None],
        grad_prior_rows[None],
        grad_attn_gain,
        w_sum[0],
        w_sum[1],
        w_sum[2],
        output_sum,
        small_own[small_lines - 1],
        jnp.transpose(small_own[:expert_count]),
        grad_prior_weight,
        small_own[expert_count:mixes].reshape(consts, 2, shard_width),
        small_own[mixes : mixes + consts],
        share_gate.astype(F32),
        share_up.astype(F32),
        share_down.astype(F32),
    )


def solution(mesh):
    return jax.shard_map(
        shards,
        mesh=mesh,
        in_specs=(
            P("expert", "context", None),
            P("expert", "context", None),
            P("expert", "context", None),
            P("expert", "context"),
            P("expert", "context", None),
            P(),
            P("context", None),
            P("context", None),
            P("context", None),
            P("context", None),
            P(),
            P(),
            P(),
            P(),
            P(),
            P("expert", "context", None),
            P("expert", "context", None),
            P("expert", "context", None),
        ),
        out_specs=(
            P("expert", "context", None),
            P("expert", "context", None),
            P("expert", "context", None),
            P("context"),
            P("context", None),
            P("context", None),
            P("context", None),
            P("context", None),
            P("context"),
            P("context", None),
            P(),
            P(None, None, "context"),
            P(None, "context"),
            P("expert", "context", None),
            P("expert", "context", None),
            P("expert", "context", None),
        ),
        check_vma=False,
    )
```

time: 1300 us -> 569 us (0.44)
  waiting for transfers between devices: 709 us -> 2.64 us
  Pallas kernels: 0 us -> 424 us
  matrix products: 341 us -> 25.6 us
  blocking collectives: 100 us -> 0 us
  local copies, waits for them, and re-layouts: 59.5 us -> 43.9 us
    pallas_call x0 -> x12, Pallas kernels: none -> 424 us  [the longest x6 189 us: swap(): pl.pallas_call(functools.partial(swap_kernel, axis, stride, count, same),...]
    reduce_scatter x7 -> x3, waiting for transfers between devices: 406 us -> 0.01 us  [the longest x1 0.01 us: shards(): lax.psum_scatter(grad_gate, 'context', scatter_dimension=1, tiled=True)]
    dot_general x44 -> x14, matrix products: 338 us -> 23.2 us  [the longest x2 3.79 us: pick(): jnp.dot(pick_either, rows, preferred_element_type=F32).astype(BF16)]
    all_gather x11 -> x3, waiting for transfers between devices: 160 us -> 0.02 us  [the longest x1 0.01 us: shards(): down_full = lax.all_gather(down_weight, 'context', axis=1, tiled=True)]
    all_to_all x4 -> x3, waiting for transfers between devices: 81.6 us -> 0.01 us  [exchange(): lax.all_to_all(value, axis_name, split_axis=axis, concat_axis=axis, tiled...]
    psum x2 -> x0, blocking collectives: 59.2 us -> none  [the longest x1 39.3 us: shards(): grad_prior_weight = lax.psum(grad_prior_local, ('expert', 'context'))]
    unnamed x25 -> x6, waiting for transfers between devices: 40.4 us -> 2.61 us
    all_gather x3 -> x0, blocking collectives: 28.2 us -> none  [the longest x1 11 us: shards(): lax.all_gather(jnp.transpose(log_total), 'context', axis=0, tiled=True)]
  transfers between devices with their start and end apart: 26 -> 9, of which waited for: 19 -> 0; matrix products, arithmetic and copies ran while one was open for 32% -> 18% of each run, Pallas kernels for 0% -> 68%
where the time goes in v1:
time: 569 us; the launch traced here: 567 us
  Pallas kernels  424 us (75%)
  local copies, waits for them, and re-layouts  43.9 us (8%)
  other arithmetic  38.7 us (7%)
  matrix products  25.6 us (4%)
  starting transfers between devices  17.2 us (3%)
  between operations  15.4 us (3%)
    pallas_call x6, Pallas kernels, swap(): pl.pallas_call(functools.partial(swap_kernel, axis, stride, count, same),...  189 us
    pallas_call x1, Pallas kernels, gather(): pl.pallas_call(functools.partial(gather_kernel, chips, ranks, split), out...  66.9 us
    pallas_call x1, Pallas kernels, attn_backward(): pl.pallas_call(functools.partial(attn_backward_kernel, heads, size, ranks...  57.8 us
    pallas_call x1, Pallas kernels, experts(): pl.pallas_call(expert_kernel, grid=(count, hidden // HIDDEN_TILE), out_sh...  37.3 us
    pallas_call x1, Pallas kernels, attn_forward(): pl.pallas_call(functools.partial(attn_forward_kernel, heads, size, ranks,...  37.2 us
    pallas_call x2, Pallas kernels, granules(): pl.pallas_call(functools.partial(granule_kernel, ranks, shard_granules, o...  35.8 us
    all_to_all x3, starting transfers between devices, exchange(): lax.all_to_all(value, axis_name, split_axis=axis, concat_axis=axis, tiled...  16.7 us
  transfers between devices with their start and end apart: 9, of which 0 were waited for; matrix products, arithmetic and copies ran while one was open for 18% of the time, Pallas kernels for 68%

profile of v1, /device:TPU:0, one launch (start us, length us, event | category | flops | bytes accessed | tf_op | source)
XLA Modules:
  0.0 567.3 jit_solution(5336308811667885319)
XLA Ops:
  9.9 1.7 reduce-window.6
  12.7 1.8 convolution_convert_fusion.1
  14.5 6.5 %all-to-all-start = ((bf16[4,2,96,768]{3,2,1,0:T(8,128)(2,1)}), bf16[4,2,96,768]{3,2,1,0:T(8,128)(2,1)}, u32[]{:S(2)}, u32[]{:S(2)}) async-start(bf16[4,2,96,768]{3,2,1,0:T(8,128)(2,1)} %bitcast.24), calls=%async_computation | async-start | bytes 2359296 | tf_op jit(solution)/shard_map/all_to_all | solution.py:608
  21.6 0.9 pad_maximum_fusion.1
  22.8 1.0 fusion.9.refs_2_
  24.4 66.9 %gather.1 = (f32[8,8,384]{2,1,0:T(8,128)}, bf16[8,576,96]{2,1,0:T(8,128)(2,1)}, bf16[8,384,768]{2,1,0:T(8,128)(2,1)}, bf16[8,96,768]{2,1,0:T(8,128)(2,1)}) custom-call(f32[8,384]{1,0:T(8,128)} %broadcast_in_dim.103.refs_0_, bf16[4,576,96]{2,1,0:T(8,128)(2,1)} %bitcast.169, bf16[384,768]{1,0:T(8,128)(2,1)} %fusion.9.refs_2_, bf16[96,768]{1,0:T(8,128)(2,1)} %refs_3_.1), custom_call_target="tpu_custom_call" | custom-call | tf_op jit(solution)/shard_map/gather/pallas_call | solution.py:492
  91.3 0.9 slice.135
  92.2 1.7 copy.155.ids_col_ref
  93.9 1.6 copy.153
  95.5 1.3 copy.154.wt_ref
  96.8 2.3 multiply_sine_fusion
  99.2 37.2 %attn_forward.1 = (bf16[1536,192]{1,0:T(8,128)(2,1)}, f32[192,1536]{1,0:T(8,128)}, f32[3,1536]{1,0:T(4,128)}, bf16[192,1536]{1,0:T(8,128)(2,1)}, bf16[3,3072,64]...) custom-call(bf16[3072,768]{1,0:T(8,128)(2,1)} %bitcast.198, ...), custom_call_target="tpu_custom_call" | custom-call | flops 42550001664 | tf_op jit(solution)/shard_map/attn_forward/pallas_call | solution.py:281
  136.4 16.3 %granules.2 = bf16[12,128,192]{2,1,0:T(8,128)(2,1)} custom-call(bf16[12,128,192]{2,1,0:T(8,128)(2,1)} %bitcast.182), custom_call_target="tpu_custom_call" | custom-call | tf_op jit(solution)/shard_map/granules/pallas_call | solution.py:591
  152.7 1.5 copy.156
  154.2 2.3 multiply_reduce_fusion.2
  156.5 1.3 fusion.24
  160.0 1.9 convolution_convert_fusion.2
  162.0 27.1 %swap.6 = (f32[4,8,128]{2,1,0:T(8,128)}, bf16[4,2,96,768]{3,2,1,0:T(8,128)(2,1)}) custom-call(f32[4,8,128]{2,1,0:T(8,128)} %pad.15.refs_0_, bf16[4,2,96,768]{3,2,1,0:T(8,128)(2,1)} %bitcast.178), custom_call_target="tpu_custom_call" | custom-call | tf_op jit(solution)/shard_map/swap/pallas_call | solution.py:407
  189.8 1.0 reshape.264.prob_ref
  190.8 37.3 %experts.1 = (bf16[4,2,96,768]{3,2,1,0:T(8,128)(2,1)}, bf16[4,2,96,768]{3,2,1,0:T(8,128)(2,1)}, f32[2,384,1]{2,1,0:T(8,128)}, bf16[2,768,2048]{2,1,0:T(8,128)(2,...) custom-call(bf16[4,2,96,768]{3,2,1,0:T(8,128)(2,1)} %get-tuple-element.50.rows_ref, ...), custom_call_target="tpu_custom_call" | custom-call | flops 42550001664 | tf_op jit(solution)/shard_map/experts/pallas_call | solution.py:330
  229.3 0.9 fusion.17
  231.7 31.7 %swap.7 = (f32[4,8,128]{2,1,0:T(8,128)}, bf16[4,2,96,768]{3,2,1,0:T(8,128)(2,1)}) custom-call(f32[4,8,128]{2,1,0:T(8,128)} %pad.16.refs_0_, bf16[4,2,96,768]{3,2,1,0:T(8,128)(2,1)} %get-tuple-element.54.refs_1_), custom_call_target="tpu_custom_call" | custom-call | tf_op jit(solution)/shard_map/swap/pallas_call | solution.py:407
  267.3 2.0 fusion.48
  269.3 3.3 multiply_reduce_fusion
  272.5 1.7 concatenate.42
  274.3 0.9 convolution_bitcast_fusion.1
  275.4 0.7 copy.177
  276.8 1.8 convert_add_fusion
  280.0 1.2 copy.170
  281.2 19.5 %granules.3 = bf16[12,128,192]{2,1,0:T(8,128)(2,1)} custom-call(bf16[12,128,192]{2,1,0:T(8,128)(2,1)} %bitcast.165), custom_call_target="tpu_custom_call" | custom-call | tf_op jit(solution)/shard_map/granules/pallas_call | solution.py:591
  300.7 57.8 %attn_backward.1 = (bf16[3072,768]{1,0:T(8,128)(2,1)}, f32[576,768]{1,0:T(8,128)}) custom-call(bf16[1536,192]{1,0:T(8,128)(2,1)} %bitcast.181, bf16[3072,768]{1,0:T(8,128)(2,1)} %bitcast.199, bf16[576,768]{1,0:T(8,128)(2,1)} %copy.154.wt_ref, f32[32,3072]{1,0:T(8,128)} %get-tuple-element.186.cos_ref, f32[32,3072]{1,0:T(8,128)} %get-tuple-element.185.sin_ref, ...), custom_call_target="tpu_custom_call" | custom-call | flops 66700001280 | tf_op jit(solution)/shard_map/attn_backward/pallas_call | solution.py:304
  358.5 3.0 copy.174
  362.2 2.2 fusion.22
  364.8 1.2 copy-done.8
  366.2 2.1 copy.181
  368.4 5.0 copy.216
  373.4 1.8 convolution_convert_fusion
  375.2 5.3 all-to-all-start.2
  380.5 13.6 %swap.8 = (bf16[2,4,384,768]{3,2,1,0:T(8,128)(2,1)}, f32[2,4,600,96]{3,2,1,0:T(8,128)}) custom-call(bf16[2,4,384,768]{3,2,1,0:T(8,128)(2,1)} %bitcast.155, f32[2,4,600,96]{3,2,1,0:T(8,128)} %bitcast.156), custom_call_target="tpu_custom_call" | custom-call | tf_op jit(solution)/shard_map/swap/pallas_call | solution.py:407
  394.1 3.2 add_bitcast_fusion.refs_1_
  397.3 4.4 fusion.refs_0_
  401.7 60.4 %swap.9 = (bf16[4,384,768]{2,1,0:T(8,128)(2,1)}, f32[4,600,96]{2,1,0:T(8,128)}) custom-call(bf16[4,384,768]{2,1,0:T(8,128)(2,1)} %fusion.refs_0_, f32[4,600,96]{2,1,0:T(8,128)} %add_bitcast_fusion.refs_1_), custom_call_target="tpu_custom_call" | custom-call | tf_op jit(solution)/shard_map/swap/pallas_call | solution.py:407
  462.2 1.4 slice_reduce_fusion.4.refs_1_
  463.6 0.8 convolution_bitcast_fusion
  464.4 2.2 slice.246
  466.5 2.1 copy.182
  468.7 2.4 concatenate.39
  471.0 1.4 copy.184
  472.4 2.2 convert_reduce_fusion
  474.9 1.4 fusion.14
  476.3 4.9 all-to-all-start.1
  481.4 0.8 copy-done.11
  482.2 0.9 maximum_bitcast_fusion.refs_0_
  483.1 41.5 %swap.10 = (bf16[4,4,24,768]{3,2,1,0:T(8,128)(2,1)}, f32[4,24,96]{2,1,0:T(8,128)}) custom-call(bf16[4,4,24,768]{3,2,1,0:T(8,128)(2,1)} %maximum_bitcast_fusion.refs_0_, f32[24,96]{1,0:T(8,128)} %slice_reduce_fusion.4.refs_1_), custom_call_target="tpu_custom_call" | custom-call | tf_op jit(solution)/shard_map/swap/pallas_call | solution.py:407
  524.5 1.9 reduce_sum.260.refs_0_
  526.4 14.5 %swap.11 = bf16[4,4,24,768]{3,2,1,0:T(8,128)(2,1)} custom-call(bf16[4,24,768]{2,1,0:T(8,128)(2,1)} %reduce_sum.260.refs_0_), custom_call_target="tpu_custom_call" | custom-call | tf_op jit(solution)/shard_map/swap/pallas_call | solution.py:407
  542.8 1.2 convert_bitcast_fusion
  544.0 0.8 fusion.72
  545.3 1.3 dynamic-slice_divide_fusion
  547.8 2.5 fusion.6
  550.4 2.8 fusion.8
  553.2 2.5 convert_element_type.144
  555.6 2.5 convert_element_type.145
  558.1 2.4 convert_element_type.146
  (252 shorter events, 21.5 us)
Async XLA Ops:
  7.2 150.6 %copy-start = (f32[12,12]{1,0:T(8,128)S(1)}, f32[12,12]{1,0:T(8,128)}, u32[]{:S(2)}) copy-start(f32[12,12]{1,0:T(8,128)} %param.30) | copy-start | bytes 1732
  7.2 2.2 copy-start.67
  7.2 183.6 %all-gather.4.cloned.1.call-start = ((), (), s32[]{:S(2)}) async-start(), calls=%async_computation.6 | async-start | bytes 7077888 | tf_op jit(solution)/shard_map/all_gather | solution.py:696
  7.9 182.9 %all-gather.6.cloned.1.call-start = ((), (), s32[]{:S(2)}) async-start(), calls=%async_computation.7 | async-start | bytes 7077888 | tf_op jit(solution)/shard_map/all_gather | solution.py:697
  8.7 182.1 %all-gather.8.cloned.1.call-start = ((), (), s32[]{:S(2)}) async-start(), calls=%async_computation.8 | async-start | bytes 7077888 | tf_op jit(solution)/shard_map/all_gather | solution.py:698
  9.4 3.2 copy-start.5
  12.6 147.4 %copy-start.44 = (s32[384]{0:T(512)}, s32[384]{0:T(512)S(1)}, u32[]{:S(2)}) copy-start(s32[384]{0:T(512)S(1)} %get-tuple-element.160) | copy-start | bytes 4612
  12.6 147.4 %copy-start.47 = (s32[384]{0:T(512)}, s32[384]{0:T(512)S(1)}, u32[]{:S(2)}) copy-start(s32[384]{0:T(512)S(1)} %get-tuple-element.159) | copy-start | bytes 4612
  14.5 6.5 %copy-start.23 = (bf16[96,768]{1,0:T(8,128)(2,1)S(1)}, bf16[96,768]{1,0:T(8,128)(2,1)}, u32[]{:S(2)}) copy-start(bf16[96,768]{1,0:T(8,128)(2,1)} %param.24) | copy-start | bytes 442372
  14.5 6.7 %copy-start.21 = (bf16[96,768]{1,0:T(8,128)(2,1)S(1)}, bf16[96,768]{1,0:T(8,128)(2,1)}, u32[]{:S(2)}) copy-start(bf16[96,768]{1,0:T(8,128)(2,1)} %param.25) | copy-start | bytes 442372
  14.5 6.9 %copy-start.19 = (bf16[96,768]{1,0:T(8,128)(2,1)S(1)}, bf16[96,768]{1,0:T(8,128)(2,1)}, u32[]{:S(2)}) copy-start(bf16[96,768]{1,0:T(8,128)(2,1)} %param.26) | copy-start | bytes 442372
  14.5 7.0 %copy-start.71 = (s32[1,384]{1,0:T(1,128)S(1)}, s32[1,384]{1,0:T(1,128)}, u32[]{:S(2)}) copy-start(s32[1,384]{1,0:T(1,128)} %param.21) | copy-start | bytes 4612
  14.5 176.3 %all-to-all-start = ((bf16[4,2,96,768]{3,2,1,0:T(8,128)(2,1)}), bf16[4,2,96,768]{3,2,1,0:T(8,128)(2,1)}, u32[]{:S(2)}, u32[]{:S(2)}) async-start(bf16[4,2,96,768]{3,2,1,0:T(8,128)(2,1)} %bitcast.24), calls=%async_computation | async-start | bytes 2359296 | tf_op jit(solution)/shard_map/all_to_all | solution.py:608
  21.0 532.2 %reduce-scatter.4.cloned.1.call-start = ((), (), s32[]{:S(2)}) async-start(), calls=%async_computation.9 | async-start | bytes 7077888 | tf_op jit(solution)/shard_map/reduce_scatter | solution.py:744
  21.2 1.5 copy-start.39
  22.7 68.6 %copy-start.41 = (f32[384]{0:T(512)}, f32[384]{0:T(512)S(1)}, u32[]{:S(2)}) copy-start(f32[384]{0:T(512)S(1)} %add_rsqrt_fusion.1) | copy-start | bytes 4612
  92.2 3.3 copy-start.37
  154.1 2.3 copy-start.9
  154.1 2.3 copy-start.54
  154.2 2.4 copy-start.26
  154.2 2.4 copy-start.32
  156.5 120.4 %copy-start.1 = (f32[384,768]{1,0:T(8,128)}, f32[384,768]{1,0:T(8,128)S(1)}, u32[]{:S(2)}) copy-start(f32[384,768]{1,0:T(8,128)S(1)} %get-tuple-element.190) | copy-start | bytes 3538948
  156.5 5.5 copy-start.31
  158.4 3.5 copy-start.65
  228.2 327.4 %reduce-scatter.6.cloned.1.call-start = ((), (), s32[]{:S(2)}) async-start(), calls=%async_computation.10 | async-start | bytes 7077888 | tf_op jit(solution)/shard_map/reduce_scatter | solution.py:745
  228.8 329.3 %reduce-scatter.8.cloned.1.call-start = ((), (), s32[]{:S(2)}) async-start(), calls=%async_computation.11 | async-start | bytes 7077888 | tf_op jit(solution)/shard_map/reduce_scatter | solution.py:746
  229.1 36.7 %copy-start.35 = (f32[384,2,2]{0,1,2:T(2,128)}, f32[384,2,2]{0,1,2:T(2,128)S(1)}, u32[]{:S(2)}) copy-start(f32[384,2,2]{0,1,2:T(2,128)S(1)} %broadcast_divide_fusion) | copy-start | bytes 18436
  230.4 33.8 %copy-start.45 = (s32[384]{0:T(512)S(1)}, s32[384]{0:T(512)}, u32[]{:S(2)}) copy-start(s32[384]{0:T(512)} %copy-done.44) | copy-start | bytes 4612
  230.4 33.8 %copy-start.48 = (s32[384]{0:T(512)S(1)}, s32[384]{0:T(512)}, u32[]{:S(2)}) copy-start(s32[384]{0:T(512)} %copy-done.47) | copy-start | bytes 4612
  266.0 3.2 copy-start.72
  276.8 1.8 copy-start.16
  358.5 3.0 copy-start.29
  358.5 3.0 copy-start.36
  358.5 3.6 copy-start.2
  358.5 3.6 copy-start.17
  358.5 3.6 copy-start.34
  361.5 2.8 copy-start.27
  362.2 2.3 copy-start.12
  364.4 1.6 copy-start.8
  368.4 5.0 copy-start.4
  368.4 5.0 copy-start.10
  375.2 101.1 %all-to-all-start.2 = ((bf16[8,96,768]{2,1,0:T(8,128)(2,1)}), bf16[8,96,768]{2,1,0:T(8,128)(2,1)S(1)}, u32[]{:S(2)}, u32[]{:S(2)}) async-start(bf16[8,96,768]{2,1,0:T(8,128)(2,1)} %bitcast.162), calls=%async_computation.2 | async-start | bytes 2359296 | tf_op jit(solution)/shard_map/all_to_all | solution.py:608
  401.7 61.9 %copy-start.18 = (f32[384,12]{0,1:T(8,128)S(1)}, f32[384,12]{0,1:T(8,128)}, u32[]{:S(2)}) copy-start(f32[384,12]{0,1:T(8,128)} %get-tuple-element.181) | copy-start | bytes 55300
  472.4 2.2 copy-start.7
  472.4 2.2 copy-start.40
  472.4 2.2 copy-start.42
  476.3 71.4 %all-to-all-start.1 = ((bf16[4,2,96,768]{3,2,1,0:T(8,128)(2,1)}), bf16[4,2,96,768]{3,2,1,0:T(8,128)(2,1)}, u32[]{:S(2)}, u32[]{:S(2)}) async-start(bf16[4,2,96,768]{3,2,1,0:T(8,128)(2,1)} %get-tuple-element.52), calls=%async_computation.1 | async-start | bytes 2359296 | tf_op jit(solution)/shard_map/all_to_all | solution.py:608
  524.5 16.4 %copy-start.38 = (f32[4,24,96]{2,1,0:T(8,128)S(1)}, f32[4,24,96]{2,1,0:T(8,128)}, u32[]{:S(2)}) copy-start(f32[4,24,96]{2,1,0:T(8,128)} %get-tuple-element.70) | copy-start | bytes 110596
  544.8 5.5 copy-start.13
  544.8 5.5 copy-start.14
  544.8 5.5 copy-start.15
  544.8 2.9 copy-start.49
  544.8 2.9 copy-start.51
  544.8 2.9 copy-start.53
  544.8 2.9 copy-start.56
  544.8 2.9 copy-start.58
  544.9 2.9 copy-start.60
  544.9 2.9 copy-start.62
  544.9 2.9 copy-start.66
  544.9 2.9 copy-start.68
  544.9 2.9 copy-start.69
  544.9 2.9 copy-start.70
  547.8 2.6 copy-start.46
  547.8 2.6 copy-start.64
  (18 other events, 19.5 us)
Sparse Core Ops, SparseCore 0:
  9.9 78.9 all-gather.3
  90.8 45.3 all-gather.5
  138.2 47.3 all-gather.7
  228.3 74.7 reduce-scatter.3
  306.3 60.7 reduce-scatter.5
  370.3 92.0 reduce-scatter.7

commit v2 on v1

--- a/solution.py
+++ b/solution.py
@@ -140,8 +140,8 @@
     heads, size, ranks, scale,
     grad_ref, a_ref, wt_ref, cos_ref, sin_ref, ids_col_ref, ids_row_ref,
     out_t_ref, lse_ref, query_t_ref, key_ref, key_t_ref, value_ref,
-    da_ref, grad_w_ref,
-    query_ref, own_grad_ref, dq_ref, dk_ref, dv_ref,
+    da_ref, pieces_ref,
+    query_ref, own_grad_ref, dq_ref, dk_ref, dv_ref, grad_w_ref,
 ):
     length = a_ref.shape[0]
     width = heads * size
@@ -213,6 +213,9 @@
         return carry
 
     lax.fori_loop(0, tiles, finish, 0)
+    shard = pieces_ref.shape[2]
+    for piece in range(pieces_ref.shape[0]):
+        pieces_ref[piece] = grad_w_ref[:, piece * shard : (piece + 1) * shard]
 
 
 def expert_kernel(
@@ -294,12 +297,14 @@
     )(a_full, weights_t, cos_t, sin_t, ids[:, None], ids[None, :])
 
 
-def attn_backward(grad_full, a_full, weights_t, cos_t, sin_t, ids, kept, heads, size, ranks):
+def attn_backward(
+    grad_full, a_full, weights_t, cos_t, sin_t, ids, kept, heads, size, ranks, context
+):
     length = a_full.shape[0]
     width = heads * size
     shapes = (
         jax.ShapeDtypeStruct(a_full.shape, BF16),
-        jax.ShapeDtypeStruct(weights_t.shape, F32),
+        jax.ShapeDtypeStruct((context, weights_t.shape[0], a_full.shape[1] // context), F32),
     )
     return pl.pallas_call(
         functools.partial(attn_backward_kernel, heads, size, ranks, size ** (-0.5)),
@@ -312,6 +317,7 @@
             pltpu.VMEM((width, TILE), F32),
             pltpu.VMEM((heads, length, size), F32),
             pltpu.VMEM((heads, length, size), F32),
+            pltpu.VMEM(weights_t.shape, F32),
         ],
         compiler_params=pltpu.CompilerParams(vmem_limit_bytes=63 << 20),
         cost_estimate=cost(58),
@@ -602,6 +608,195 @@
         ),
         name="granules",
     )(rows)
+
+
+def finish_kernel(
+    chips, owners, groups,
+    da_ref, pieces_ref, small_ref, output_ref,
+    total_ref, sums_ref, small_all_ref,
+    da_twin, da_sum, da_in, w_twin, w_sum, w_in, s_twin, s_sum, s_in, s_total,
+    stack_ref, shares, shares_in, block_ref,
+    pair_send, pair_recv, chip_send, chip_recv, row_send, row_recv,
+):
+    place = lax.axis_index("context")
+    row = lax.axis_index("expert")
+    chip, core = place // 2, lax.rem(place, 2)
+    partner = 2 * chip + 1 - core
+    barrier = pltpu.get_barrier_semaphore()
+
+    def greet(device):
+        pl.semaphore_signal(
+            barrier, inc=1, device_id=device, device_id_type=pl.DeviceIdType.MESH
+        )
+
+    def remote(source, target, send, recv, device):
+        return pltpu.make_async_remote_copy(
+            src_ref=source, dst_ref=target, send_sem=send, recv_sem=recv,
+            device_id=device, device_id_type=pl.DeviceIdType.MESH,
+        )
+
+    greet({"context": partner})
+    for far in range(1, chips):
+        greet({"context": 2 * lax.rem(chip + far, chips) + core})
+    for far in range(1, owners):
+        greet({"expert": lax.rem(row + far, owners)})
+    pl.semaphore_wait(barrier, chips + owners - 1)
+
+    order = list(range(1, chips)) + [0]
+    pair = {}
+    for item, (source, target) in enumerate(
+        ((small_ref, s_twin), (pieces_ref, w_twin), (da_ref, da_twin))
+    ):
+        for far in order:
+            peer = lax.rem(chip + far, chips)
+            pair[item, far] = remote(
+                source.at[2 * peer + 1 - core], target.at[peer],
+                pair_send.at[item, far], pair_recv.at[item, far], {"context": partner},
+            )
+            pair[item, far].start()
+
+    def across(item, source, target, far):
+        peer = lax.rem(chip + far, chips)
+        return remote(
+            source.at[peer], target.at[chip], chip_send.at[item, far], chip_recv.at[item, far],
+            {"context": 2 * peer + core},
+        )
+
+    for far in order:
+        peer = lax.rem(chip + far, chips)
+        mine = 2 * peer + core
+        pair[0, far].wait_recv()
+        s_sum[peer] = small_ref[mine] + s_twin[peer]
+        pair[1, far].wait_recv()
+        w_sum[peer] = (pieces_ref[mine] + w_twin[peer]).astype(BF16)
+    moved = {}
+    for far in range(1, chips):
+        moved[0, far] = across(0, s_sum, s_in, far)
+        moved[0, far].start()
+        moved[1, far] = across(1, w_sum, w_in, far)
+        moved[1, far].start()
+    last = None
+    for far in order:
+        peer = lax.rem(chip + far, chips)
+        pair[2, far].wait_recv()
+        da_sum[peer] = (
+            da_ref[2 * peer + core].astype(F32) + da_twin[peer].astype(F32)
+        ).astype(BF16)
+        if last is not None:
+            moved[2, last] = across(2, da_sum, da_in, last)
+            moved[2, last].start()
+        last = far
+    for far in range(1, chips):
+        moved[0, far].wait_recv()
+        moved[1, far].wait_recv()
+    s_in[chip] = s_sum[chip]
+    w_in[chip] = w_sum[chip]
+
+    width = w_sum.shape[1] // 3
+    shard = w_sum.shape[2]
+    per_group = chips // groups
+    for group in range(groups):
+        total = w_in[group * per_group].astype(F32)
+        for other in range(1, per_group):
+            total = total + w_in[group * per_group + other].astype(F32)
+        for which in range(3):
+            stack_ref[which * shard : (which + 1) * shard, group * width : (group + 1) * width] = (
+                total[which * width : (which + 1) * width].T
+            )
+    stack_ref[3 * shard :, :] = output_ref[...]
+    lines = shares.shape[1]
+    for owner in range(owners):
+        shares[owner] = stack_ref[owner * lines : (owner + 1) * lines, :].astype(BF16)
+    total = s_in[0]
+    for other in range(1, chips):
+        total = total + s_in[other]
+    s_total[...] = total
+    rows = {}
+    for far in range(1, owners):
+        peer = lax.rem(row + far, owners)
+        rows[0, far] = remote(
+            shares.at[peer], shares_in.at[row], row_send.at[0, far], row_recv.at[0, far],
+            {"expert": peer},
+        )
+        rows[0, far].start()
+        rows[1, far] = remote(
+            s_total, small_all_ref.at[row], row_send.at[1, far], row_recv.at[1, far],
+            {"expert": peer},
+        )
+        rows[1, far].start()
+    shares_in[row] = shares[row]
+    small_all_ref[row] = total
+    for far in range(1, owners):
+        rows[0, far].wait_recv()
+    summed = shares_in[0].astype(F32)
+    for other in range(1, owners):
+        summed = summed + shares_in[other].astype(F32)
+    block_ref[...] = summed.astype(BF16)
+    for far in range(1, chips):
+        moved[2, far].wait_recv()
+    for far in range(1, owners):
+        peer = lax.rem(row + far, owners)
+        rows[2, far] = remote(
+            block_ref, sums_ref.at[row], row_send.at[2, far], row_recv.at[2, far],
+            {"expert": peer},
+        )
+        rows[2, far].start()
+    sums_ref[row] = summed.astype(BF16)
+    da_in[chip] = da_sum[chip]
+    total = da_in[0].astype(F32)
+    for other in range(1, chips):
+        total = total + da_in[other].astype(F32)
+    total_ref[...] = total
+    for far in range(1, owners):
+        rows[1, far].wait_recv()
+        rows[2, far].wait_recv()
+    for copy in list(pair.values()) + list(moved.values()) + list(rows.values()):
+        copy.wait_send()
+
+
+def finish(da, pieces, small, output_share, owners, groups, number):
+    context, tokens, width = da.shape
+    chips = context // 2
+    lines, shard = pieces.shape[1:]
+    few = small.shape[1]
+    stack = 3 * shard + output_share.shape[0]
+    block = (stack // owners, width)
+    return pl.pallas_call(
+        functools.partial(finish_kernel, chips, owners, groups),
+        out_shape=(
+            jax.ShapeDtypeStruct((tokens, width), F32),
+            jax.ShapeDtypeStruct((owners,) + block, BF16),
+            jax.ShapeDtypeStruct((owners, few, shard), F32),
+        ),
+        in_specs=vmem(4),
+        out_specs=vmem(3),
+        scratch_shapes=[
+            pltpu.VMEM((chips, tokens, width), BF16),
+            pltpu.VMEM((chips, tokens, width), BF16),
+            pltpu.VMEM((chips, tokens, width), BF16),
+            pltpu.VMEM((chips, lines, shard), F32),
+            pltpu.VMEM((chips, lines, shard), BF16),
+            pltpu.VMEM((chips, lines, shard), BF16),
+            pltpu.VMEM((chips, few, shard), F32),
+            pltpu.VMEM((chips, few, shard), F32),
+            pltpu.VMEM((chips, few, shard), F32),
+            pltpu.VMEM((few, shard), F32),
+            pltpu.VMEM((stack, width), F32),
+            pltpu.VMEM((owners,) + block, BF16),
+            pltpu.VMEM((owners,) + block, BF16),
+            pltpu.VMEM(block, BF16),
+            pltpu.SemaphoreType.DMA((3, chips)),
+            pltpu.SemaphoreType.DMA((3, chips)),
+            pltpu.SemaphoreType.DMA((3, chips)),
+            pltpu.SemaphoreType.DMA((3, chips)),
+            pltpu.SemaphoreType.DMA((3, owners)),
+            pltpu.SemaphoreType.DMA((3, owners)),
+        ],
+        compiler_params=pltpu.CompilerParams(
+            collective_id=number, has_side_effects=True, vmem_limit_bytes=60 << 20
+        ),
+        name="finish",
+    )(da, pieces, small, output_share)
 
 
 def exchange(value, axis_name, axis):
@@ -687,7 +882,8 @@
     def pick(rows):
         return jnp.dot(pick_either, rows, preferred_element_type=F32).astype(BF16).reshape(blocks)
 
-    grad_arrived = exchange(pick(cotangent_low), "expert", 0)
+    cotangent_late, a_full = lax.optimization_barrier((cotangent_low, a_full))
+    grad_arrived = exchange(pick(cotangent_late), "expert", 0)
 
     (
         attn_out, out_t, log_total, query_t, key_heads, key_t, value_heads,
@@ -749,6 +945,7 @@
     slot_dot, grad_back = swap((spread(owner_dot), grad_rows), "expert", 1, owners, 3)
     slot_dot = slot_dot[:, :per_owner, :CAP].reshape(slot_count)
     grad_back = grad_back.reshape(slot_count, model_width)
+    expert_out, grad_back = lax.optimization_barrier((expert_out, grad_back))
     returned = exchange(expert_out, "expert", 0).reshape(slot_count, model_width)
 
     const_soft = jax.nn.softmax(narrow_out[:, expert_count:].reshape(token_rows, consts, 2), axis=2)
@@ -821,6 +1018,7 @@
         axis=0,
     )
     small = jnp.pad(small, ((0, -small.shape[0] % 8), (0, 0), (0, 0)))
+    small = jnp.transpose(small, (1, 0, 2))
 
     grad_normed_two = grad_moe_input * moe_gain
     grad_after = cotangent + inv_rms2 * (
@@ -841,43 +1039,20 @@
         grad_output_local.reshape(context, shard_width, model_width), "context", 0
     )
 
-    da_part, grad_w = attn_backward(
-        grad_own, a_full, weights_t, cos_t, sin_t, ids, kept, heads, head_size, ranks
-    )
-    chips = context // 2
-    core = lax.rem(lax.axis_index("context"), 2)
-    both_parts = jnp.concatenate(
-        [grad_w.reshape(3 * width, context, shard_width), small], axis=0
-    )
-    both_lines = both_parts.shape[0]
-    both_parts = jnp.transpose(both_parts, (1, 0, 2)).reshape(chips, 2, both_lines, shard_width)
-    da_part = da_part.reshape(chips, 2, token_rows, model_width)
-    da_twin, both_twin = swap(
-        (jnp.swapaxes(da_part, 0, 1), jnp.swapaxes(both_parts, 0, 1)), "context", 1, 2, 5
-    )
-    da_chip = (da_twin[0].astype(F32) + da_twin[1].astype(F32)).astype(BF16)
-    both_chip = both_twin[0] + both_twin[1]
-    da_all, both_all = swap((da_chip, both_chip), "context", 2, chips, 6)
-    grad_attn_input = jnp.sum(da_all.astype(F32), axis=0)
+    output_share = jnp.sum(output_parts.astype(F32), axis=0)
+    da_part, w_pieces = attn_backward(
+        grad_own, a_full, weights_t, cos_t, sin_t, ids, kept, heads, head_size, ranks, context
+    )
+    da_part, returned = lax.optimization_barrier((da_part, returned))
+    grad_attn_input, sums, small_all = finish(
+        da_part.reshape(context, token_rows, model_width), w_pieces, small, output_share,
+        owners, groups, 5,
+    )
     grad_normed_one = grad_attn_input * attn_gain
     grad_input = grad_after + inv_rms1 * (
         grad_normed_one - normed_one * jnp.mean(grad_normed_one * normed_one, axis=1, keepdims=True)
     )
-
-    per_group = ranks // 2
-    w_blocks = both_all[:, : 3 * width].reshape(groups, per_group, 3, width, shard_width)
-    w_blocks = jnp.sum(w_blocks, axis=1)
-    w_share = jnp.transpose(w_blocks, (1, 3, 0, 2)).reshape(3, shard_width, model_width)
-    output_share = jnp.sum(output_parts.astype(F32), axis=0)
-    shares = jnp.concatenate([w_share, output_share[None]], axis=0).reshape(
-        4, owners, shard_width // owners, model_width
-    )
-    shares = jnp.transpose(shares.astype(BF16), (1, 0, 2, 3))
-    small_ctx = jnp.sum(both_all[:, 3 * width :], axis=0)
-    shares_all, small_all = swap((shares, small_ctx), "expert", 1, owners, 7, (False, True))
-    share_sum = jnp.sum(shares_all.astype(F32), axis=0).astype(BF16)
-    (sums,) = swap((share_sum,), "expert", 1, owners, 8, (True,))
-    sums = jnp.transpose(sums.astype(F32), (1, 0, 2, 3)).reshape(4, shard_width, model_width)
+    sums = sums.astype(F32).reshape(4, shard_width, model_width)
     w_sum, output_sum = sums[:3], sums[3]
     small_own = jnp.sum(small_all, axis=0)
     grad_attn_gain = jnp.sum(

time: 569 us -> 490 us (0.86)
  Pallas kernels: 424 us -> 380 us
  local copies, waits for them, and re-layouts: 43.9 us -> 21.5 us
  other arithmetic: 38.7 us -> 23.8 us
    pallas_call x6 -> x2, Pallas kernels: 189 us -> 57.9 us  [swap(): pl.pallas_call(functools.partial(swap_kernel, axis, stride, count, same),...]
    pallas_call x0 -> x1, Pallas kernels: none -> 76.7 us  [finish(): pl.pallas_call(functools.partial(finish_kernel, chips, owners, groups), o...]
    pallas_call x2, Pallas kernels: 35.8 us -> 45.9 us  [granules(): pl.pallas_call(functools.partial(granule_kernel, ranks, shard_granules, o...]
    reshape x2 -> x0, local copies, waits for them, and re-layouts: 7.13 us -> none  [the longest x1 5.01 us: shards(): da_part = da_part.reshape(chips, 2, token_rows, model_width)]
  transfers between devices with their start and end apart: 9 -> 9, of which waited for: 0 -> 0; matrix products, arithmetic and copies ran while one was open for 18% -> 14% of each run, Pallas kernels for 68% -> 70%
where the time goes in v2:
time: 490 us; the launch traced here: 489 us
  Pallas kernels  380 us (78%)
  matrix products  26 us (5%)
  other arithmetic  23.8 us (5%)
  local copies, waits for them, and re-layouts  21.5 us (4%)
  starting transfers between devices  19.3 us (4%)
  between operations  15.3 us (3%)
    pallas_call x1, Pallas kernels, finish(): pl.pallas_call(functools.partial(finish_kernel, chips, owners, groups), o...  76.7 us
    pallas_call x1, Pallas kernels, gather(): pl.pallas_call(functools.partial(gather_kernel, chips, ranks, split), out...  64.6 us
    pallas_call x1, Pallas kernels, attn_backward(): pl.pallas_call(functools.partial(attn_backward_kernel, heads, size, ranks...  60.4 us
    pallas_call x2, Pallas kernels, swap(): pl.pallas_call(functools.partial(swap_kernel, axis, stride, count, same),...  57.9 us
    pallas_call x2, Pallas kernels, granules(): pl.pallas_call(functools.partial(granule_kernel, ranks, shard_granules, o...  45.9 us
    pallas_call x1, Pallas kernels, attn_forward(): pl.pallas_call(functools.partial(attn_forward_kernel, heads, size, ranks,...  37.4 us
    pallas_call x1, Pallas kernels, experts(): pl.pallas_call(expert_kernel, grid=(count, hidden // HIDDEN_TILE), out_sh...  37.2 us
    all_to_all x3, starting transfers between devices, exchange(): lax.all_to_all(value, axis_name, split_axis=axis, concat_axis=axis, tiled...  18.9 us
  transfers between devices with their start and end apart: 9, of which 0 were waited for; matrix products, arithmetic and copies ran while one was open for 14% of the time, Pallas kernels for 70%

profile of v2, /device:TPU:0, one launch (start us, length us, event | category | flops | bytes accessed | tf_op | source)
XLA Modules:
  0.0 488.6 jit_solution(3546008150456116824)
XLA Ops:
  7.3 0.7 all-gather.4.cloned.1.call-update
  8.0 0.7 all-gather.6.cloned.1.call-update
  8.8 0.7 all-gather.8.cloned.1.call-update
  10.5 0.9 pad_maximum_fusion
  11.7 1.0 fusion.8.refs_2_
  12.7 0.6 broadcast_in_dim.102.refs_0_
  13.3 64.6 %gather.1 = (f32[8,8,384]{2,1,0:T(8,128)}, bf16[8,576,96]{2,1,0:T(8,128)(2,1)}, bf16[8,384,768]{2,1,0:T(8,128)(2,1)}, bf16[8,96,768]{2,1,0:T(8,128)(2,1)}) custom-call(f32[8,384]{1,0:T(8,128)} %broadcast_in_dim.102.refs_0_, bf16[4,576,96]{2,1,0:T(8,128)(2,1)} %bitcast.149, bf16[384,768]{1,0:T(8,128)(2,1)} %fusion.8.refs_2_, bf16[96,768]{1,0:T(8,128)(2,1)} %refs_3_.1), custom_call_target="tpu_custom_call" | custom-call | tf_op jit(solution)/shard_map/gather/pallas_call | solution.py:498
  77.9 1.7 reduce-window.6
  80.7 1.8 convolution_convert_fusion.1
  82.5 5.1 %all-to-all-start = ((bf16[4,2,96,768]{3,2,1,0:T(8,128)(2,1)}), bf16[4,2,96,768]{3,2,1,0:T(8,128)(2,1)}, u32[]{:S(2)}, u32[]{:S(2)}) async-start(bf16[4,2,96,768]{3,2,1,0:T(8,128)(2,1)} %bitcast.24), calls=%async_computation | async-start | bytes 2359296 | tf_op jit(solution)/shard_map/all_to_all | solution.py:803
  87.7 1.0 slice.111
  88.7 1.7 copy.107.ids_col_ref
  90.4 0.7 copy.105
  91.0 1.3 copy.106.wt_ref
  92.3 2.3 multiply_sine_fusion
  94.6 37.4 %attn_forward.1 = (bf16[1536,192]{1,0:T(8,128)(2,1)}, f32[192,1536]{1,0:T(8,128)}, f32[3,1536]{1,0:T(4,128)}, bf16[192,1536]{1,0:T(8,128)(2,1)}, bf16[3,3072,64]...) custom-call(bf16[3072,768]{1,0:T(8,128)(2,1)} %bitcast.172, ...), custom_call_target="tpu_custom_call" | custom-call | flops 42550001664 | tf_op jit(solution)/shard_map/attn_forward/pallas_call | solution.py:284
  132.0 18.3 %granules.2 = bf16[12,128,192]{2,1,0:T(8,128)(2,1)} custom-call(bf16[12,128,192]{2,1,0:T(8,128)(2,1)} %bitcast.158), custom_call_target="tpu_custom_call" | custom-call | tf_op jit(solution)/shard_map/granules/pallas_call | solution.py:597
  150.3 1.5 copy.108
  151.8 2.3 multiply_reduce_fusion.2
  154.2 1.3 fusion.23
  157.0 0.6 pad.15.refs_0_
  157.6 1.9 convolution_convert_fusion.2
  159.6 26.2 %swap.2 = (f32[4,8,128]{2,1,0:T(8,128)}, bf16[4,2,96,768]{3,2,1,0:T(8,128)(2,1)}) custom-call(f32[4,8,128]{2,1,0:T(8,128)} %pad.15.refs_0_, bf16[4,2,96,768]{3,2,1,0:T(8,128)(2,1)} %bitcast.154), custom_call_target="tpu_custom_call" | custom-call | tf_op jit(solution)/shard_map/swap/pallas_call | solution.py:413
  185.8 0.7 slice_bitcast_fusion.5
  186.5 1.0 reshape.229.prob_ref
  187.6 37.2 %experts.1 = (bf16[4,2,96,768]{3,2,1,0:T(8,128)(2,1)}, bf16[4,2,96,768]{3,2,1,0:T(8,128)(2,1)}, f32[2,384,1]{2,1,0:T(8,128)}, bf16[2,768,2048]{2,1,0:T(8,128)(2,...) custom-call(bf16[4,2,96,768]{3,2,1,0:T(8,128)(2,1)} %get-tuple-element.54.rows_ref, ...), custom_call_target="tpu_custom_call" | custom-call | flops 42550001664 | tf_op jit(solution)/shard_map/experts/pallas_call | solution.py:336
  225.7 0.9 fusion.16
  227.1 0.6 pad.16.refs_0_
  227.7 31.7 %swap.3 = (f32[4,8,128]{2,1,0:T(8,128)}, bf16[4,2,96,768]{3,2,1,0:T(8,128)(2,1)}) custom-call(f32[4,8,128]{2,1,0:T(8,128)} %pad.16.refs_0_, bf16[4,2,96,768]{3,2,1,0:T(8,128)(2,1)} %get-tuple-element.59.refs_1_), custom_call_target="tpu_custom_call" | custom-call | tf_op jit(solution)/shard_map/swap/pallas_call | solution.py:413
  259.4 0.7 slice.130
  260.6 0.7 subtract_multiply_fusion
  261.4 0.6 fusion.20
  262.0 0.6 slice_reduce_fusion.12
  262.7 2.0 fusion.46
  264.7 2.3 multiply_reduce_fusion
  267.4 0.7 copy-done.11
  268.1 1.8 convolution_convert_fusion
  269.9 3.6 all-to-all-start.2
  273.8 1.1 copy.125
  274.8 1.9 convolution_convert_fusion.3
  277.1 1.2 copy.122
  278.3 27.6 %granules.3 = bf16[12,128,192]{2,1,0:T(8,128)(2,1)} custom-call(bf16[12,128,192]{2,1,0:T(8,128)(2,1)} %bitcast.147), custom_call_target="tpu_custom_call" | custom-call | tf_op jit(solution)/shard_map/granules/pallas_call | solution.py:597
  305.9 10.2 %all-to-all-start.1 = ((bf16[4,2,96,768]{3,2,1,0:T(8,128)(2,1)}), bf16[4,2,96,768]{3,2,1,0:T(8,128)(2,1)}, u32[]{:S(2)}, u32[]{:S(2)}) async-start(bf16[4,2,96,768]{3,2,1,0:T(8,128)(2,1)} %get-tuple-element.70), calls=%async_computation.1 | async-start | bytes 2359296 | tf_op jit(solution)/shard_map/all_to_all | solution.py:803
  316.1 60.4 %attn_backward.1 = (bf16[3072,768]{1,0:T(8,128)(2,1)}, f32[8,576,96]{2,1,0:T(8,128)}) custom-call(bf16[1536,192]{1,0:T(8,128)(2,1)} %bitcast.157, bf16[3072,768]{1,0:T(8,128)(2,1)} %bitcast.173, bf16[576,768]{1,0:T(8,128)(2,1)} %copy.106.wt_ref, f32[32,3072]{1,0:T(8,128)} %get-tuple-element.176.cos_ref, f32[32,3072]{1,0:T(8,128)} %get-tuple-element.175.sin_ref, ...), custom_call_target="tpu_custom_call" | custom-call | flops 66700001280 | tf_op jit(solution)/shard_map/attn_backward/pallas_call | solution.py:309
  376.6 2.2 fusion.21
  379.6 0.6 copy.128
  380.2 1.9 fusion.61
  382.1 0.7 fusion.45.small_ref
  382.8 0.9 convert_reduce_fusion.output_ref
  383.7 76.7 %finish.1 = (f32[384,768]{1,0:T(8,128)}, bf16[4,96,768]{2,1,0:T(8,128)(2,1)}, f32[4,24,96]{2,1,0:T(8,128)}) custom-call(bf16[8,384,768]{2,1,0:T(8,128)(2,1)} %bitcast.143, f32[8,576,96]{2,1,0:T(8,128)} %get-tuple-element.73.pieces_ref, f32[8,24,96]{2,1,0:T(8,128)} %fusion.45.small_ref, f32[96,768]{1,0:T(8,128)} %convert_reduce_fusion.output_ref), custom_call_target="tpu_custom_call" | custom-call | tf_op jit(solution)/shard_map/finish/pallas_call | solution.py:764
  460.4 1.3 convert_element_type.119
  461.8 0.6 slice.170
  462.3 0.6 fusion.71
  462.9 0.7 slice.141
  464.1 1.0 add_reduce_fusion.1
  465.1 0.6 dynamic-slice_divide_fusion
  466.2 0.6 slice_bitcast_fusion.4
  466.8 0.7 slice_bitcast_fusion
  467.7 2.5 fusion.4
  470.2 2.9 fusion.7
  473.1 1.4 fusion.13
  474.5 2.5 convert_element_type.123
  477.0 2.5 convert_element_type.124
  479.4 2.4 convert_element_type.125
  (229 shorter events, 8.4 us)
Async XLA Ops:
  7.2 148.3 %copy-start = (f32[12,12]{1,0:T(8,128)S(1)}, f32[12,12]{1,0:T(8,128)}, u32[]{:S(2)}) copy-start(f32[12,12]{1,0:T(8,128)} %param.30) | copy-start | bytes 1732
  7.2 2.3 copy-start.63
  7.2 180.3 %all-gather.4.cloned.1.call-start = ((), (), s32[]{:S(2)}) async-start(), calls=%async_computation.6 | async-start | bytes 7077888 | tf_op jit(solution)/shard_map/all_gather | solution.py:892
  7.9 2.0 copy-start.18
  8.0 2.2 copy-start.16
  8.0 179.6 %all-gather.6.cloned.1.call-start = ((), (), s32[]{:S(2)}) async-start(), calls=%async_computation.7 | async-start | bytes 7077888 | tf_op jit(solution)/shard_map/all_gather | solution.py:893
  8.7 1.6 copy-start.14
  8.7 1.8 copy-start.67
  8.7 178.8 %all-gather.8.cloned.1.call-start = ((), (), s32[]{:S(2)}) async-start(), calls=%async_computation.8 | async-start | bytes 7077888 | tf_op jit(solution)/shard_map/all_gather | solution.py:894
  9.8 1.7 copy-start.6
  11.7 66.2 %copy-start.36 = (f32[384]{0:T(512)}, f32[384]{0:T(512)S(1)}, u32[]{:S(2)}) copy-start(f32[384]{0:T(512)S(1)} %add_rsqrt_fusion.1) | copy-start | bytes 4612
  13.3 67.4 %copy-start.5 = (bf16[1,384,768]{2,1,0:T(8,128)(2,1)S(1)}, bf16[1,384,768]{2,1,0:T(8,128)(2,1)}, u32[]{:S(2)}) copy-start(bf16[1,384,768]{2,1,0:T(8,128)(2,1)} %param.22) | copy-start | bytes 1769476
  80.7 1.9 copy-start.39
  80.7 1.9 copy-start.42
  82.5 105.0 %all-to-all-start = ((bf16[4,2,96,768]{3,2,1,0:T(8,128)(2,1)}), bf16[4,2,96,768]{3,2,1,0:T(8,128)(2,1)}, u32[]{:S(2)}, u32[]{:S(2)}) async-start(bf16[4,2,96,768]{3,2,1,0:T(8,128)(2,1)} %bitcast.24), calls=%async_computation | async-start | bytes 2359296 | tf_op jit(solution)/shard_map/all_to_all | solution.py:803
  87.7 2.7 copy-start.12
  87.7 386.8 %reduce-scatter.4.cloned.1.call-start = ((), (), s32[]{:S(2)}) async-start(), calls=%async_computation.9 | async-start | bytes 7077888 | tf_op jit(solution)/shard_map/reduce_scatter | solution.py:940
  88.7 1.7 copy-start.32
  151.8 2.3 copy-start.10
  151.8 2.3 copy-start.49
  151.8 2.4 copy-start.21
  151.8 2.4 copy-start.27
  154.1 112.9 %copy-start.1 = (f32[384,768]{1,0:T(8,128)}, f32[384,768]{1,0:T(8,128)S(1)}, u32[]{:S(2)}) copy-start(f32[384,768]{1,0:T(8,128)S(1)} %get-tuple-element.180) | copy-start | bytes 3538948
  154.1 2.5 copy-start.40
  154.1 2.5 copy-start.43
  154.2 5.4 %copy-start.26 = (f32[4,768]{1,0:T(4,128)}, f32[4,768]{1,0:T(4,128)S(1)}, u32[]{:S(2)}) copy-start(f32[4,768]{1,0:T(4,128)S(1)} %reshape.210) | copy-start | bytes 36868
  156.1 3.5 copy-start.60
  224.8 252.1 %reduce-scatter.6.cloned.1.call-start = ((), (), s32[]{:S(2)}) async-start(), calls=%async_computation.10 | async-start | bytes 7077888 | tf_op jit(solution)/shard_map/reduce_scatter | solution.py:941
  225.5 35.8 %copy-start.30 = (f32[384,2,2]{0,1,2:T(2,128)}, f32[384,2,2]{0,1,2:T(2,128)S(1)}, u32[]{:S(2)}) copy-start(f32[384,2,2]{0,1,2:T(2,128)S(1)} %broadcast_divide_fusion) | copy-start | bytes 18436
  262.0 2.7 copy-start.68
  262.7 2.0 copy-start.28
  268.1 6.7 %copy-start.3 = (f32[384,768]{1,0:T(8,128)}, f32[384,768]{1,0:T(8,128)S(1)}, u32[]{:S(2)}) copy-start(f32[384,768]{1,0:T(8,128)S(1)} %convert_add_fusion) | copy-start | bytes 3538948
  269.9 36.0 %all-to-all-start.2 = ((bf16[8,96,768]{2,1,0:T(8,128)(2,1)}), bf16[8,96,768]{2,1,0:T(8,128)(2,1)S(1)}, u32[]{:S(2)}, u32[]{:S(2)}) async-start(bf16[8,96,768]{2,1,0:T(8,128)(2,1)} %bitcast.144), calls=%async_computation.2 | async-start | bytes 2359296 | tf_op jit(solution)/shard_map/all_to_all | solution.py:803
  273.5 205.9 %reduce-scatter.8.cloned.1.call-start = ((), (), s32[]{:S(2)}) async-start(), calls=%async_computation.11 | async-start | bytes 7077888 | tf_op jit(solution)/shard_map/reduce_scatter | solution.py:942
  305.9 10.2 %copy-start.7 = (bf16[8,96,768]{2,1,0:T(8,128)(2,1)}, bf16[8,96,768]{2,1,0:T(8,128)(2,1)S(1)}, u32[]{:S(2)}) copy-start(bf16[8,96,768]{2,1,0:T(8,128)(2,1)S(1)} %all-to-all-done.2) | copy-start | bytes 3538948
  305.9 77.7 %all-to-all-start.1 = ((bf16[4,2,96,768]{3,2,1,0:T(8,128)(2,1)}), bf16[4,2,96,768]{3,2,1,0:T(8,128)(2,1)}, u32[]{:S(2)}, u32[]{:S(2)}) async-start(bf16[4,2,96,768]{3,2,1,0:T(8,128)(2,1)} %get-tuple-element.70), calls=%async_computation.1 | async-start | bytes 2359296 | tf_op jit(solution)/shard_map/all_to_all | solution.py:803
  316.1 60.4 %copy-start.13 = (f32[384,12]{0,1:T(8,128)S(1)}, f32[384,12]{0,1:T(8,128)}, u32[]{:S(2)}) copy-start(f32[384,12]{0,1:T(8,128)} %get-tuple-element.171) | copy-start | bytes 55300
  316.1 60.4 %copy-start.29 = (f32[384,4]{0,1:T(4,128)S(1)}, f32[384,4]{0,1:T(4,128)}, u32[]{:S(2)}) copy-start(f32[384,4]{0,1:T(4,128)} %copy-done.28) | copy-start | bytes 18436
  376.5 2.4 copy-start.62
  376.5 2.5 copy-start.25
  376.5 3.7 copy-start.23
  376.5 3.7 copy-start.31
  376.6 6.2 %copy-start.8 = (bf16[8,96,768]{2,1,0:T(8,128)(2,1)S(1)}, bf16[8,96,768]{2,1,0:T(8,128)(2,1)}, u32[]{:S(2)}) copy-start(bf16[8,96,768]{2,1,0:T(8,128)(2,1)} %copy-done.7) | copy-start | bytes 3538948
  460.4 3.2 copy-start.9
  460.4 3.2 copy-start.35
  460.4 3.2 copy-start.37
  461.7 2.2 copy-start.15
  461.7 2.2 copy-start.17
  461.7 2.2 copy-start.19
  463.9 3.6 copy-start.2
  464.0 3.6 copy-start.44
  464.0 3.6 copy-start.46
  464.0 3.6 copy-start.48
  464.0 3.6 copy-start.51
  464.0 3.6 copy-start.53
  464.0 3.6 copy-start.55
  464.0 3.6 copy-start.57
  464.0 3.6 copy-start.61
  464.0 3.6 copy-start.64
  464.0 3.6 copy-start.65
  464.1 3.6 copy-start.66
  467.7 2.5 copy-start.41
  467.7 2.5 copy-start.59
  470.2 2.9 copy-start.4
  (14 other events, 15.8 us)
Sparse Core Ops, SparseCore 0:
  9.9 75.1 all-gather.3
  87.0 45.6 all-gather.5
  134.6 47.8 all-gather.7
  224.9 82.5 reduce-scatter.3
  310.7 63.7 reduce-scatter.5
  377.8 85.0 reduce-scatter.7

commit v3 on v2

--- a/solution.py
+++ b/solution.py
@@ -51,37 +51,193 @@
 
 
 def lanes(start):
-    return pl.ds(pl.multiple_of(start * TILE, TILE), TILE)
+    return span(start, TILE)
+
+
+def span(start, size):
+    return pl.ds(pl.multiple_of(start * size, size), size)
+
+
+def cost(micros):
+    return pl.CostEstimate(flops=micros * 1_150_000_000, bytes_accessed=0, transcendentals=0)
+
+
+def vmem(count):
+    return [pl.BlockSpec(memory_space=pltpu.VMEM)] * count
+
+
+def hbm(count):
+    return [pl.BlockSpec(memory_space=pl.ANY)] * count
+
+
+def params(number=None, limit=60):
+    if number is None:
+        return pltpu.CompilerParams(vmem_limit_bytes=limit << 20)
+    return pltpu.CompilerParams(
+        collective_id=number, has_side_effects=True, vmem_limit_bytes=limit << 20
+    )
+
+
+def remote(source, target, send, recv, device):
+    return pltpu.make_async_remote_copy(
+        src_ref=source, dst_ref=target, send_sem=send, recv_sem=recv,
+        device_id=device, device_id_type=pl.DeviceIdType.MESH,
+    )
+
+
+def meet(context, owners):
+    place, row = lax.axis_index("context"), lax.axis_index("expert")
+    barrier = pltpu.get_barrier_semaphore()
+    for far in range(1, context):
+        pl.semaphore_signal(
+            barrier, inc=1, device_id={"context": lax.rem(place + far, context)},
+            device_id_type=pl.DeviceIdType.MESH,
+        )
+    for far in range(1, owners):
+        pl.semaphore_signal(
+            barrier, inc=1, device_id={"expert": lax.rem(row + far, owners)},
+            device_id_type=pl.DeviceIdType.MESH,
+        )
+    pl.semaphore_wait(barrier, context + owners - 2)
+    return place, row
 
 
 def attn_forward_kernel(
-    heads, size, ranks, scale,
-    a_ref, wt_ref, cos_ref, sin_ref, ids_col_ref, ids_row_ref,
+    dims,
+    ids_ref, pieces_ref, input_ref, cos_ref, sin_ref, grads_ref, output_ref, gate_ref, up_ref,
     out_ref, out_t_ref, lse_ref, query_t_ref, key_ref, key_t_ref, value_ref,
-    value_t_ref, scores_ref, acc_ref,
+    a_ref, ids_all_ref, wt_ref, output_all_ref, wide_ref, grads_all_ref,
+    w_all_ref, value_t_ref, scores_ref, acc_ref,
+    local_sem, send_sem, recv_sem, pass_sem, land_sem, row_send, row_recv, wide_send, wide_recv,
 ):
+    heads, size, ranks, scale, context, owners, roles = dims
     length = a_ref.shape[0]
+    rows = length // context
+    shard = output_ref.shape[0]
+    half = wide_ref.shape[2]
     width = heads * size
     tiles = length // TILE
     own_tiles = tiles // ranks
     ext = size + EXTRA
-    tail = (lax.broadcasted_iota(jnp.int32, (EXTRA, TILE), 0) == 0).astype(BF16)
+    chips = context // 2
+    place, row = meet(context, owners)
+    chip, core = place // 2, lax.rem(place, 2)
+    partner = place + 1 - 2 * core
+
+    def source(item, device):
+        return (ids_ref, pieces_ref.at[device // ranks], input_ref, output_ref)[item]
+
+    def target(item, device):
+        return (
+            ids_all_ref.at[:, span(device, rows)],
+            w_all_ref.at[device],
+            a_ref.at[span(device, rows), :],
+            output_all_ref.at[span(device, shard), :],
+        )[item]
+
+    def sends(item, far):
+        peer = partner if isinstance(far, int) and far == 0 else None
+        if peer is None:
+            peer = 2 * lax.rem(chip + far, chips) + core
+        return remote(
+            source(item, peer), target(item, place), send_sem.at[item, far],
+            recv_sem.at[item, far], {"context": peer},
+        )
+
+    def passes(item, far):
+        block = target(item, 2 * lax.rem(chip + chips - far, chips) + core)
+        return remote(
+            block, block, pass_sem.at[item, far], land_sem.at[item, far], {"context": partner}
+        )
+
+    def keeps(item):
+        return pltpu.make_async_copy(
+            source(item, place), target(item, place), local_sem.at[item]
+        )
+
+    for item in range(4):
+        for far in list(range(1, chips)) + [0]:
+            sends(item, far).start()
+        keeps(item).start()
+    to_rows = []
+    for far in range(1, owners):
+        peer = lax.rem(row + far, owners)
+        to_rows.append(
+            remote(
+                grads_ref.at[peer], grads_all_ref.at[row], row_send.at[far], row_recv.at[far],
+                {"expert": peer},
+            )
+        )
+    to_rows.append(
+        pltpu.make_async_copy(grads_ref.at[row], grads_all_ref.at[row], local_sem.at[4])
+    )
+    wide = []
+    for which, weight in enumerate((gate_ref, up_ref)):
+        spot = wide_ref.at[which, span(place, shard), :]
+
+        def block(device):
+            role = device // 2 // (chips // roles)
+            return weight.at[role, :, span(lax.rem(device, 2), half)]
+
+        for far in range(1, context):
+            peer = lax.rem(place + far, context)
+            wide.append(
+                remote(
+                    block(peer), spot, wide_send.at[which, far], wide_recv.at[which, far],
+                    {"context": peer},
+                )
+            )
+        wide.append(pltpu.make_async_copy(block(place), spot, local_sem.at[5 + which]))
+    for copy in to_rows + wide:
+        copy.start()
+
+    tail = (lax.broadcasted_iota(jnp.int32, (EXTRA, rows), 0) == 0).astype(BF16)
+    for item in range(2):
+        for far in range(1, chips):
+            sends(item, far).wait_recv()
+            passes(item, far).start()
+        sends(item, 0).wait_recv()
+        keeps(item).wait()
+        for far in range(1, chips):
+            passes(item, far).wait_recv()
+    for device in range(context):
+        wt_ref[:, device * shard : (device + 1) * shard] = w_all_ref[device]
 
     def project(step, carry):
-        at = lanes(step)
+        far, second = step // 2, lax.rem(step, 2)
+        block = 2 * lax.rem(chip + chips - far, chips) + jnp.where(second == 0, core, 1 - core)
+
+        @pl.when(jnp.logical_and(far == 0, second == 0))
+        def _():
+            keeps(2).wait()
+
+        @pl.when(jnp.logical_and(far == 0, second == 1))
+        def _():
+            sends(2, 0).wait_recv()
+
+        @pl.when(jnp.logical_and(far > 0, second == 0))
+        def _():
+            sends(2, far).wait_recv()
+            passes(2, far).start()
+
+        @pl.when(jnp.logical_and(far > 0, second == 1))
+        def _():
+            passes(2, far).wait_recv()
+
+        at = span(block, rows)
         both = dot(wt_ref[width:, :], a_ref[at, :], 1, 1)
         key_t = turn(both[:width], cos_ref[:, at], sin_ref[:, at], heads, size)
         key_t_ref[:, at] = key_t.astype(BF16)
         value_t = both[width:]
         for head in range(heads):
-            rows = slice(head * size, (head + 1) * size)
-            key_ref[head, at, :] = key_t[rows].T.astype(BF16)
-            value_ref[head, at, :] = value_t[rows].T.astype(BF16)
-            value_t_ref[head * ext : head * ext + size, at] = value_t[rows].astype(BF16)
+            here = slice(head * size, (head + 1) * size)
+            key_ref[head, at, :] = key_t[here].T.astype(BF16)
+            value_ref[head, at, :] = value_t[here].T.astype(BF16)
+            value_t_ref[head * ext : head * ext + size, at] = value_t[here].astype(BF16)
             value_t_ref[head * ext + size : (head + 1) * ext, at] = tail
         return carry
 
-    lax.fori_loop(0, tiles, project, 0)
+    lax.fori_loop(0, 2 * chips, project, 0)
 
     def attend(index, carry):
         tile = own_tile(index, ranks)
@@ -90,13 +246,13 @@
         query_t = turn(query_t, cos_ref[:, at], sin_ref[:, at], heads, size)
         query_t = query_t.astype(BF16) * jnp.asarray(scale, BF16)
         query_t_ref[:, lanes(index)] = query_t
-        query_ids = ids_row_ref[:, at]
+        query_ids = ids_all_ref[0:1, at]
 
         def score(step, tops, masked):
             here = lanes(step)
             fresh = []
             if masked:
-                allowed = ids_col_ref[here, :] <= query_ids
+                allowed = ids_all_ref[:, here].T[:, 0:1] <= query_ids
             for head in range(heads):
                 part = dot(key_ref[head, here, :], query_t[head * size : (head + 1) * size])
                 if masked:
@@ -134,24 +290,155 @@
         return carry
 
     lax.fori_loop(0, own_tiles, attend, 0)
+    for far in range(1, chips):
+        sends(3, far).wait_recv()
+        passes(3, far).start()
+    sends(3, 0).wait_recv()
+    keeps(3).wait()
+    for far in range(1, chips):
+        passes(3, far).wait_recv()
+    for item in range(4):
+        sends(item, 0).wait_send()
+        for far in range(1, chips):
+            sends(item, far).wait_send()
+            passes(item, far).wait_send()
+    for copy in to_rows + wide:
+        copy.wait()
+
+
+def attn_forward(
+    ids, pieces, attn_input, cos_t, sin_t, grads, output_weight, gate_weight, up_weight,
+    heads, size, ranks, context, roles, number,
+):
+    rows, model = attn_input.shape
+    owners = grads.shape[0]
+    length = rows * context
+    own = length // ranks
+    width = heads * size
+    ext = size + EXTRA
+    shard = output_weight.shape[0]
+    chips = context // 2
+    shapes = (
+        jax.ShapeDtypeStruct((own, width), BF16),
+        jax.ShapeDtypeStruct((width, own), F32),
+        jax.ShapeDtypeStruct((heads, own), F32),
+        jax.ShapeDtypeStruct((width, own), BF16),
+        jax.ShapeDtypeStruct((heads, length, size), BF16),
+        jax.ShapeDtypeStruct((width, length), BF16),
+        jax.ShapeDtypeStruct((heads, length, size), BF16),
+        jax.ShapeDtypeStruct((length, model), BF16),
+        jax.ShapeDtypeStruct((8, length), F32),
+        jax.ShapeDtypeStruct((3 * width, model), BF16),
+        jax.ShapeDtypeStruct((model, model), BF16),
+        jax.ShapeDtypeStruct((2, model, gate_weight.shape[2] // 2), BF16),
+        jax.ShapeDtypeStruct(grads.shape, BF16),
+    )
+    dims = (heads, size, ranks, size ** (-0.5), context, owners, roles)
+    return pl.pallas_call(
+        functools.partial(attn_forward_kernel, dims),
+        out_shape=shapes,
+        in_specs=vmem(5) + hbm(4),
+        out_specs=vmem(10) + hbm(3),
+        scratch_shapes=[
+            pltpu.VMEM((context, 3 * width, shard), BF16),
+            pltpu.VMEM((heads * ext, length), BF16),
+            pltpu.VMEM((heads, length, TILE), F32),
+            pltpu.VMEM((heads, ext, TILE), F32),
+            pltpu.SemaphoreType.DMA((7,)),
+            pltpu.SemaphoreType.DMA((4, chips)),
+            pltpu.SemaphoreType.DMA((4, chips)),
+            pltpu.SemaphoreType.DMA((4, chips)),
+            pltpu.SemaphoreType.DMA((4, chips)),
+            pltpu.SemaphoreType.DMA((owners,)),
+            pltpu.SemaphoreType.DMA((owners,)),
+            pltpu.SemaphoreType.DMA((2, context)),
+            pltpu.SemaphoreType.DMA((2, context)),
+        ],
+        compiler_params=params(number, 62),
+        cost_estimate=cost(80),
+        name="attn_forward",
+    )(ids, pieces, attn_input, cos_t, sin_t, grads, output_weight, gate_weight, up_weight)
 
 
 def attn_backward_kernel(
-    heads, size, ranks, scale,
-    grad_ref, a_ref, wt_ref, cos_ref, sin_ref, ids_col_ref, ids_row_ref,
+    dims,
+    grad_ref, a_ref, wt_ref, cos_ref, sin_ref, ids_all_ref,
     out_t_ref, lse_ref, query_t_ref, key_ref, key_t_ref, value_ref,
-    da_ref, pieces_ref,
+    wide_ref, down_ref, outs_ref, output_ref,
+    da_ref, pieces_ref, wide_in_ref, down_in_ref, outs_in_ref, output_in_ref,
     query_ref, own_grad_ref, dq_ref, dk_ref, dv_ref, grad_w_ref,
+    wide_send, wide_recv, down_send, down_recv, output_send, output_recv,
+    row_send, row_recv, local_sem,
 ):
+    heads, size, ranks, scale, context, owners, roles = dims
     length = a_ref.shape[0]
+    shard = pieces_ref.shape[2]
     width = heads * size
     tiles = length // TILE
     own_tiles = tiles // ranks
+    chips = context // 2
+    place, row = meet(context, owners)
+    chip, core = place // 2, lax.rem(place, 2)
+    copies = []
+    for far in range(context):
+        peer = lax.rem(place + far, context)
+        pairs = (
+            (wide_ref.at[:, span(peer, shard), :], wide_in_ref, wide_send, wide_recv),
+            (output_ref.at[span(peer, shard), :], output_in_ref, output_send, output_recv),
+        )
+        for item, (source, target, send, recv) in enumerate(pairs):
+            if far == 0:
+                copies.append(
+                    pltpu.make_async_copy(source, target.at[place], local_sem.at[item])
+                )
+            else:
+                copies.append(
+                    remote(
+                        source, target.at[place], send.at[far], recv.at[far], {"context": peer}
+                    )
+                )
+    for far in range(owners):
+        peer = lax.rem(row + far, owners)
+        if far == 0:
+            copies.append(
+                pltpu.make_async_copy(outs_ref.at[row], outs_in_ref.at[row], local_sem.at[2])
+            )
+        else:
+            copies.append(
+                remote(
+                    outs_ref.at[peer], outs_in_ref.at[row], row_send.at[far], row_recv.at[far],
+                    {"expert": peer},
+                )
+            )
+    for copy in copies:
+        copy.start()
+    down_rows = down_in_ref.shape[1]
+
+    def down_copy(index, here):
+        device = core * chips + index
+        source = down_ref.at[span(index, down_rows), :]
+        spot = down_in_ref.at[chip]
+        if here:
+            return pltpu.make_async_copy(source, spot, down_recv.at[chip])
+        return remote(
+            source, spot, down_send.at[index], down_recv.at[chip], {"context": device}
+        )
+
+    for index in range(chips):
+        here = core * chips + index == place
+
+        @pl.when(here)
+        def _():
+            down_copy(index, True).start()
+
+        @pl.when(jnp.logical_not(here))
+        def _():
+            down_copy(index, False).start()
+
     dk_ref[...] = jnp.zeros_like(dk_ref)
     dv_ref[...] = jnp.zeros_like(dv_ref)
     da_ref[...] = jnp.zeros_like(da_ref)
     grad_w_ref[...] = jnp.zeros_like(grad_w_ref)
-
     def attend(index, carry):
         tile = own_tile(index, ranks)
         at = lanes(tile)
@@ -159,7 +446,7 @@
         grad_rows = grad_ref[lanes(index), :]
         grad_t = grad_rows.astype(F32).T
         query_rows = query_t.astype(F32).T.astype(BF16)
-        query_ids = ids_row_ref[:, at]
+        query_ids = ids_all_ref[0:1, at]
         deltas, tops, grads_low = [], [], []
         for head in range(heads):
             rows = slice(head * size, (head + 1) * size)
@@ -175,7 +462,7 @@
         def chunk(step, carry, masked):
             here = lanes(step)
             if masked:
-                allowed = ids_col_ref[here, :] <= query_ids
+                allowed = ids_all_ref[:, here].T[:, 0:1] <= query_ids
             for head in range(heads):
                 rows = slice(head * size, (head + 1) * size)
                 scores = dot(key_ref[head, here, :], query_t[rows]) - tops[head]
@@ -213,104 +500,58 @@
         return carry
 
     lax.fori_loop(0, tiles, finish, 0)
-    shard = pieces_ref.shape[2]
     for piece in range(pieces_ref.shape[0]):
         pieces_ref[piece] = grad_w_ref[:, piece * shard : (piece + 1) * shard]
-
-
-def expert_kernel(
-    rows_ref, grad_ref, prob_ref, gate_ref, up_ref, down_ref,
-    out_ref, grad_rows_ref, dot_ref, grad_gate_ref, grad_up_ref, grad_down_ref,
-    rows_t_ref, dye_ref, out_acc_ref, grad_acc_ref,
+    for copy in copies:
+        copy.wait()
+    for index in range(chips):
+        here = core * chips + index == place
+        giver = 2 * index + place // chips
+
+        @pl.when(jnp.logical_not(here))
+        def _():
+            down_copy(index, False).wait_send()
+
+        land = down_in_ref.at[index]
+
+        @pl.when(giver == place)
+        def _():
+            pltpu.make_async_copy(
+                down_ref.at[span(0, down_rows), :], land, down_recv.at[index]
+            ).wait()
+
+        @pl.when(giver != place)
+        def _():
+            remote(
+                down_ref.at[span(0, down_rows), :], land, down_send.at[index],
+                down_recv.at[index], {"context": giver},
+            ).wait_recv()
+
+
+def attn_backward(
+    grad_own, a_full, weights_t, cos_t, sin_t, ids, kept,
+    grad_wide, grad_down, outs, grad_output, heads, size, ranks, context, roles, number,
 ):
-    step = pl.program_id(1)
-
-    @pl.when(step == 0)
-    def _():
-        rows_t_ref[...] = rows_ref[:, 0].reshape(dye_ref.shape).astype(F32).T.astype(BF16)
-        grads = grad_ref[:, 0].reshape(dye_ref.shape).astype(F32)
-        dye_ref[...] = (grads * prob_ref[0]).astype(BF16)
-        out_acc_ref[...] = jnp.zeros_like(out_acc_ref)
-        grad_acc_ref[...] = jnp.zeros_like(grad_acc_ref)
-
-    rows = rows_ref[:, 0].reshape(dye_ref.shape)
-    dye = dye_ref[...]
-    gate = gate_ref[0]
-    up = up_ref[0]
-    down = down_ref[0]
-    gate_pre = dot(rows, gate)
-    up_pre = dot(rows, up)
-    sigmoid = jax.nn.sigmoid(gate_pre)
-    silu = gate_pre * sigmoid
-    hidden = silu * up_pre
-    hidden_low = hidden.astype(BF16)
-    out_acc_ref[...] += dot(hidden_low, down)
-    grad_hidden = dot(dye, down, 1, 1).astype(BF16).astype(F32)
-    grad_down_ref[0] = dot(hidden.T.astype(BF16), dye).astype(BF16)
-    grad_gate = (grad_hidden * up_pre * sigmoid * (1.0 + gate_pre * (1.0 - sigmoid))).astype(BF16)
-    grad_up = (grad_hidden * silu).astype(BF16)
-    grad_gate_ref[0] = dot(rows_t_ref[...], grad_gate).astype(BF16)
-    grad_up_ref[0] = dot(rows_t_ref[...], grad_up).astype(BF16)
-    grad_acc_ref[...] += dot(grad_gate, gate, 1, 1) + dot(grad_up, up, 1, 1)
-
-    @pl.when(step == pl.num_programs(1) - 1)
-    def _():
-        out_low = out_acc_ref[...].astype(BF16)
-        blocks = out_ref.shape[:1] + out_ref.shape[2:]
-        out_ref[:, 0] = out_low.reshape(blocks)
-        grad_rows_ref[:, 0] = grad_acc_ref[...].astype(BF16).reshape(blocks)
-        grads = grad_ref[:, 0].reshape(dye_ref.shape).astype(F32)
-        dot_ref[0] = jnp.sum(out_low.astype(F32) * grads, axis=1, keepdims=True)
-
-
-def vmem(count):
-    return [pl.BlockSpec(memory_space=pltpu.VMEM)] * count
-
-
-def attn_forward(a_full, weights_t, cos_t, sin_t, ids, heads, size, ranks):
-    length = a_full.shape[0]
-    own = length // ranks
+    length, model = a_full.shape
     width = heads * size
-    ext = size + EXTRA
-    shapes = (
-        jax.ShapeDtypeStruct((own, width), BF16),
-        jax.ShapeDtypeStruct((width, own), F32),
-        jax.ShapeDtypeStruct((heads, own), F32),
-        jax.ShapeDtypeStruct((width, own), BF16),
-        jax.ShapeDtypeStruct((heads, length, size), BF16),
-        jax.ShapeDtypeStruct((width, length), BF16),
-        jax.ShapeDtypeStruct((heads, length, size), BF16),
-    )
-    return pl.pallas_call(
-        functools.partial(attn_forward_kernel, heads, size, ranks, size ** (-0.5)),
-        out_shape=shapes,
-        in_specs=vmem(6),
-        out_specs=vmem(7),
-        scratch_shapes=[
-            pltpu.VMEM((heads * ext, length), BF16),
-            pltpu.VMEM((heads, length, TILE), F32),
-            pltpu.VMEM((heads, ext, TILE), F32),
-        ],
-        compiler_params=pltpu.CompilerParams(vmem_limit_bytes=60 << 20),
-        cost_estimate=cost(37),
-        name="attn_forward",
-    )(a_full, weights_t, cos_t, sin_t, ids[:, None], ids[None, :])
-
-
-def attn_backward(
-    grad_full, a_full, weights_t, cos_t, sin_t, ids, kept, heads, size, ranks, context
-):
-    length = a_full.shape[0]
-    width = heads * size
+    owners = outs.shape[0]
+    shard = model // context
+    chips = context // 2
+    down_rows = grad_down.shape[0] // chips
     shapes = (
         jax.ShapeDtypeStruct(a_full.shape, BF16),
-        jax.ShapeDtypeStruct((context, weights_t.shape[0], a_full.shape[1] // context), F32),
-    )
+        jax.ShapeDtypeStruct((context, weights_t.shape[0], shard), F32),
+        jax.ShapeDtypeStruct((context, 2, shard, grad_wide.shape[2]), BF16),
+        jax.ShapeDtypeStruct((chips, down_rows, model), BF16),
+        jax.ShapeDtypeStruct(outs.shape, BF16),
+        jax.ShapeDtypeStruct((context, shard, model), BF16),
+    )
+    dims = (heads, size, ranks, size ** (-0.5), context, owners, roles)
     return pl.pallas_call(
-        functools.partial(attn_backward_kernel, heads, size, ranks, size ** (-0.5)),
+        functools.partial(attn_backward_kernel, dims),
         out_shape=shapes,
-        in_specs=vmem(13),
-        out_specs=vmem(2),
+        in_specs=vmem(12) + hbm(4),
+        out_specs=vmem(2) + hbm(4),
         scratch_shapes=[
             pltpu.VMEM((heads, TILE, size), BF16),
             pltpu.VMEM((heads, TILE, size), BF16),
@@ -318,195 +559,389 @@
             pltpu.VMEM((heads, length, size), F32),
             pltpu.VMEM((heads, length, size), F32),
             pltpu.VMEM(weights_t.shape, F32),
-        ],
-        compiler_params=pltpu.CompilerParams(vmem_limit_bytes=63 << 20),
-        cost_estimate=cost(58),
+        ]
+        + [pltpu.SemaphoreType.DMA((context,))] * 2
+        + [pltpu.SemaphoreType.DMA((chips,))] * 2
+        + [pltpu.SemaphoreType.DMA((context,))] * 2
+        + [pltpu.SemaphoreType.DMA((owners,))] * 2
+        + [pltpu.SemaphoreType.DMA((3,))],
+        compiler_params=params(number, 63),
+        cost_estimate=cost(60),
         name="attn_backward",
-    )(grad_full, a_full, weights_t, cos_t, sin_t, ids[:, None], ids[None, :], *kept)
-
-
-def experts(rows, grads, gates, gate_full, up_full, down_full):
-    owners, count, cap, width = rows.shape
-    slots = owners * cap
-    hidden = gate_full.shape[2]
-    per_row = pl.BlockSpec((owners, 1, cap, width), lambda e, t: (0, e, 0, 0))
-    column = pl.BlockSpec((1, slots, 1), lambda e, t: (e, 0, 0))
-    wide = pl.BlockSpec((1, width, HIDDEN_TILE), lambda e, t: (e, 0, t))
-    tall = pl.BlockSpec((1, HIDDEN_TILE, width), lambda e, t: (e, t, 0))
+    )(
+        grad_own, a_full, weights_t, cos_t, sin_t, ids, *kept,
+        grad_wide, grad_down, outs, grad_output,
+    )
+
+
+def expert_kernel(
+    rows_ref, grad_ref, prob_ref, wide_ref, down_ref,
+    out_ref, grad_rows_ref, dot_ref, grad_wide_ref, grad_down_ref,
+    rows_t_ref, dye_ref, out_acc_ref, grad_acc_ref,
+):
+    step = pl.program_id(0)
+    flat = dye_ref.shape
+
+    @pl.when(step == 0)
+    def _():
+        rows_t_ref[...] = rows_ref[...].reshape(flat).astype(F32).T.astype(BF16)
+        grads = grad_ref[...].reshape(flat).astype(F32)
+        dye_ref[...] = (grads * prob_ref[...]).astype(BF16)
+        out_acc_ref[...] = jnp.zeros_like(out_acc_ref)
+        grad_acc_ref[...] = jnp.zeros_like(grad_acc_ref)
+
+    rows = rows_ref[...].reshape(flat)
+    dye = dye_ref[...]
+    gate, up, down = wide_ref[0], wide_ref[1], down_ref[...]
+    gate_pre = dot(rows, gate)
+    up_pre = dot(rows, up)
+    sigmoid = jax.nn.sigmoid(gate_pre)
+    silu = gate_pre * sigmoid
+    hidden = silu * up_pre
+    out_acc_ref[...] += dot(hidden.astype(BF16), down)
+    grad_hidden = dot(dye, down, 1, 1).astype(BF16).astype(F32)
+    grad_down_ref[...] = dot(hidden.T.astype(BF16), dye).astype(BF16)
+    grad_gate = (grad_hidden * up_pre * sigmoid * (1.0 + gate_pre * (1.0 - sigmoid))).astype(BF16)
+    grad_up = (grad_hidden * silu).astype(BF16)
+    grad_wide_ref[0] = dot(rows_t_ref[...], grad_gate).astype(BF16)
+    grad_wide_ref[1] = dot(rows_t_ref[...], grad_up).astype(BF16)
+    grad_acc_ref[...] += dot(grad_gate, gate, 1, 1) + dot(grad_up, up, 1, 1)
+
+    @pl.when(step == pl.num_programs(0) - 1)
+    def _():
+        out = out_acc_ref[...]
+        out_ref[...] = out.astype(BF16).reshape(out_ref.shape)
+        grad_rows_ref[...] = grad_acc_ref[...].astype(BF16).reshape(out_ref.shape)
+        grads = grad_ref[...].reshape(flat).astype(F32)
+        dot_ref[...] = jnp.sum(out * grads, axis=1, keepdims=True)
+
+
+def experts(rows, grads, gates, wide_full, down_full):
+    width = rows.shape[-1]
+    slots = rows.size // width
+    hidden = wide_full.shape[2]
+    per_row = pl.BlockSpec(rows.shape, lambda t: (0,) * rows.ndim)
+    column = pl.BlockSpec((slots, 1), lambda t: (0, 0))
+    wide = pl.BlockSpec((2, width, HIDDEN_TILE), lambda t: (0, 0, t))
+    tall = pl.BlockSpec((HIDDEN_TILE, width), lambda t: (t, 0))
     return pl.pallas_call(
         expert_kernel,
-        grid=(count, hidden // HIDDEN_TILE),
+        grid=(hidden // HIDDEN_TILE,),
         out_shape=(
             jax.ShapeDtypeStruct(rows.shape, BF16),
             jax.ShapeDtypeStruct(rows.shape, BF16),
-            jax.ShapeDtypeStruct((count, slots, 1), F32),
-            jax.ShapeDtypeStruct(gate_full.shape, BF16),
-            jax.ShapeDtypeStruct(up_full.shape, BF16),
+            jax.ShapeDtypeStruct((slots, 1), F32),
+            jax.ShapeDtypeStruct(wide_full.shape, BF16),
             jax.ShapeDtypeStruct(down_full.shape, BF16),
         ),
-        in_specs=[per_row, per_row, column, wide, wide, tall],
-        out_specs=(per_row, per_row, column, wide, wide, tall),
+        in_specs=[per_row, per_row, column, wide, tall],
+        out_specs=(per_row, per_row, column, wide, tall),
         scratch_shapes=[
             pltpu.VMEM((width, slots), BF16),
             pltpu.VMEM((slots, width), BF16),
             pltpu.VMEM((slots, width), F32),
             pltpu.VMEM((slots, width), F32),
         ],
-        compiler_params=pltpu.CompilerParams(vmem_limit_bytes=60 << 20),
+        compiler_params=params(),
         cost_estimate=cost(37),
         name="experts",
-    )(rows, grads, gates, gate_full, up_full, down_full)
-
-
-def cost(micros):
-    return pl.CostEstimate(flops=micros * 1_150_000_000, bytes_accessed=0, transcendentals=0)
-
-
-def swap_kernel(axis, stride, count, same, *refs):
-    total = len(same)
-    sources, targets = refs[:total], refs[total : 2 * total]
-    local_sem, send_sem, recv_sem = refs[2 * total :]
-    place = lax.axis_index(axis)
-    mine = lax.rem(place // stride, count)
-    barrier = pltpu.get_barrier_semaphore()
-    for far in range(1, count):
-        peer = lax.rem(mine + far, count)
-        pl.semaphore_signal(
-            barrier, inc=1, device_id={axis: place + (peer - mine) * stride},
-            device_id_type=pl.DeviceIdType.MESH,
-        )
-    pl.semaphore_wait(barrier, count - 1)
-    copies = []
-    for item in range(total):
-        for far in range(1, count):
-            peer = lax.rem(mine + far, count)
-            copies.append(
-                pltpu.make_async_remote_copy(
-                    src_ref=sources[item] if same[item] else sources[item].at[peer],
-                    dst_ref=targets[item].at[mine],
-                    send_sem=send_sem.at[item, far],
-                    recv_sem=recv_sem.at[item, far],
-                    device_id={axis: place + (peer - mine) * stride},
-                    device_id_type=pl.DeviceIdType.MESH,
-                )
-            )
-            copies[-1].start()
-    for item in range(total):
-        copies.append(
-            pltpu.make_async_copy(
-                sources[item] if same[item] else sources[item].at[mine],
-                targets[item].at[mine],
-                local_sem.at[item],
-            )
-        )
-        copies[-1].start()
-    for copy in copies:
-        copy.wait()
-
-
-def swap(arrays, axis, stride, count, number, same=None):
-    same = same or (False,) * len(arrays)
-    shapes = tuple(
-        jax.ShapeDtypeStruct(((count,) if own else ()) + array.shape, array.dtype)
-        for array, own in zip(arrays, same)
-    )
-    return pl.pallas_call(
-        functools.partial(swap_kernel, axis, stride, count, same),
-        out_shape=shapes,
-        in_specs=vmem(len(arrays)),
-        out_specs=vmem(len(arrays)),
-        scratch_shapes=[
-            pltpu.SemaphoreType.DMA((len(arrays),)),
-            pltpu.SemaphoreType.DMA((len(arrays), count)),
-            pltpu.SemaphoreType.DMA((len(arrays), count)),
-        ],
-        compiler_params=pltpu.CompilerParams(
-            collective_id=number, has_side_effects=True, vmem_limit_bytes=60 << 20
-        ),
-        name="swap",
-    )(*arrays)
-
-
-def gather_kernel(chips, ranks, split, *refs):
-    total = len(split)
-    sources, targets = refs[:total], refs[total : 2 * total]
-    local_sem, send_sem, recv_sem, pass_sem, land_sem = refs[2 * total :]
-    place = lax.axis_index("context")
+    )(rows, grads, gates, wide_full, down_full)
+
+
+def dispatch_kernel(
+    context, roles,
+    gates_ref, rows_ref, grad_ref, down_ref,
+    gates_all, rows_all, grad_all, down_all,
+    gates_stage, rows_stage,
+    local_sem, send_sem, recv_sem, pass_sem, land_sem, twin_sem, come_sem, relay_sem, reach_sem,
+    down_send, down_recv,
+):
+    owners = rows_ref.shape[0]
+    chips = context // 2
+    place, row = meet(context, owners)
     chip, core = place // 2, lax.rem(place, 2)
-    partner = 2 * chip + 1 - core
-
-    def piece(item, device):
-        return sources[item].at[device // ranks] if split[item] else sources[item]
-
-    def remote(source, target, send, recv, device):
-        return pltpu.make_async_remote_copy(
-            src_ref=source, dst_ref=target, send_sem=send, recv_sem=recv,
-            device_id={"context": device}, device_id_type=pl.DeviceIdType.MESH,
-        )
-
-    barrier = pltpu.get_barrier_semaphore()
-    for far in range(1, chips):
-        pl.semaphore_signal(
-            barrier, inc=1, device_id={"context": 2 * lax.rem(chip + far, chips) + core},
-            device_id_type=pl.DeviceIdType.MESH,
-        )
-    pl.semaphore_signal(
-        barrier, inc=1, device_id={"context": partner}, device_id_type=pl.DeviceIdType.MESH
-    )
-    pl.semaphore_wait(barrier, chips)
-    sent = {}
-    for item in range(total):
-        for far in range(chips):
-            peer = partner if far == 0 else 2 * lax.rem(chip + far, chips) + core
+    partner = {"context": place + 1 - 2 * core}
+    slot = chip // (chips // roles)
+    other = (roles - 1) - slot
+    twin = {"context": 2 * lax.rem(chip + chips // 2, chips) + core}
+    sent, others, local, passed, lent, relayed = {}, {}, [], [], {}, []
+    for far in range(1, owners):
+        peer = lax.rem(row + far, owners)
+        pairs = [
+            (gates_ref.at[peer], gates_all.at[slot, core, row]),
+            (rows_ref.at[peer, slot], rows_all.at[slot, core, row]),
+        ]
+        if roles > 1:
+            pairs.append((rows_ref.at[peer, other], rows_stage.at[row]))
+        for item, (source, target) in enumerate(pairs):
             sent[item, far] = remote(
-                piece(item, peer), targets[item].at[place],
-                send_sem.at[item, far], recv_sem.at[item, far], peer,
+                source, target, send_sem.at[item, far], recv_sem.at[item, far], {"expert": peer}
             )
             sent[item, far].start()
-    local = []
-    for item in range(total):
-        local.append(
-            pltpu.make_async_copy(
-                piece(item, place), targets[item].at[place], local_sem.at[item]
+    own = (
+        (gates_ref.at[row], gates_all.at[slot, core, row]),
+        (rows_ref.at[row, slot], rows_all.at[slot, core, row]),
+        (grad_ref.at[:, slot], grad_all.at[slot, core]),
+    )
+    for item, (source, target) in enumerate(own):
+        local.append(pltpu.make_async_copy(source, target, local_sem.at[item]))
+        local[-1].start()
+        passed.append(
+            remote(source, target, pass_sem.at[item, 0], land_sem.at[item, 0], partner)
+        )
+        passed[-1].start()
+    if roles > 1:
+        own = (
+            (gates_ref.at[row], gates_all.at[slot, core, row], gates_all.at[other, core, row]),
+            (rows_ref.at[row, other], rows_all.at[slot, core, row], rows_all.at[other, core, row]),
+            (grad_ref.at[:, other], grad_all.at[slot, core], grad_all.at[other, core]),
+        )
+        for item, (source, target, arriving) in enumerate(own):
+            lent[item, 0] = (
+                remote(source, target, twin_sem.at[item, 0], come_sem.at[item, 0], twin), arriving
             )
-        )
-        local[-1].start()
-    passed = []
-    for item in range(total):
-        for far in range(1, chips):
+            lent[item, 0][0].start()
+
+    half = place // chips
+    down_rows = down_ref.shape[1]
+    spot = down_all.at[span(lax.rem(place, chips), down_rows), :]
+
+    def down_copy(far, here):
+        to_chip = lax.rem(chip + far, chips)
+        source = down_ref.at[to_chip // (chips // roles)]
+        if here:
+            return pltpu.make_async_copy(source, spot, down_recv.at[lax.rem(place, chips)])
+        return remote(
+            source, spot, down_send.at[far], down_recv.at[lax.rem(place, chips)],
+            {"context": 2 * to_chip + half},
+        )
+
+    for far in range(1, chips):
+        down_copy(far, False).start()
+
+    @pl.when(half == core)
+    def _():
+        down_copy(0, True).start()
+
+    @pl.when(half != core)
+    def _():
+        down_copy(0, False).start()
+
+    for far in range(1, owners):
+        peer = lax.rem(row + owners - far, owners)
+        for item in range(2):
             sent[item, far].wait_recv()
-            block = targets[item].at[2 * lax.rem(chip + chips - far, chips) + core]
+            block = (gates_all, rows_all)[item].at[slot, core, peer]
             passed.append(
                 remote(block, block, pass_sem.at[item, far], land_sem.at[item, far], partner)
             )
             passed[-1].start()
-    for item in range(total):
-        sent[item, 0].wait_recv()
-        for far in range(chips):
-            sent[item, far].wait_send()
-    for copy in local + passed:
+            if roles > 1:
+                if item == 1:
+                    sent[2, far].wait_recv()
+                source = block if item == 0 else rows_stage.at[peer]
+                arriving = (gates_all, rows_all)[item].at[other, core, peer]
+                lent[item, far] = (
+                    remote(source, block, twin_sem.at[item, far], come_sem.at[item, far], twin),
+                    arriving,
+                )
+                lent[item, far][0].start()
+    for (item, far), (copy, arriving) in lent.items():
+        copy.wait_recv()
+        relayed.append(
+            remote(
+                arriving, arriving, relay_sem.at[item, far], reach_sem.at[item, far], partner
+            )
+        )
+        relayed[-1].start()
+    for copy in sent.values():
+        copy.wait_send()
+    for copy, arriving in lent.values():
+        copy.wait_send()
+    for copy in local + passed + relayed:
         copy.wait()
-
-
-def gather(arrays, split, context, ranks, number):
+    for far in range(1, chips):
+        down_copy(far, False).wait_send()
+
+    @pl.when(half != core)
+    def _():
+        down_copy(0, False).wait_send()
+
+    for index in range(chips):
+        giver = core * chips + index
+        land = down_all.at[span(index, down_rows), :]
+
+        @pl.when(giver == place)
+        def _():
+            pltpu.make_async_copy(down_ref.at[0], land, down_recv.at[index]).wait()
+
+        @pl.when(giver != place)
+        def _():
+            remote(
+                down_ref.at[0], land, down_send.at[0], down_recv.at[index], {"context": giver}
+            ).wait_recv()
+
+
+def dispatch(gates, rows, grads, down_weight, context, roles, number):
+    owners, _, cap, width = rows.shape
     chips = context // 2
-    total = len(arrays)
-    shapes = tuple(
-        jax.ShapeDtypeStruct((context,) + (array.shape[1:] if cut else array.shape), array.dtype)
-        for array, cut in zip(arrays, split)
-    )
+    down_rows = down_weight.shape[1]
     return pl.pallas_call(
-        functools.partial(gather_kernel, chips, ranks, split),
-        out_shape=shapes,
-        in_specs=vmem(total),
-        out_specs=vmem(total),
-        scratch_shapes=[pltpu.SemaphoreType.DMA((total,))]
-        + [pltpu.SemaphoreType.DMA((total, chips))] * 4,
-        compiler_params=pltpu.CompilerParams(
-            collective_id=number, has_side_effects=True, vmem_limit_bytes=60 << 20
+        functools.partial(dispatch_kernel, context, roles),
+        out_shape=(
+            jax.ShapeDtypeStruct((roles, 2) + gates.shape, gates.dtype),
+            jax.ShapeDtypeStruct((roles, 2, owners, cap, width), BF16),
+            jax.ShapeDtypeStruct((roles, 2, owners, cap, width), BF16),
+            jax.ShapeDtypeStruct((chips * down_rows, width), BF16),
         ),
-        name="gather",
-    )(*arrays)
+        in_specs=vmem(3) + hbm(1),
+        out_specs=vmem(3) + hbm(1),
+        scratch_shapes=[
+            pltpu.VMEM(gates.shape, gates.dtype),
+            pltpu.VMEM((owners, cap, width), BF16),
+            pltpu.SemaphoreType.DMA((3,)),
+        ]
+        + [pltpu.SemaphoreType.DMA((3, owners))] * 8
+        + [pltpu.SemaphoreType.DMA((chips,))] * 2,
+        compiler_params=params(number),
+        name="dispatch",
+    )(gates, rows, grads, down_weight)
+
+
+def collect_kernel(
+    context, roles,
+    dots_ref, grad_ref, out_ref, dots_back, grad_back, out_back,
+    dots_twin, grad_twin, out_twin, dots_sum, grad_sum, out_sum, dots_relay, grad_relay,
+    pair_send, pair_recv, send_sem, recv_sem, lend_sem, come_sem, relay_send, relay_recv,
+    out_send, out_recv, out_lend, out_come,
+):
+    owners = grad_ref.shape[2]
+    chips = context // 2
+    place, row = meet(context, owners)
+    chip, core = place // 2, lax.rem(place, 2)
+    partner = {"context": place + 1 - 2 * core}
+    slot = chip // (chips // roles)
+    other = (roles - 1) - slot
+    twin = {"context": 2 * lax.rem(chip + chips // 2, chips) + core}
+    order = list(range(1, owners)) + [0]
+    turns = (other, slot) if roles > 1 else (slot,)
+    pair, sent, lent, relayed, outs, loans = {}, {}, {}, {}, [], []
+    items = (
+        (dots_ref, dots_twin, dots_sum, dots_relay, dots_back),
+        (grad_ref, grad_twin, grad_sum, grad_relay, grad_back),
+    )
+    for far in order:
+        peer = lax.rem(row + far, owners)
+        for which, spot in enumerate(turns):
+            for item, (source, landing, _, _, _) in enumerate(items):
+                pair[item, which, far] = remote(
+                    source.at[spot, 1 - core, peer], landing.at[spot, peer],
+                    pair_send.at[item, which, far], pair_recv.at[item, which, far], partner,
+                )
+                pair[item, which, far].start()
+    for which, spot in enumerate(turns):
+        outs.append(
+            remote(
+                out_ref.at[spot, 1 - core], out_twin.at[spot],
+                out_send.at[which], out_recv.at[which], partner,
+            )
+        )
+        outs[-1].start()
+
+    def leave(which, far):
+        peer = lax.rem(row + far, owners)
+        spot = turns[which]
+        for item, (_, _, total, relay, back) in enumerate(items):
+            if roles > 1 and which == 0:
+                target = back.at[row, slot] if far == 0 else relay.at[peer]
+                lent[item, far] = remote(
+                    total.at[spot, peer], target, lend_sem.at[item, far],
+                    come_sem.at[item, far], twin,
+                )
+                lent[item, far].start()
+            elif far > 0:
+                sent[item, far] = remote(
+                    total.at[spot, peer], back.at[row, slot], send_sem.at[item, far],
+                    recv_sem.at[item, far], {"expert": peer},
+                )
+                sent[item, far].start()
+
+    last = None
+    for far in order:
+        peer = lax.rem(row + far, owners)
+        for which, spot in enumerate(turns):
+            for item, (source, landing, total, _, _) in enumerate(items):
+                pair[item, which, far].wait_recv()
+                summed = source[spot, core, peer].astype(F32) + landing[spot, peer].astype(F32)
+                total[spot, peer] = summed.astype(total.dtype)
+            if last is not None:
+                leave(*last)
+            last = (which, far)
+    dots_back[row, slot] = dots_sum[slot, row]
+    grad_back[row, slot] = grad_sum[slot, row]
+    leave(*last)
+    if roles > 1:
+        for far in range(1, owners):
+            peer = lax.rem(row + far, owners)
+            for item, (_, _, _, relay, back) in enumerate(items):
+                lent[item, far].wait_recv()
+                relayed[item, far] = remote(
+                    relay.at[peer], back.at[row, other], relay_send.at[item, far],
+                    relay_recv.at[item, far], {"expert": peer},
+                )
+                relayed[item, far].start()
+    for which, spot in enumerate(turns):
+        outs[which].wait_recv()
+        for peer in range(owners):
+            summed = out_ref[spot, core, peer].astype(F32) + out_twin[spot, peer].astype(F32)
+            if roles > 1 and which == 0:
+                out_sum[peer] = summed.astype(BF16)
+            else:
+                out_back[peer, slot] = summed.astype(BF16)
+    if roles > 1:
+        loans.append(
+            remote(out_sum, out_back.at[:, slot], out_lend, out_come, twin)
+        )
+        loans[-1].start()
+        for item in range(2):
+            lent[item, 0].wait_recv()
+    for copy in list(pair.values()) + outs + list(lent.values()):
+        copy.wait_send()
+    for copy in list(sent.values()) + list(relayed.values()) + loans:
+        copy.wait()
+
+
+def collect(dots, grads, outs, context, roles, number):
+    _, _, owners, cap, width = grads.shape
+    home = (owners, roles, cap, width)
+    small = (owners, roles) + dots.shape[3:]
+    return pl.pallas_call(
+        functools.partial(collect_kernel, context, roles),
+        out_shape=(
+            jax.ShapeDtypeStruct(small, F32),
+            jax.ShapeDtypeStruct(home, BF16),
+            jax.ShapeDtypeStruct(home, BF16),
+        ),
+        in_specs=vmem(3),
+        out_specs=vmem(3),
+        scratch_shapes=[
+            pltpu.VMEM((roles, owners) + dots.shape[3:], F32),
+            pltpu.VMEM((roles, owners, cap, width), BF16),
+            pltpu.VMEM((roles, owners, cap, width), BF16),
+            pltpu.VMEM((roles, owners) + dots.shape[3:], F32),
+            pltpu.VMEM((roles, owners, cap, width), BF16),
+            pltpu.VMEM((owners, cap, width), BF16),
+            pltpu.VMEM((owners,) + dots.shape[3:], F32),
+            pltpu.VMEM((owners, cap, width), BF16),
+            pltpu.SemaphoreType.DMA((2, roles, owners)),
+            pltpu.SemaphoreType.DMA((2, roles, owners)),
+        ]
+        + [pltpu.SemaphoreType.DMA((2, owners))] * 6
+        + [pltpu.SemaphoreType.DMA((roles,))] * 2
+        + [pltpu.SemaphoreType.DMA] * 2,
+        compiler_params=params(number),
+        name="collect",
+    )(dots, grads, outs)
 
 
 def granule_kernel(ranks, shard_granules, outward, source_ref, target_ref, send_sem, recv_sem):
@@ -627,12 +1062,6 @@
     def greet(device):
         pl.semaphore_signal(
             barrier, inc=1, device_id=device, device_id_type=pl.DeviceIdType.MESH
-        )
-
-    def remote(source, target, send, recv, device):
-        return pltpu.make_async_remote_copy(
-            src_ref=source, dst_ref=target, send_sem=send, recv_sem=recv,
-            device_id=device, device_id_type=pl.DeviceIdType.MESH,
         )
 
     greet({"context": partner})
@@ -703,7 +1132,10 @@
             stack_ref[which * shard : (which + 1) * shard, group * width : (group + 1) * width] = (
                 total[which * width : (which + 1) * width].T
             )
-    stack_ref[3 * shard :, :] = output_ref[...]
+    total = output_ref[0].astype(F32)
+    for other in range(1, output_ref.shape[0]):
+        total = total + output_ref[other].astype(F32)
+    stack_ref[3 * shard :, :] = total
     lines = shares.shape[1]
     for owner in range(owners):
         shares[owner] = stack_ref[owner * lines : (owner + 1) * lines, :].astype(BF16)
@@ -754,12 +1186,12 @@
         copy.wait_send()
 
 
-def finish(da, pieces, small, output_share, owners, groups, number):
+def finish(da, pieces, small, output_parts, owners, groups, number):
     context, tokens, width = da.shape
     chips = context // 2
     lines, shard = pieces.shape[1:]
     few = small.shape[1]
-    stack = 3 * shard + output_share.shape[0]
+    stack = 4 * shard
     block = (stack // owners, width)
     return pl.pallas_call(
         functools.partial(finish_kernel, chips, owners, groups),
@@ -796,11 +1228,7 @@
             collective_id=number, has_side_effects=True, vmem_limit_bytes=60 << 20
         ),
         name="finish",
-    )(da, pieces, small, output_share)
-
-
-def exchange(value, axis_name, axis):
-    return lax.all_to_all(value, axis_name, split_axis=axis, concat_axis=axis, tiled=True)
+    )(da, pieces, small, output_parts)
 
 
 def shards(
@@ -836,6 +1264,7 @@
     per_owner = gate_weight.shape[0]
     slot_count = per_owner * owners * CAP
     shard_width = model_width // context
+    roles = per_owner
     residual = hidden_in[0].astype(F32)
     prior_rows = prior_logits[0]
     route_rows = routes[0]
@@ -849,14 +1278,6 @@
     stacked = jnp.stack([query_weight, key_weight, value_weight])
     stacked = stacked.reshape(3, shard_width, groups, width)
     pieces = jnp.transpose(stacked, (2, 0, 3, 1)).reshape(groups, 3 * width, shard_width)
-    ids_all, w_all, a_all, output_all = gather(
-        (ids_wide, pieces, attn_input, output_weight),
-        (False, True, False, False), context, ranks, 0,
-    )
-    a_full = a_all.reshape(length, model_width)
-    output_full = output_all.reshape(model_width, model_width)
-    ids = ids_all[:, 0, :].reshape(length)
-    weights_t = jnp.transpose(w_all, (1, 0, 2)).reshape(3 * width, model_width)
     half = head_size // 2
     freq = jnp.power(THETA, -2.0 * jnp.arange(half, dtype=F32) / head_size)
     angle = freq[:, None] * jnp.arange(length, dtype=jnp.int32).astype(F32)[None, :]
@@ -882,16 +1303,14 @@
     def pick(rows):
         return jnp.dot(pick_either, rows, preferred_element_type=F32).astype(BF16).reshape(blocks)
 
-    cotangent_late, a_full = lax.optimization_barrier((cotangent_low, a_full))
-    grad_arrived = exchange(pick(cotangent_late), "expert", 0)
-
     (
         attn_out, out_t, log_total, query_t, key_heads, key_t, value_heads,
-    ) = attn_forward(a_full, weights_t, cos_t, sin_t, ids, heads, head_size, ranks)
+        a_full, ids, weights_t, output_full, wide_full, grad_arrived,
+    ) = attn_forward(
+        ids_wide, pieces, attn_input, cos_t, sin_t, pick(cotangent_low),
+        output_weight, gate_weight, up_weight, heads, head_size, ranks, context, roles, 0,
+    )
     kept = (out_t, log_total, query_t, key_heads, key_t, value_heads)
-    gate_full = lax.all_gather(gate_weight, "context", axis=1, tiled=True)
-    up_full = lax.all_gather(up_weight, "context", axis=1, tiled=True)
-    down_full = lax.all_gather(down_weight, "context", axis=1, tiled=True)
     granule = TILE // 2
     shard_granules = token_rows // granule
     out_blocks = granules(
@@ -929,24 +1348,24 @@
         values = values.reshape(owners, per_owner, CAP)
         return jnp.pad(values, ((0, 0), (0, 8 - per_owner), (0, 128 - CAP)))
 
-    gates, arrived = swap(
-        (spread(slot_gate), pick(moe_input.astype(BF16))), "expert", 1, owners, 2
-    )
-    gates = jnp.transpose(gates[:, :per_owner, :CAP], (1, 0, 2)).reshape(per_owner, -1, 1)
-
-    expert_out, grad_rows, owner_dot, grad_gate, grad_up, grad_down = experts(
-        arrived, grad_arrived, gates, gate_full, up_full, down_full
-    )
-    share_gate = lax.psum_scatter(grad_gate, "context", scatter_dimension=1, tiled=True)
-    share_up = lax.psum_scatter(grad_up, "context", scatter_dimension=1, tiled=True)
-    share_down = lax.psum_scatter(grad_down, "context", scatter_dimension=1, tiled=True)
-
-    owner_dot = jnp.transpose(owner_dot.reshape(per_owner, owners, CAP), (1, 0, 2))
-    slot_dot, grad_back = swap((spread(owner_dot), grad_rows), "expert", 1, owners, 3)
-    slot_dot = slot_dot[:, :per_owner, :CAP].reshape(slot_count)
+    gates, arrived, grad_arrived, down_full = dispatch(
+        spread(slot_gate), pick(moe_input.astype(BF16)), grad_arrived, down_weight,
+        context, roles, 2,
+    )
+    role = lax.axis_index("context") // 2 // (context // 2 // roles)
+    gates = lax.dynamic_index_in_dim(gates, role, 3, keepdims=False)[..., :CAP].reshape(-1, 1)
+
+    expert_out, grad_rows, owner_dot, grad_wide, grad_down = experts(
+        arrived, grad_arrived, gates, wide_full, down_full
+    )
+    owner_dot = jnp.pad(
+        owner_dot.reshape(roles, 2, owners, 1, CAP), ((0, 0),) * 3 + ((0, 7), (0, 128 - CAP))
+    )
+    slot_dot, grad_back, expert_out = collect(
+        owner_dot, grad_rows, expert_out, context, roles, 3
+    )
+    slot_dot = slot_dot[:, :, 0, :CAP].reshape(slot_count)
     grad_back = grad_back.reshape(slot_count, model_width)
-    expert_out, grad_back = lax.optimization_barrier((expert_out, grad_back))
-    returned = exchange(expert_out, "expert", 0).reshape(slot_count, model_width)
 
     const_soft = jax.nn.softmax(narrow_out[:, expert_count:].reshape(token_rows, consts, 2), axis=2)
     const_gate = gated[:, FFN_E + 2 :]
@@ -1035,17 +1454,21 @@
     grad_output_local = lax.dot_general(
         mix_low, grad_attn_low, (((0,), (0,)), ((), ())), preferred_element_type=F32
     ).astype(BF16)
-    output_parts = exchange(
-        grad_output_local.reshape(context, shard_width, model_width), "context", 0
-    )
-
-    output_share = jnp.sum(output_parts.astype(F32), axis=0)
-    da_part, w_pieces = attn_backward(
-        grad_own, a_full, weights_t, cos_t, sin_t, ids, kept, heads, head_size, ranks, context
-    )
-    da_part, returned = lax.optimization_barrier((da_part, returned))
+    da_part, w_pieces, wide_parts, down_parts, returned, output_parts = attn_backward(
+        grad_own, a_full, weights_t, cos_t, sin_t, ids, kept,
+        grad_wide, grad_down, expert_out, grad_output_local,
+        heads, head_size, ranks, context, roles, 6,
+    )
+    returned = returned.reshape(slot_count, model_width)
+    same = context // 2 // roles
+    wide_parts = wide_parts.reshape(roles, same, 2, 2, shard_width, -1)
+    wide_sum = jnp.sum(wide_parts.astype(F32), axis=1)
+    wide_sum = jnp.transpose(wide_sum, (2, 0, 3, 1, 4)).reshape(2, roles, shard_width, -1)
+    down_sum = jnp.sum(
+        down_parts.reshape(roles, same, -1, model_width).astype(F32), axis=1
+    )
     grad_attn_input, sums, small_all = finish(
-        da_part.reshape(context, token_rows, model_width), w_pieces, small, output_share,
+        da_part.reshape(context, token_rows, model_width), w_pieces, small, output_parts,
         owners, groups, 5,
     )
     grad_normed_one = grad_attn_input * attn_gain
@@ -1089,9 +1512,9 @@
         grad_prior_weight,
         small_own[expert_count:mixes].reshape(consts, 2, shard_width),
         small_own[mixes : mixes + consts],
-        share_gate.astype(F32),
-        share_up.astype(F32),
-        share_down.astype(F32),
+        wide_sum[0],
+        wide_sum[1],
+        down_sum,
     )
 
 

time: 490 us -> 444 us (0.906); the launches traced: 489 us -> 436 us
  starting transfers between devices: 19.3 us -> 0 us
  between operations: 15.3 us -> 1.66 us
  Pallas kernels: 380 us -> 369 us
  matrix products: 26 us -> 17.4 us
  local copies, waits for them, and re-layouts: 21.5 us -> 26.6 us
    pallas_call x6 -> x5, Pallas kernels: 258 us -> 283 us  [the longest x1 84.8 us: attn_forward(): pl.pallas_call(functools.partial(attn_forward_kernel, dims), out_shape=sh...]
    pallas_call x1, Pallas kernels: 76.7 us -> 57 us  [finish(): pl.pallas_call(functools.partial(finish_kernel, chips, owners, groups), o...]
    all_to_all x3 -> x0, starting transfers between devices: 18.9 us -> none  [exchange(): lax.all_to_all(value, axis_name, split_axis=axis, concat_axis=axis, tiled...]
    pallas_call x2, Pallas kernels: 45.9 us -> 28.4 us  [granules(): pl.pallas_call(functools.partial(granule_kernel, ranks, shard_granules, o...]
    convert_element_type x3 -> x0, other arithmetic: 7.29 us -> none  [the longest x1 2.45 us: shards(): share_gate.astype(F32)]
    squeeze x0 -> x2, local copies, waits for them, and re-layouts: none -> 4.98 us  [the longest x1 2.49 us: shards(): wide_sum[0]]
  transfers between devices with their start and end apart: 9 -> 0, of which waited for: 0 -> 0; matrix products, arithmetic and copies ran while one was open for 14% -> 0% of each run, Pallas kernels for 70% -> 0%
where the time goes in v3:
time: 444 us; the launch traced here: 436 us
  Pallas kernels  369 us (83%)
  local copies, waits for them, and re-layouts  26.6 us (6%)
  other arithmetic  21.6 us (5%)
  matrix products  17.4 us (4%)
    pallas_call x1, Pallas kernels, attn_forward(): pl.pallas_call(functools.partial(attn_forward_kernel, dims), out_shape=sh...  84.8 us
    pallas_call x1, Pallas kernels, attn_backward(): pl.pallas_call(functools.partial(attn_backward_kernel, dims), out_shape=s...  74.4 us
    pallas_call x1, Pallas kernels, finish(): pl.pallas_call(functools.partial(finish_kernel, chips, owners, groups), o...  57 us
    pallas_call x1, Pallas kernels, dispatch(): pl.pallas_call(functools.partial(dispatch_kernel, context, roles), out_sh...  54.3 us
    pallas_call x1, Pallas kernels, collect(): pl.pallas_call(functools.partial(collect_kernel, context, roles), out_sha...  35.6 us
    pallas_call x1, Pallas kernels, experts(): pl.pallas_call(expert_kernel, grid=(hidden // HIDDEN_TILE,), out_shape=(j...  33.9 us
    pallas_call x2, Pallas kernels, granules(): pl.pallas_call(functools.partial(granule_kernel, ranks, shard_granules, o...  28.4 us

profile of v3, /device:TPU:0, one launch (start us, length us, event | category | flops | bytes accessed | tf_op | source)
XLA Modules:
  0.0 435.8 jit_solution(8114221230404221688)
XLA Ops:
  0.7 0.9 copy.135
  1.7 1.7 reduce-window.6
  4.3 0.3 slice_reduce_fusion.3
  4.6 1.9 convolution_convert_fusion.2
  6.5 2.3 multiply_sine_fusion
  9.0 1.0 fusion.8.input_ref
  10.6 1.0 pad_maximum_fusion
  11.6 0.6 broadcast_in_dim.102.ids_ref
  12.2 84.8 %attn_forward.1 = (bf16[1536,192]{1,0:T(8,128)(2,1)}, f32[192,1536]{1,0:T(8,128)}, f32[3,1536]{1,0:T(4,128)}, bf16[192,1536]{1,0:T(8,128)(2,1)}, bf16[3,3072,64]...) custom-call(f32[8,384]{1,0:T(8,128)} %broadcast_in_dim.102.ids_ref, ...), custom_call_target="tpu_custom_call" | custom-call | flops 92000002048 | tf_op jit(solution)/shard_map/attn_forward/pallas_call | solution.py:337
  97.0 14.7 %granules.2 = bf16[12,128,192]{2,1,0:T(8,128)(2,1)} custom-call(bf16[12,128,192]{2,1,0:T(8,128)(2,1)} %bitcast.151), custom_call_target="tpu_custom_call" | custom-call | tf_op jit(solution)/shard_map/granules/pallas_call | solution.py:1032
  111.8 1.5 copy.140
  113.3 2.1 multiply_reduce_fusion.2
  115.4 1.3 fusion.23
  116.7 0.2 fusion.74
  117.0 0.3 slice_reduce_fusion.1
  117.3 0.3 add_reduce_fusion
  117.7 0.6 pad.16.gates_ref
  118.3 1.9 convolution_convert_fusion.1
  120.2 54.3 %dispatch.1 = (f32[2,2,4,8,128]{4,3,2,1,0:T(8,128)}, bf16[2,2,4,96,768]{4,3,2,1,0:T(8,128)(2,1)}, bf16[2,2,4,96,768]{4,3,2,1,0:T(8,128)(2,1)}, bf16[1024,768]{1,0:T(8,128)(2,1)}) custom-call(f32[4,8,128]{2,1,0:T(8,128)} %pad.16.gates_ref, bf16[4,2,96,768]{3,2,1,0:T(8,128)(2,1)} %bitcast.149, bf16[4,2,96,768]{3,2,1,0:T(8,128)(2,1)} %get-tuple-element.52.grad_ref, ...), custom_call_target="tpu_custom_call" | custom-call | tf_op jit(solution)/shard_map/dispatch/pallas_call | solution.py:789
  174.6 0.9 constant_dynamic-slice_fusion
  175.5 1.6 reshape.226.prob_ref
  177.0 33.9 %experts.1 = (bf16[2,2,4,96,768]{4,3,2,1,0:T(8,128)(2,1)}, bf16[2,2,4,96,768]{4,3,2,1,0:T(8,128)(2,1)}, f32[1536,1]{1,0:T(8,128)}, bf16[2,768,1024]{2,1,0:T(8,128)(2,1)}, bf16[1024,768]{1,0:T(8,128)(2,1)}) custom-call(bf16[2,2,4,96,768]{4,3,2,1,0:T(8,128)(2,1)} %get-tuple-element.53.rows_ref, bf16[2,2,4,96,768]{4,3,2,1,0:T(8,128)(2,1)} %get-tuple-element.54.grad_ref, ...), custom_call_target="tpu_custom_call" | custom-call | flops 42550001664 | tf_op jit(solution)/shard_map/experts/pallas_call | solution.py:627
  210.9 1.4 reduce.14
  212.4 0.7 pad.17.dots_ref
  213.0 35.6 %collect.1 = (f32[4,2,8,128]{3,2,1,0:T(8,128)}, bf16[4,2,96,768]{3,2,1,0:T(8,128)(2,1)}, bf16[4,2,96,768]{3,2,1,0:T(8,128)(2,1)}) custom-call(f32[2,2,4,8,128]{4,3,2,1,0:T(8,128)} %pad.17.dots_ref, bf16[2,2,4,96,768]{4,3,2,1,0:T(8,128)(2,1)} %get-tuple-element.59.grad_ref, bf16[2,2,4,96,768]{4,3,2,1,0:T(8,128)(2,1)} %get-tuple-element.60.out_ref), custom_call_target="tpu_custom_call" | custom-call | tf_op jit(solution)/shard_map/collect/pallas_call | solution.py:918
  248.7 0.8 slice_reduce_fusion.4
  249.6 0.4 select_reduce_fusion.1
  250.1 0.9 fusion.16
  251.3 0.6 fusion.20
  252.0 1.2 fusion.48
  253.3 1.1 multiply_reduce_fusion
  254.3 0.4 convert_add_fusion
  254.7 1.8 convolution_convert_fusion.output_ref
  256.6 0.7 convolution_convert_fusion.3
  257.2 0.3 copy.147
  257.5 1.2 copy.148
  258.7 13.7 %granules.3 = bf16[12,128,192]{2,1,0:T(8,128)(2,1)} custom-call(bf16[12,128,192]{2,1,0:T(8,128)(2,1)} %bitcast.144), custom_call_target="tpu_custom_call" | custom-call | tf_op jit(solution)/shard_map/granules/pallas_call | solution.py:1032
  272.4 74.4 %attn_backward.1 = (bf16[3072,768]{1,0:T(8,128)(2,1)}, f32[8,576,96]{2,1,0:T(8,128)}, bf16[8,2,96,1024]{3,2,1,0:T(8,128)(2,1)}, bf16[4,256,768]{2,1,0:T(8,128)(2...) custom-call(bf16[1536,192]{1,0:T(8,128)(2,1)} %bitcast.150, ...), custom_call_target="tpu_custom_call" | custom-call | flops 69000003584 | tf_op jit(solution)/shard_map/attn_backward/pallas_call | solution.py:550
  346.8 3.1 convert_reduce_fusion
  349.9 1.5 fusion.72
  351.4 1.2 copy.152
  352.6 2.5 squeeze.56
  355.1 2.6 copy.153
  357.7 2.5 squeeze.57
  360.2 0.8 fusion.21
  361.2 0.3 copy.149
  361.5 0.8 fusion.63
  362.8 0.7 fusion.47.small_ref
  363.5 57.0 %finish.1 = (f32[384,768]{1,0:T(8,128)}, bf16[4,96,768]{2,1,0:T(8,128)(2,1)}, f32[4,24,96]{2,1,0:T(8,128)}) custom-call(bf16[8,384,768]{2,1,0:T(8,128)(2,1)} %bitcast.141, f32[8,576,96]{2,1,0:T(8,128)} %get-tuple-element.77.pieces_ref, f32[8,24,96]{2,1,0:T(8,128)} %fusion.47.small_ref, bf16[8,96,768]{2,1,0:T(8,128)(2,1)} %get-tuple-element.78.output_ref), custom_call_target="tpu_custom_call" | custom-call | tf_op jit(solution)/shard_map/finish/pallas_call | solution.py:1196
  420.6 1.2 convert_element_type.119
  421.8 1.0 add_reduce_fusion.1
  422.9 0.6 dynamic-slice_divide_fusion
  423.5 0.7 slice_bitcast_fusion
  424.2 1.9 fusion.9
  426.2 1.4 fusion.13
  427.6 0.6 fusion.73
  428.1 0.7 slice.145
  428.8 0.6 slice_bitcast_fusion.4
  429.4 0.6 slice.177
  430.0 0.5 slice_bitcast_fusion.7
  430.5 1.3 fusion.4
  431.8 1.6 fusion.7
  433.4 1.4 convert_reduce_fusion.1
  434.9 0.6 copy.154
  (123 shorter events, 3.6 us)
Async XLA Ops:
  0.6 116.0 %copy-start = (f32[12,12]{1,0:T(8,128)S(1)}, f32[12,12]{1,0:T(8,128)}, u32[]{:S(2)}) copy-start(f32[12,12]{1,0:T(8,128)} %param.30) | copy-start | bytes 1732
  0.7 3.9 copy-start.5
  4.6 4.2 copy-start.6
  6.5 2.6 copy-start.21
  6.5 3.6 copy-start.15
  8.8 1.4 copy-start.13
  8.8 1.6 copy-start.11
  9.0 1.2 copy-start.23
  10.1 1.5 copy-start.27
  113.2 2.1 copy-start.26
  113.3 2.1 copy-start.17
  113.3 2.1 copy-start.19
  115.3 139.0 %copy-start.1 = (f32[384,768]{1,0:T(8,128)}, f32[384,768]{1,0:T(8,128)S(1)}, u32[]{:S(2)}) copy-start(f32[384,768]{1,0:T(8,128)S(1)} %get-tuple-element.218) | copy-start | bytes 3538948
  115.3 1.4 copy-start.18
  213.0 37.0 %copy-start.25 = (f32[2,768]{1,0:T(2,128)S(1)}, f32[2,768]{1,0:T(2,128)}, u32[]{:S(2)}) copy-start(f32[2,768]{1,0:T(2,128)} %param.32) | copy-start | bytes 18436
  252.0 1.3 copy-start.28
  254.7 1.8 copy-start.3
  254.7 1.8 copy-start.10
  357.7 2.5 copy-start.2
  420.5 1.2 copy-start.12
  420.5 1.2 copy-start.14
  420.5 1.2 copy-start.16
  421.8 1.1 copy-start.22
  421.8 2.4 copy-start.7
  421.8 2.4 copy-start.24
  423.5 2.7 copy-start.4
  423.5 2.7 copy-start.8
  426.2 1.4 copy-start.20
  426.2 4.3 copy-start.29
  431.8 1.6 copy-start.9

commit v4 on v3

--- a/solution.py
+++ b/solution.py
@@ -50,6 +50,51 @@
     return (index // 2) * (2 * ranks) + jnp.where(place == 0, rank, 2 * ranks - 1 - rank)
 
 
+def granule_of(slot, ranks):
+    return own_tile(slot // 2, ranks) * 2 + lax.rem(slot, 2)
+
+
+def owner_rank(granule, ranks):
+    spot = lax.rem(granule // 2, 2 * ranks)
+    return jnp.minimum(spot, 2 * ranks - 1 - spot)
+
+
+def owner_slot(granule, ranks):
+    tile = granule // 2
+    upper = jnp.where(lax.rem(tile, 2 * ranks) >= ranks, 1, 0)
+    return (tile // (2 * ranks) * 2 + upper) * 2 + lax.rem(granule, 2)
+
+
+def here_or_away(device, source, target, send, recv):
+    place = lax.axis_index("context")
+
+    @pl.when(device == place)
+    def _():
+        pltpu.make_async_copy(source, target, recv).start()
+
+    @pl.when(device != place)
+    def _():
+        remote(source, target, send, recv, {"context": device}).start()
+
+
+def wait_sent(device, source, target, send, recv):
+    @pl.when(device != lax.axis_index("context"))
+    def _():
+        remote(source, target, send, recv, {"context": device}).wait_send()
+
+
+def wait_landed(device, source, target, send, recv):
+    place = lax.axis_index("context")
+
+    @pl.when(device == place)
+    def _():
+        pltpu.make_async_copy(source, target, recv).wait()
+
+    @pl.when(device != place)
+    def _():
+        remote(source, target, send, recv, {"context": device}).wait_recv()
+
+
 def lanes(start):
     return span(start, TILE)
 
@@ -83,6 +128,15 @@
         src_ref=source, dst_ref=target, send_sem=send, recv_sem=recv,
         device_id=device, device_id_type=pl.DeviceIdType.MESH,
     )
+
+
+def chip_at(chip, far, chips, square, back=False):
+    if square:
+        x, y = lax.rem(chip, 2), chip // 2
+        x = x + (far % 2) * (1 - 2 * x)
+        y = y + (far // 2) * (1 - 2 * y)
+        return 2 * y + x
+    return lax.rem(chip + (chips - far if back else far), chips)
 
 
 def meet(context, owners):
@@ -105,12 +159,15 @@
 def attn_forward_kernel(
     dims,
     ids_ref, pieces_ref, input_ref, cos_ref, sin_ref, grads_ref, output_ref, gate_ref, up_ref,
-    out_ref, out_t_ref, lse_ref, query_t_ref, key_ref, key_t_ref, value_ref,
-    a_ref, ids_all_ref, wt_ref, output_all_ref, wide_ref, grads_all_ref,
-    w_all_ref, value_t_ref, scores_ref, acc_ref,
-    local_sem, send_sem, recv_sem, pass_sem, land_sem, row_send, row_recv, wide_send, wide_recv,
+    out_t_ref, lse_ref, query_t_ref, ids_all_ref, wt_ref,
+    key_out, key_t_out, value_out, a_out, mix_ref,
+    output_all_ref, wide_ref, grads_all_ref, stage_ref,
+    w_all_ref, value_t_ref, scores_ref, acc_ref, key_ref, key_t_ref, value_ref, a_ref, out_ref,
+    keep_sem, granule_send, granule_recv,
+    local_sem, send_sem, recv_sem, pass_sem, land_sem, half_send, half_recv,
+    row_send, row_recv, hop_send, hop_recv, lend_send, lend_recv, wide_send, wide_recv,
 ):
-    heads, size, ranks, scale, context, owners, roles = dims
+    heads, size, ranks, scale, context, owners, roles, square = dims
     length = a_ref.shape[0]
     rows = length // context
     shard = output_ref.shape[0]
@@ -123,6 +180,9 @@
     place, row = meet(context, owners)
     chip, core = place // 2, lax.rem(place, 2)
     partner = place + 1 - 2 * core
+    slot = chip // (chips // roles)
+    other = (roles - 1) - slot
+    twin = 2 * lax.rem(chip + chips // 2, chips) + core
 
     def source(item, device):
         return (ids_ref, pieces_ref.at[device // ranks], input_ref, output_ref)[item]
@@ -135,17 +195,21 @@
             output_all_ref.at[span(device, shard), :],
         )[item]
 
+    def from_chip(far):
+        return 2 * chip_at(chip, far, chips, square, True) + core
+
     def sends(item, far):
-        peer = partner if isinstance(far, int) and far == 0 else None
-        if peer is None:
-            peer = 2 * lax.rem(chip + far, chips) + core
+        if isinstance(far, int) and far == 0:
+            peer = partner
+        else:
+            peer = 2 * chip_at(chip, far, chips, square) + core
         return remote(
             source(item, peer), target(item, place), send_sem.at[item, far],
             recv_sem.at[item, far], {"context": peer},
         )
 
     def passes(item, far):
-        block = target(item, 2 * lax.rem(chip + chips - far, chips) + core)
+        block = target(item, from_chip(far))
         return remote(
             block, block, pass_sem.at[item, far], land_sem.at[item, far], {"context": partner}
         )
@@ -155,23 +219,69 @@
             source(item, place), target(item, place), local_sem.at[item]
         )
 
-    for item in range(4):
-        for far in list(range(1, chips)) + [0]:
+    def halves(far):
+        upper = rows // 2
+        start = from_chip(far) * rows + (far - 1) * upper
+        block = a_ref.at[pl.ds(pl.multiple_of(start, upper), upper), :]
+        return remote(
+            block, block, half_send.at[far], half_recv.at[far],
+            {"context": 2 * chip_at(chip, 3 - far, chips, square) + core},
+        )
+
+    def corner(far):
+        upper = rows // 2
+        start = from_chip(3) * rows + (far - 1) * upper
+        block = a_ref.at[pl.ds(pl.multiple_of(start, upper), upper), :]
+        return remote(block, block, half_send.at[far], half_recv.at[far], {"context": partner})
+
+    direct = {item: list(range(1, chips)) for item in range(4)}
+    if square:
+        direct[2] = [1, 2]
+    def begin(item):
+        for far in direct[item] + [0]:
             sends(item, far).start()
         keeps(item).start()
-    to_rows = []
-    for far in range(1, owners):
+
+    for item in range(3):
+        begin(item)
+    shard_granules = rows // (TILE // 2)
+    group = place // ranks
+    owned = out_ref.shape[0]
+
+    def outgoing(step):
+        granule = granule_of(step, ranks)
+        target_slot = group * shard_granules + lax.rem(granule, shard_granules)
+        return (
+            granule // shard_granules, out_ref.at[step], mix_ref.at[target_slot],
+            granule_send.at[step], granule_recv.at[target_slot],
+        )
+
+    def part(device, which):
+        return grads_ref.at[device, which]
+
+    to_rows, hops, lends = {}, {}, {}
+    for far in range(owners):
         peer = lax.rem(row + far, owners)
-        to_rows.append(
-            remote(
-                grads_ref.at[peer], grads_all_ref.at[row], row_send.at[far], row_recv.at[far],
-                {"expert": peer},
-            )
-        )
-    to_rows.append(
-        pltpu.make_async_copy(grads_ref.at[row], grads_all_ref.at[row], local_sem.at[4])
-    )
-    wide = []
+        spots = [(slot, grads_all_ref.at[slot, core, row])]
+        if roles > 1:
+            spots.append((other, stage_ref.at[row]))
+        for which, (role, spot) in enumerate(spots):
+            if far > 0:
+                to_rows[which, far] = remote(
+                    part(peer, role), spot, row_send.at[which, far], row_recv.at[which, far],
+                    {"expert": peer},
+                )
+            elif which == 0:
+                to_rows[which, far] = pltpu.make_async_copy(part(row, role), spot, local_sem.at[4])
+            else:
+                lends[0] = remote(
+                    part(row, role), grads_all_ref.at[slot, core, row], lend_send.at[0],
+                    lend_recv.at[0], {"context": twin},
+                )
+    for copy in to_rows.values():
+        copy.start()
+
+    wide_out, wide_on = [], []
     for which, weight in enumerate((gate_ref, up_ref)):
         spot = wide_ref.at[which, span(place, shard), :]
 
@@ -179,17 +289,43 @@
             role = device // 2 // (chips // roles)
             return weight.at[role, :, span(lax.rem(device, 2), half)]
 
-        for far in range(1, context):
-            peer = lax.rem(place + far, context)
-            wide.append(
+        if square:
+            peers = [
+                (2 * chip_at(chip, far, chips, square) + side, 2 * far + turned)
+                for far in (1, 2)
+                for turned, side in enumerate((core, 1 - core))
+            ] + [(partner, 1)]
+        else:
+            peers = [(lax.rem(place + far, context), far) for far in range(1, context)]
+        for peer, index in peers:
+            wide_out.append(
                 remote(
-                    block(peer), spot, wide_send.at[which, far], wide_recv.at[which, far],
+                    block(peer), spot, wide_send.at[which, index], wide_recv.at[which, index],
                     {"context": peer},
                 )
             )
-        wide.append(pltpu.make_async_copy(block(place), spot, local_sem.at[5 + which]))
-    for copy in to_rows + wide:
-        copy.start()
+        wide_out.append(pltpu.make_async_copy(block(place), spot, local_sem.at[5 + which]))
+        if square:
+            for turned in range(2):
+                side = core if turned == 0 else 1 - core
+                giver = 2 * chip_at(chip, 2, chips, square) + side
+                block_on = wide_ref.at[which, span(giver, shard), :]
+                wide_on.append(
+                    remote(
+                        block_on, block_on, wide_send.at[which, 6 + turned],
+                        wide_recv.at[which, 6 + turned],
+                        {"context": 2 * chip_at(chip, 1, chips, square) + core},
+                    )
+                )
+    arrives = {}
+    if square:
+        index = 0
+        for which in range(2):
+            for far in (1, 2):
+                for turned in range(2):
+                    arrives[which, far, turned] = wide_out[index]
+                    index += 1
+            index += 2
 
     tail = (lax.broadcasted_iota(jnp.int32, (EXTRA, rows), 0) == 0).astype(BF16)
     for item in range(2):
@@ -205,7 +341,9 @@
 
     def project(step, carry):
         far, second = step // 2, lax.rem(step, 2)
-        block = 2 * lax.rem(chip + chips - far, chips) + jnp.where(second == 0, core, 1 - core)
+        block = 2 * chip_at(chip, far, chips, square, True) + jnp.where(
+            second == 0, core, 1 - core
+        )
 
         @pl.when(jnp.logical_and(far == 0, second == 0))
         def _():
@@ -215,10 +353,30 @@
         def _():
             sends(2, 0).wait_recv()
 
-        @pl.when(jnp.logical_and(far > 0, second == 0))
-        def _():
-            sends(2, far).wait_recv()
-            passes(2, far).start()
+        if square:
+
+            @pl.when(jnp.logical_and(far == 1, second == 0))
+            def _():
+                for near in (1, 2):
+                    sends(2, near).wait_recv()
+                    halves(near).start()
+                    passes(2, near).start()
+                begin(3)
+                for copy in wide_out:
+                    copy.start()
+
+            @pl.when(jnp.logical_and(far == 3, second == 0))
+            def _():
+                for near in (1, 2):
+                    corner(near).wait_recv()
+                passes(2, 3).start()
+
+        else:
+
+            @pl.when(jnp.logical_and(far > 0, second == 0))
+            def _():
+                sends(2, far).wait_recv()
+                passes(2, far).start()
 
         @pl.when(jnp.logical_and(far > 0, second == 1))
         def _():
@@ -238,8 +396,73 @@
         return carry
 
     lax.fori_loop(0, 2 * chips, project, 0)
+    if not square:
+        begin(3)
+        for copy in wide_out:
+            copy.start()
+    stored = [
+        pltpu.make_async_copy(source, target, keep_sem.at[index])
+        for index, (source, target) in enumerate(
+            ((key_ref, key_out), (key_t_ref, key_t_out), (value_ref, value_out), (a_ref, a_out))
+        )
+    ]
+    for copy in stored:
+        copy.start()
+    if roles > 1:
+        lends[0].start()
+    for far in range(owners):
+        peer = lax.rem(row + owners - far, owners)
+        home = grads_all_ref.at[slot, core, peer]
+        if far > 0:
+            to_rows[0, far].wait_recv()
+        else:
+            to_rows[0, far].wait()
+        hops[far] = remote(
+            home, home, hop_send.at[0, far], hop_recv.at[0, far], {"context": partner}
+        )
+        hops[far].start()
+        if roles > 1 and far > 0:
+            to_rows[1, far].wait_recv()
+            lends[far] = remote(
+                stage_ref.at[peer], home, lend_send.at[far], lend_recv.at[far],
+                {"context": twin},
+            )
+            lends[far].start()
+
+    def relays():
+        for far in range(1, chips):
+            sends(3, far).wait_recv()
+            passes(3, far).start()
+        for far in lends:
+            lends[far].wait_recv()
+            afar(far).start()
+
+    def afar(far):
+        away = grads_all_ref.at[other, core, lax.rem(row + owners - far, owners)]
+        return remote(
+            away, away, hop_send.at[1, far], hop_recv.at[1, far], {"context": partner}
+        )
 
     def attend(index, carry):
+        @pl.when(index > 0)
+        def _():
+            for step in range(2):
+                here_or_away(*outgoing(2 * index - 2 + step))
+
+        @pl.when(index == own_tiles - 1)
+        def _():
+            relays()
+
+        if square:
+
+            @pl.when(index == own_tiles // 2)
+            def _():
+                for which in range(2):
+                    for turned in range(2):
+                        arrives[which, 2, turned].wait_recv()
+                for copy in wide_on:
+                    copy.start()
+
         tile = own_tile(index, ranks)
         at = lanes(tile)
         query_t = dot(wt_ref[:width, :], a_ref[at, :], 1, 1)
@@ -286,24 +509,50 @@
             parts.append(part)
         joined = jnp.concatenate(parts, axis=0)
         out_t_ref[:, lanes(index)] = joined
-        out_ref[lanes(index), :] = joined.T.astype(BF16)
+        turned_out = joined.T.astype(BF16)
+        out_ref[2 * index] = turned_out[: TILE // 2]
+        out_ref[2 * index + 1] = turned_out[TILE // 2 :]
         return carry
 
     lax.fori_loop(0, own_tiles, attend, 0)
-    for far in range(1, chips):
-        sends(3, far).wait_recv()
-        passes(3, far).start()
+    for step in range(2):
+        here_or_away(*outgoing(2 * own_tiles - 2 + step))
     sends(3, 0).wait_recv()
     keeps(3).wait()
     for far in range(1, chips):
         passes(3, far).wait_recv()
     for item in range(4):
-        sends(item, 0).wait_send()
+        for far in direct[item] + [0]:
+            sends(item, far).wait_send()
         for far in range(1, chips):
-            sends(item, far).wait_send()
             passes(item, far).wait_send()
-    for copy in to_rows + wide:
+    if square:
+        for far in (1, 2):
+            halves(far).wait_send()
+    forwarded = [arrives[which, 2, turned] for which, _, turned in arrives if _ == 2]
+    for copy in wide_out:
+        if any(copy is one for one in forwarded):
+            copy.wait_send()
+        else:
+            copy.wait()
+    for (which, far), copy in to_rows.items():
+        if far > 0:
+            copy.wait_send()
+    for copy in lends.values():
+        copy.wait_send()
+    for copy in wide_on + list(hops.values()) + [afar(far) for far in lends] + stored:
         copy.wait()
+
+    def settle(step, carry):
+        wait_sent(*outgoing(step))
+        giver_group, spot = step // shard_granules, lax.rem(step, shard_granules)
+        giver = giver_group * ranks + owner_rank(place * shard_granules + spot, ranks)
+        wait_landed(
+            giver, out_ref.at[0], mix_ref.at[step], granule_send.at[0], granule_recv.at[step]
+        )
+        return carry
+
+    lax.fori_loop(0, owned, settle, 0)
 
 
 def attn_forward(
@@ -318,42 +567,59 @@
     ext = size + EXTRA
     shard = output_weight.shape[0]
     chips = context // 2
+    granule = TILE // 2
+    head_shape = jax.ShapeDtypeStruct((heads, length, size), BF16)
+    turned_shape = jax.ShapeDtypeStruct((width, length), BF16)
+    a_shape = jax.ShapeDtypeStruct((length, model), BF16)
+    own_shape = jax.ShapeDtypeStruct((own // granule, granule, width), BF16)
     shapes = (
-        jax.ShapeDtypeStruct((own, width), BF16),
         jax.ShapeDtypeStruct((width, own), F32),
         jax.ShapeDtypeStruct((heads, own), F32),
         jax.ShapeDtypeStruct((width, own), BF16),
-        jax.ShapeDtypeStruct((heads, length, size), BF16),
-        jax.ShapeDtypeStruct((width, length), BF16),
-        jax.ShapeDtypeStruct((heads, length, size), BF16),
-        jax.ShapeDtypeStruct((length, model), BF16),
         jax.ShapeDtypeStruct((8, length), F32),
         jax.ShapeDtypeStruct((3 * width, model), BF16),
+        head_shape,
+        turned_shape,
+        head_shape,
+        a_shape,
+        own_shape,
         jax.ShapeDtypeStruct((model, model), BF16),
         jax.ShapeDtypeStruct((2, model, gate_weight.shape[2] // 2), BF16),
-        jax.ShapeDtypeStruct(grads.shape, BF16),
-    )
-    dims = (heads, size, ranks, size ** (-0.5), context, owners, roles)
+        jax.ShapeDtypeStruct((roles, 2, owners) + grads.shape[2:], BF16),
+        jax.ShapeDtypeStruct((owners,) + grads.shape[2:], BF16),
+    )
+    square = chips == 4 and roles == 2
+    dims = (heads, size, ranks, size ** (-0.5), context, owners, roles, square)
     return pl.pallas_call(
         functools.partial(attn_forward_kernel, dims),
         out_shape=shapes,
         in_specs=vmem(5) + hbm(4),
-        out_specs=vmem(10) + hbm(3),
+        out_specs=vmem(5) + hbm(9),
         scratch_shapes=[
             pltpu.VMEM((context, 3 * width, shard), BF16),
             pltpu.VMEM((heads * ext, length), BF16),
             pltpu.VMEM((heads, length, TILE), F32),
             pltpu.VMEM((heads, ext, TILE), F32),
+        ]
+        + [
+            pltpu.VMEM(one.shape, one.dtype)
+            for one in (head_shape, turned_shape, head_shape, a_shape, own_shape)
+        ]
+        + [
+            pltpu.SemaphoreType.DMA((4,)),
+            pltpu.SemaphoreType.DMA((own // granule,)),
+            pltpu.SemaphoreType.DMA((own // granule,)),
             pltpu.SemaphoreType.DMA((7,)),
             pltpu.SemaphoreType.DMA((4, chips)),
             pltpu.SemaphoreType.DMA((4, chips)),
             pltpu.SemaphoreType.DMA((4, chips)),
             pltpu.SemaphoreType.DMA((4, chips)),
-            pltpu.SemaphoreType.DMA((owners,)),
-            pltpu.SemaphoreType.DMA((owners,)),
-            pltpu.SemaphoreType.DMA((2, context)),
-            pltpu.SemaphoreType.DMA((2, context)),
-        ],
+            pltpu.SemaphoreType.DMA((3,)),
+            pltpu.SemaphoreType.DMA((3,)),
+        ]
+        + [pltpu.SemaphoreType.DMA((2, owners))] * 4
+        + [pltpu.SemaphoreType.DMA((owners,))] * 2
+        + [pltpu.SemaphoreType.DMA((2, context))] * 2,
         compiler_params=params(number, 62),
         cost_estimate=cost(80),
         name="attn_forward",
@@ -364,10 +630,12 @@
     dims,
     grad_ref, a_ref, wt_ref, cos_ref, sin_ref, ids_all_ref,
     out_t_ref, lse_ref, query_t_ref, key_ref, key_t_ref, value_ref,
-    wide_ref, down_ref, outs_ref, output_ref,
-    da_ref, pieces_ref, wide_in_ref, down_in_ref, outs_in_ref, output_in_ref,
+    wide_ref, outs_ref, output_ref,
+    da_ref, pieces_ref, output_sum_ref, wide_in_ref, outs_in_ref,
     query_ref, own_grad_ref, dq_ref, dk_ref, dv_ref, grad_w_ref,
-    wide_send, wide_recv, down_send, down_recv, output_send, output_recv,
+    landed_ref, output_in_ref, share_ref, shares_ref,
+    granule_send, granule_recv, share_send, share_recv,
+    wide_send, wide_recv, output_send, output_recv,
     row_send, row_recv, local_sem,
 ):
     heads, size, ranks, scale, context, owners, roles = dims
@@ -379,20 +647,41 @@
     chips = context // 2
     place, row = meet(context, owners)
     chip, core = place // 2, lax.rem(place, 2)
-    copies = []
-    for far in range(context):
-        peer = lax.rem(place + far, context)
-        pairs = (
-            (wide_ref.at[:, span(peer, shard), :], wide_in_ref, wide_send, wide_recv),
-            (output_ref.at[span(peer, shard), :], output_in_ref, output_send, output_recv),
-        )
-        for item, (source, target, send, recv) in enumerate(pairs):
+    owned = landed_ref.shape[0]
+    shard_granules = owned * ranks // context
+
+    def outgoing(step):
+        giver = step // shard_granules
+        granule = place * shard_granules + lax.rem(step, shard_granules)
+        landing = owner_slot(granule, ranks)
+        return (
+            giver * ranks + owner_rank(granule, ranks), grad_ref.at[step],
+            landed_ref.at[landing], granule_send.at[step], granule_recv.at[landing],
+        )
+
+    def launch(step, carry):
+        here_or_away(*outgoing(step))
+        return carry
+
+    lax.fori_loop(0, owned, launch, 0)
+    copies, output_copies = [], []
+    for item, (grads, target, send, recv) in enumerate(
+        (
+            (output_ref, output_in_ref, output_send, output_recv),
+            (wide_ref, wide_in_ref, wide_send, wide_recv),
+        )
+    ):
+        for far in range(context):
+            peer = lax.rem(place + far, context)
+            at = span(peer, shard)
+            source = grads.at[:, at, :] if item else grads.at[at, :]
+            group_copies = copies if item else output_copies
             if far == 0:
-                copies.append(
+                group_copies.append(
                     pltpu.make_async_copy(source, target.at[place], local_sem.at[item])
                 )
             else:
-                copies.append(
+                group_copies.append(
                     remote(
                         source, target.at[place], send.at[far], recv.at[far], {"context": peer}
                     )
@@ -410,40 +699,46 @@
                     {"expert": peer},
                 )
             )
-    for copy in copies:
-        copy.start()
-    down_rows = down_in_ref.shape[1]
-
-    def down_copy(index, here):
-        device = core * chips + index
-        source = down_ref.at[span(index, down_rows), :]
-        spot = down_in_ref.at[chip]
-        if here:
-            return pltpu.make_async_copy(source, spot, down_recv.at[chip])
-        return remote(
-            source, spot, down_send.at[index], down_recv.at[chip], {"context": device}
-        )
-
-    for index in range(chips):
-        here = core * chips + index == place
-
-        @pl.when(here)
-        def _():
-            down_copy(index, True).start()
-
-        @pl.when(jnp.logical_not(here))
-        def _():
-            down_copy(index, False).start()
-
     dk_ref[...] = jnp.zeros_like(dk_ref)
     dv_ref[...] = jnp.zeros_like(dv_ref)
     da_ref[...] = jnp.zeros_like(da_ref)
     grad_w_ref[...] = jnp.zeros_like(grad_w_ref)
+    def landed(step, carry):
+        giver = granule_of(step, ranks) // shard_granules
+        wait_landed(
+            giver, grad_ref.at[0], landed_ref.at[step], granule_send.at[0], granule_recv.at[step]
+        )
+        return carry
+
+    lax.fori_loop(0, owned, landed, 0)
+    for copy in output_copies + copies:
+        copy.start()
+
+    def share_copy(far):
+        return remote(
+            share_ref, shares_ref.at[row], share_send.at[far], share_recv.at[far],
+            {"expert": lax.rem(row + far, owners)},
+        )
+
     def attend(index, carry):
         tile = own_tile(index, ranks)
         at = lanes(tile)
         query_t = query_t_ref[:, lanes(index)]
-        grad_rows = grad_ref[lanes(index), :]
+        @pl.when(index == own_tiles // 2)
+        def _():
+            for copy in output_copies:
+                copy.wait()
+            total = output_in_ref[0].astype(F32)
+            for giver in range(1, context):
+                total = total + output_in_ref[giver].astype(F32)
+            share_ref[...] = total.astype(BF16)
+
+        @pl.when(index == own_tiles // 2 + 1)
+        def _():
+            for far in range(1, owners):
+                share_copy(far).start()
+
+        grad_rows = landed_ref[pl.ds(2 * index, 2)].reshape(TILE, width)
         grad_t = grad_rows.astype(F32).T
         query_rows = query_t.astype(F32).T.astype(BF16)
         query_ids = ids_all_ref[0:1, at]
@@ -501,57 +796,45 @@
 
     lax.fori_loop(0, tiles, finish, 0)
     for piece in range(pieces_ref.shape[0]):
-        pieces_ref[piece] = grad_w_ref[:, piece * shard : (piece + 1) * shard]
+        pieces_ref[piece] = grad_w_ref[:, piece * shard : (piece + 1) * shard].astype(BF16)
     for copy in copies:
         copy.wait()
-    for index in range(chips):
-        here = core * chips + index == place
-        giver = 2 * index + place // chips
-
-        @pl.when(jnp.logical_not(here))
-        def _():
-            down_copy(index, False).wait_send()
-
-        land = down_in_ref.at[index]
-
-        @pl.when(giver == place)
-        def _():
-            pltpu.make_async_copy(
-                down_ref.at[span(0, down_rows), :], land, down_recv.at[index]
-            ).wait()
-
-        @pl.when(giver != place)
-        def _():
-            remote(
-                down_ref.at[span(0, down_rows), :], land, down_send.at[index],
-                down_recv.at[index], {"context": giver},
-            ).wait_recv()
+    for far in range(1, owners):
+        share_copy(far).wait()
+    shares_ref[row] = share_ref[...]
+    total = shares_ref[0].astype(F32)
+    for giver in range(1, owners):
+        total = total + shares_ref[giver].astype(F32)
+    output_sum_ref[...] = total
+
+    def settle(step, carry):
+        wait_sent(*outgoing(step))
+        return carry
+
+    lax.fori_loop(0, owned, settle, 0)
 
 
 def attn_backward(
     grad_own, a_full, weights_t, cos_t, sin_t, ids, kept,
-    grad_wide, grad_down, outs, grad_output, heads, size, ranks, context, roles, number,
+    grad_wide, outs, grad_output, heads, size, ranks, context, roles, number,
 ):
     length, model = a_full.shape
     width = heads * size
     owners = outs.shape[0]
     shard = model // context
-    chips = context // 2
-    down_rows = grad_down.shape[0] // chips
     shapes = (
         jax.ShapeDtypeStruct(a_full.shape, BF16),
-        jax.ShapeDtypeStruct((context, weights_t.shape[0], shard), F32),
+        jax.ShapeDtypeStruct((context, weights_t.shape[0], shard), BF16),
+        jax.ShapeDtypeStruct((shard, model), F32),
         jax.ShapeDtypeStruct((context, 2, shard, grad_wide.shape[2]), BF16),
-        jax.ShapeDtypeStruct((chips, down_rows, model), BF16),
         jax.ShapeDtypeStruct(outs.shape, BF16),
-        jax.ShapeDtypeStruct((context, shard, model), BF16),
     )
     dims = (heads, size, ranks, size ** (-0.5), context, owners, roles)
     return pl.pallas_call(
         functools.partial(attn_backward_kernel, dims),
         out_shape=shapes,
-        in_specs=vmem(12) + hbm(4),
-        out_specs=vmem(2) + hbm(4),
+        in_specs=vmem(12) + hbm(3),
+        out_specs=vmem(3) + hbm(2),
         scratch_shapes=[
             pltpu.VMEM((heads, TILE, size), BF16),
             pltpu.VMEM((heads, TILE, size), BF16),
@@ -559,10 +842,14 @@
             pltpu.VMEM((heads, length, size), F32),
             pltpu.VMEM((heads, length, size), F32),
             pltpu.VMEM(weights_t.shape, F32),
+            pltpu.VMEM(grad_own.shape, BF16),
+            pltpu.VMEM((context, shard, model), BF16),
+            pltpu.VMEM((shard, model), BF16),
+            pltpu.VMEM((owners, shard, model), BF16),
         ]
-        + [pltpu.SemaphoreType.DMA((context,))] * 2
-        + [pltpu.SemaphoreType.DMA((chips,))] * 2
-        + [pltpu.SemaphoreType.DMA((context,))] * 2
+        + [pltpu.SemaphoreType.DMA((grad_own.shape[0],))] * 2
+        + [pltpu.SemaphoreType.DMA((owners,))] * 2
+        + [pltpu.SemaphoreType.DMA((context,))] * 4
         + [pltpu.SemaphoreType.DMA((owners,))] * 2
         + [pltpu.SemaphoreType.DMA((3,))],
         compiler_params=params(number, 63),
@@ -570,91 +857,156 @@
         name="attn_backward",
     )(
         grad_own, a_full, weights_t, cos_t, sin_t, ids, *kept,
-        grad_wide, grad_down, outs, grad_output,
+        grad_wide, outs, grad_output,
     )
 
 
 def expert_kernel(
-    rows_ref, grad_ref, prob_ref, wide_ref, down_ref,
-    out_ref, grad_rows_ref, dot_ref, grad_wide_ref, grad_down_ref,
-    rows_t_ref, dye_ref, out_acc_ref, grad_acc_ref,
+    context, owners,
+    rows_ref, grad_ref, prob_ref, wide_hbm, down_hbm,
+    out_ref, grad_rows_ref, dot_ref, grad_wide_ref, down_in_ref,
+    wide_ref, down_ref, rows_t_ref, dye_ref, out_acc_ref, grad_acc_ref, grad_down_ref,
+    load_sem, down_send, down_recv,
 ):
-    step = pl.program_id(0)
     flat = dye_ref.shape
-
-    @pl.when(step == 0)
-    def _():
-        rows_t_ref[...] = rows_ref[...].reshape(flat).astype(F32).T.astype(BF16)
-        grads = grad_ref[...].reshape(flat).astype(F32)
-        dye_ref[...] = (grads * prob_ref[...]).astype(BF16)
-        out_acc_ref[...] = jnp.zeros_like(out_acc_ref)
-        grad_acc_ref[...] = jnp.zeros_like(grad_acc_ref)
-
-    rows = rows_ref[...].reshape(flat)
-    dye = dye_ref[...]
-    gate, up, down = wide_ref[0], wide_ref[1], down_ref[...]
-    gate_pre = dot(rows, gate)
-    up_pre = dot(rows, up)
-    sigmoid = jax.nn.sigmoid(gate_pre)
-    silu = gate_pre * sigmoid
-    hidden = silu * up_pre
-    out_acc_ref[...] += dot(hidden.astype(BF16), down)
-    grad_hidden = dot(dye, down, 1, 1).astype(BF16).astype(F32)
-    grad_down_ref[...] = dot(hidden.T.astype(BF16), dye).astype(BF16)
-    grad_gate = (grad_hidden * up_pre * sigmoid * (1.0 + gate_pre * (1.0 - sigmoid))).astype(BF16)
-    grad_up = (grad_hidden * silu).astype(BF16)
-    grad_wide_ref[0] = dot(rows_t_ref[...], grad_gate).astype(BF16)
-    grad_wide_ref[1] = dot(rows_t_ref[...], grad_up).astype(BF16)
-    grad_acc_ref[...] += dot(grad_gate, gate, 1, 1) + dot(grad_up, up, 1, 1)
-
-    @pl.when(step == pl.num_programs(0) - 1)
-    def _():
-        out = out_acc_ref[...]
-        out_ref[...] = out.astype(BF16).reshape(out_ref.shape)
-        grad_rows_ref[...] = grad_acc_ref[...].astype(BF16).reshape(out_ref.shape)
-        grads = grad_ref[...].reshape(flat).astype(F32)
-        dot_ref[...] = jnp.sum(out * grads, axis=1, keepdims=True)
-
-
-def experts(rows, grads, gates, wide_full, down_full):
+    chips = context // 2
+    loads = [
+        pltpu.make_async_copy(wide_hbm, wide_ref, load_sem.at[0]),
+        pltpu.make_async_copy(down_hbm, down_ref, load_sem.at[1]),
+    ]
+    for copy in loads:
+        copy.start()
+    place, _ = meet(context, owners)
+    chip, core = place // 2, lax.rem(place, 2)
+    down_rows = down_in_ref.shape[1]
+    per_step = HIDDEN_TILE // down_rows
+    tiles = wide_ref.shape[2] // HIDDEN_TILE
+
+    def down_copy(index, here):
+        source = grad_down_ref.at[index]
+        spot = down_in_ref.at[chip]
+        if here:
+            return pltpu.make_async_copy(source, spot, down_recv.at[chip])
+        return remote(
+            source, spot, down_send.at[index], down_recv.at[chip],
+            {"context": core * chips + index},
+        )
+
+    def start_down(index):
+        here = core * chips + index == place
+
+        @pl.when(here)
+        def _():
+            down_copy(index, True).start()
+
+        @pl.when(jnp.logical_not(here))
+        def _():
+            down_copy(index, False).start()
+
+    rows_t_ref[...] = rows_ref[...].reshape(flat).astype(F32).T.astype(BF16)
+    dye_ref[...] = (grad_ref[...].reshape(flat).astype(F32) * prob_ref[...]).astype(BF16)
+    out_acc_ref[...] = jnp.zeros_like(out_acc_ref)
+    grad_acc_ref[...] = jnp.zeros_like(grad_acc_ref)
+    for copy in loads:
+        copy.wait()
+
+    def hidden_tile(step, carry):
+        tile = lax.rem(step + (1 - lax.rem(chip, 2)) * (tiles // 2), tiles)
+        at = span(tile, HIDDEN_TILE)
+        rows = rows_ref[...].reshape(flat)
+        dye = dye_ref[...]
+        gate, up, down = wide_ref[0, :, at], wide_ref[1, :, at], down_ref[at, :]
+        gate_pre = dot(rows, gate)
+        up_pre = dot(rows, up)
+        sigmoid = jax.nn.sigmoid(gate_pre)
+        silu = gate_pre * sigmoid
+        hidden = silu * up_pre
+        grad_down = dot(hidden.T.astype(BF16), dye).astype(BF16)
+        for index in range(per_step):
+            grad_down_ref[tile * per_step + index] = grad_down[
+                index * down_rows : (index + 1) * down_rows
+            ]
+        grad_hidden = dot(dye, down, 1, 1).astype(BF16).astype(F32)
+        for index in range(per_step):
+            start_down(tile * per_step + index)
+        out_acc_ref[...] += dot(hidden.astype(BF16), down)
+        grad_gate = (
+            grad_hidden * up_pre * sigmoid * (1.0 + gate_pre * (1.0 - sigmoid))
+        ).astype(BF16)
+        grad_up = (grad_hidden * silu).astype(BF16)
+        grad_wide_ref[0, :, at] = dot(rows_t_ref[...], grad_gate).astype(BF16)
+        grad_wide_ref[1, :, at] = dot(rows_t_ref[...], grad_up).astype(BF16)
+        grad_acc_ref[...] += dot(grad_gate, gate, 1, 1) + dot(grad_up, up, 1, 1)
+        return carry
+
+    lax.fori_loop(0, tiles, hidden_tile, 0)
+    out = out_acc_ref[...]
+    out_ref[...] = out.astype(BF16).reshape(out_ref.shape)
+    grad_rows_ref[...] = grad_acc_ref[...].astype(BF16).reshape(out_ref.shape)
+    grads = grad_ref[...].reshape(flat).astype(F32)
+    dot_ref[...] = jnp.sum(out * grads, axis=1, keepdims=True)
+    for index in range(chips):
+        here = core * chips + index == place
+        giver = 2 * index + place // chips
+        land = down_in_ref.at[index]
+
+        @pl.when(jnp.logical_not(here))
+        def _():
+            down_copy(index, False).wait_send()
+
+        @pl.when(giver == place)
+        def _():
+            pltpu.make_async_copy(grad_down_ref.at[0], land, down_recv.at[index]).wait()
+
+        @pl.when(giver != place)
+        def _():
+            remote(
+                grad_down_ref.at[0], land, down_send.at[index], down_recv.at[index],
+                {"context": giver},
+            ).wait_recv()
+
+
+def experts(rows, grads, gates, wide_full, down_full, context, owners, number):
     width = rows.shape[-1]
     slots = rows.size // width
     hidden = wide_full.shape[2]
-    per_row = pl.BlockSpec(rows.shape, lambda t: (0,) * rows.ndim)
-    column = pl.BlockSpec((slots, 1), lambda t: (0, 0))
-    wide = pl.BlockSpec((2, width, HIDDEN_TILE), lambda t: (0, 0, t))
-    tall = pl.BlockSpec((HIDDEN_TILE, width), lambda t: (t, 0))
+    blocks = (context // 2, hidden // (context // 2), width)
     return pl.pallas_call(
-        expert_kernel,
-        grid=(hidden // HIDDEN_TILE,),
+        functools.partial(expert_kernel, context, owners),
         out_shape=(
             jax.ShapeDtypeStruct(rows.shape, BF16),
             jax.ShapeDtypeStruct(rows.shape, BF16),
             jax.ShapeDtypeStruct((slots, 1), F32),
             jax.ShapeDtypeStruct(wide_full.shape, BF16),
-            jax.ShapeDtypeStruct(down_full.shape, BF16),
+            jax.ShapeDtypeStruct(blocks, BF16),
         ),
-        in_specs=[per_row, per_row, column, wide, tall],
-        out_specs=(per_row, per_row, column, wide, tall),
+        in_specs=vmem(3) + hbm(2),
+        out_specs=vmem(4) + hbm(1),
         scratch_shapes=[
+            pltpu.VMEM(wide_full.shape, BF16),
+            pltpu.VMEM(down_full.shape, BF16),
             pltpu.VMEM((width, slots), BF16),
             pltpu.VMEM((slots, width), BF16),
             pltpu.VMEM((slots, width), F32),
             pltpu.VMEM((slots, width), F32),
+            pltpu.VMEM(blocks, BF16),
+            pltpu.SemaphoreType.DMA((2,)),
+            pltpu.SemaphoreType.DMA((context // 2,)),
+            pltpu.SemaphoreType.DMA((context // 2,)),
         ],
-        compiler_params=params(),
+        compiler_params=params(number),
         cost_estimate=cost(37),
         name="experts",
     )(rows, grads, gates, wide_full, down_full)
 
 
 def dispatch_kernel(
-    context, roles,
-    gates_ref, rows_ref, grad_ref, down_ref,
-    gates_all, rows_all, grad_all, down_all,
-    gates_stage, rows_stage,
+    context, roles, square,
+    gates_ref, rows_ref, down_ref,
+    gates_all, rows_all, down_all,
+    rows_stage,
     local_sem, send_sem, recv_sem, pass_sem, land_sem, twin_sem, come_sem, relay_sem, reach_sem,
-    down_send, down_recv,
+    down_send, down_recv, down_on,
 ):
     owners = rows_ref.shape[0]
     chips = context // 2
@@ -664,7 +1016,7 @@
     slot = chip // (chips // roles)
     other = (roles - 1) - slot
     twin = {"context": 2 * lax.rem(chip + chips // 2, chips) + core}
-    sent, others, local, passed, lent, relayed = {}, {}, [], [], {}, []
+    sent, local, passed, lent, relayed = {}, [], [], {}, []
     for far in range(1, owners):
         peer = lax.rem(row + far, owners)
         pairs = [
@@ -681,7 +1033,6 @@
     own = (
         (gates_ref.at[row], gates_all.at[slot, core, row]),
         (rows_ref.at[row, slot], rows_all.at[slot, core, row]),
-        (grad_ref.at[:, slot], grad_all.at[slot, core]),
     )
     for item, (source, target) in enumerate(own):
         local.append(pltpu.make_async_copy(source, target, local_sem.at[item]))
@@ -694,7 +1045,6 @@
         own = (
             (gates_ref.at[row], gates_all.at[slot, core, row], gates_all.at[other, core, row]),
             (rows_ref.at[row, other], rows_all.at[slot, core, row], rows_all.at[other, core, row]),
-            (grad_ref.at[:, other], grad_all.at[slot, core], grad_all.at[other, core]),
         )
         for item, (source, target, arriving) in enumerate(own):
             lent[item, 0] = (
@@ -704,20 +1054,18 @@
 
     half = place // chips
     down_rows = down_ref.shape[1]
-    spot = down_all.at[span(lax.rem(place, chips), down_rows), :]
+    index = lax.rem(place, chips)
+    spot = down_all.at[span(index, down_rows), :]
 
     def down_copy(far, here):
-        to_chip = lax.rem(chip + far, chips)
+        to_chip = chip_at(chip, far, chips, square)
         source = down_ref.at[to_chip // (chips // roles)]
         if here:
-            return pltpu.make_async_copy(source, spot, down_recv.at[lax.rem(place, chips)])
+            return pltpu.make_async_copy(source, spot, down_recv.at[index])
         return remote(
-            source, spot, down_send.at[far], down_recv.at[lax.rem(place, chips)],
+            source, spot, down_send.at[far], down_recv.at[index],
             {"context": 2 * to_chip + half},
         )
-
-    for far in range(1, chips):
-        down_copy(far, False).start()
 
     @pl.when(half == core)
     def _():
@@ -726,6 +1074,35 @@
     @pl.when(half != core)
     def _():
         down_copy(0, False).start()
+
+    fars = [1, 2] if square else list(range(1, chips))
+    for far in fars:
+        down_copy(far, False).start()
+
+    def arrival(number):
+        land = down_all.at[span(number, down_rows), :]
+        giver = core * chips + number
+
+        @pl.when(giver == place)
+        def _():
+            pltpu.make_async_copy(down_ref.at[0], land, down_recv.at[number]).wait()
+
+        @pl.when(giver != place)
+        def _():
+            remote(
+                down_ref.at[0], land, down_send.at[0], down_recv.at[number], {"context": giver}
+            ).wait_recv()
+
+    def onward(number):
+        land = down_all.at[span(number, down_rows), :]
+        return remote(
+            land, land, down_on.at[number], down_recv.at[number],
+            {"context": 2 * chip_at(chip, 1, chips, square) + core},
+        )
+
+    def from_below(number):
+        giver = core * chips + number
+        return giver // 2 == chip_at(chip, 2, chips, square)
 
     for far in range(1, owners):
         peer = lax.rem(row + owners - far, owners)
@@ -746,6 +1123,14 @@
                     arriving,
                 )
                 lent[item, far][0].start()
+        if square and far == 1:
+            for number in range(chips):
+
+                @pl.when(from_below(number))
+                def _():
+                    arrival(number)
+                    onward(number).start()
+
     for (item, far), (copy, arriving) in lent.items():
         copy.wait_recv()
         relayed.append(
@@ -760,52 +1145,51 @@
         copy.wait_send()
     for copy in local + passed + relayed:
         copy.wait()
-    for far in range(1, chips):
+    for far in fars:
         down_copy(far, False).wait_send()
 
     @pl.when(half != core)
     def _():
         down_copy(0, False).wait_send()
 
-    for index in range(chips):
-        giver = core * chips + index
-        land = down_all.at[span(index, down_rows), :]
-
-        @pl.when(giver == place)
-        def _():
-            pltpu.make_async_copy(down_ref.at[0], land, down_recv.at[index]).wait()
-
-        @pl.when(giver != place)
-        def _():
-            remote(
-                down_ref.at[0], land, down_send.at[0], down_recv.at[index], {"context": giver}
-            ).wait_recv()
-
-
-def dispatch(gates, rows, grads, down_weight, context, roles, number):
+    for number in range(chips):
+        if square:
+
+            @pl.when(from_below(number))
+            def _():
+                onward(number).wait_send()
+
+            @pl.when(jnp.logical_not(from_below(number)))
+            def _():
+                arrival(number)
+
+        else:
+            arrival(number)
+
+
+def dispatch(gates, rows, down_weight, context, roles, number):
     owners, _, cap, width = rows.shape
     chips = context // 2
     down_rows = down_weight.shape[1]
+    square = chips == 4 and roles == 2
     return pl.pallas_call(
-        functools.partial(dispatch_kernel, context, roles),
+        functools.partial(dispatch_kernel, context, roles, square),
         out_shape=(
             jax.ShapeDtypeStruct((roles, 2) + gates.shape, gates.dtype),
             jax.ShapeDtypeStruct((roles, 2, owners, cap, width), BF16),
-            jax.ShapeDtypeStruct((roles, 2, owners, cap, width), BF16),
             jax.ShapeDtypeStruct((chips * down_rows, width), BF16),
         ),
-        in_specs=vmem(3) + hbm(1),
-        out_specs=vmem(3) + hbm(1),
+        in_specs=vmem(2) + hbm(1),
+        out_specs=vmem(2) + hbm(1),
         scratch_shapes=[
-            pltpu.VMEM(gates.shape, gates.dtype),
             pltpu.VMEM((owners, cap, width), BF16),
-            pltpu.SemaphoreType.DMA((3,)),
+            pltpu.SemaphoreType.DMA((2,)),
         ]
         + [pltpu.SemaphoreType.DMA((3, owners))] * 8
-        + [pltpu.SemaphoreType.DMA((chips,))] * 2,
+        + [pltpu.SemaphoreType.DMA((chips,))] * 3,
         compiler_params=params(number),
         name="dispatch",
-    )(gates, rows, grads, down_weight)
+    )(gates, rows, down_weight)
 
 
 def collect_kernel(
@@ -944,110 +1328,9 @@
     )(dots, grads, outs)
 
 
-def granule_kernel(ranks, shard_granules, outward, source_ref, target_ref, send_sem, recv_sem):
-    place = lax.axis_index("context")
-    context = lax.axis_size("context")
-    group, rank = place // ranks, lax.rem(place, ranks)
-    groups = context // ranks
-    owned = context * shard_granules // ranks
-    barrier = pltpu.get_barrier_semaphore()
-    for far in range(1, context):
-        pl.semaphore_signal(
-            barrier, inc=1, device_id={"context": lax.rem(place + far, context)},
-            device_id_type=pl.DeviceIdType.MESH,
-        )
-    pl.semaphore_wait(barrier, context - 1)
-
-    def owner_rank(granule):
-        spot = lax.rem(granule // 2, 2 * ranks)
-        return jnp.minimum(spot, 2 * ranks - 1 - spot)
-
-    def owner_slot(granule):
-        tile = granule // 2
-        spot = lax.rem(tile, 2 * ranks)
-        upper = jnp.where(spot >= ranks, 1, 0)
-        return (tile // (2 * ranks) * 2 + upper) * 2 + lax.rem(granule, 2)
-
-    def granule_of(slot):
-        return own_tile(slot // 2, ranks) * 2 + lax.rem(slot, 2)
-
-    def remote(source, target, index, device):
-        return pltpu.make_async_remote_copy(
-            src_ref=source, dst_ref=target, send_sem=send_sem.at[index],
-            recv_sem=recv_sem.at[index], device_id={"context": device},
-            device_id_type=pl.DeviceIdType.MESH,
-        )
-
-    def outgoing(step):
-        if outward:
-            granule = granule_of(step)
-            home = granule // shard_granules
-            slot = group * shard_granules + lax.rem(granule, shard_granules)
-            return home, source_ref.at[step], slot
-        other, spot = step // shard_granules, step % shard_granules
-        granule = place * shard_granules + spot
-        return other * ranks + owner_rank(granule), source_ref.at[step], owner_slot(granule)
-
-    def incoming(step):
-        if outward:
-            other, spot = step // shard_granules, step % shard_granules
-            return other * ranks + owner_rank(place * shard_granules + spot)
-        return granule_of(step) // shard_granules
-
-    for step in range(owned):
-        device, source, slot = outgoing(step)
-
-        @pl.when(device == place)
-        def _():
-            pltpu.make_async_copy(source, target_ref.at[slot], recv_sem.at[slot]).start()
-
-        @pl.when(device != place)
-        def _():
-            pltpu.make_async_remote_copy(
-                src_ref=source, dst_ref=target_ref.at[slot], send_sem=send_sem.at[step],
-                recv_sem=recv_sem.at[slot], device_id={"context": device},
-                device_id_type=pl.DeviceIdType.MESH,
-            ).start()
-
-    for step in range(owned):
-        device, source, slot = outgoing(step)
-
-        @pl.when(device != place)
-        def _():
-            remote(source, target_ref.at[slot], step, device).wait_send()
-
-        sender = incoming(step)
-
-        @pl.when(sender == place)
-        def _():
-            pltpu.make_async_copy(source_ref.at[0], target_ref.at[step], recv_sem.at[step]).wait()
-
-        @pl.when(sender != place)
-        def _():
-            remote(source_ref.at[0], target_ref.at[step], step, sender).wait_recv()
-
-
-def granules(rows, ranks, shard_granules, outward, number):
-    owned = rows.shape[0]
-    return pl.pallas_call(
-        functools.partial(granule_kernel, ranks, shard_granules, outward),
-        out_shape=jax.ShapeDtypeStruct(rows.shape, rows.dtype),
-        in_specs=vmem(1),
-        out_specs=vmem(1)[0],
-        scratch_shapes=[
-            pltpu.SemaphoreType.DMA((owned,)),
-            pltpu.SemaphoreType.DMA((owned,)),
-        ],
-        compiler_params=pltpu.CompilerParams(
-            collective_id=number, has_side_effects=True, vmem_limit_bytes=60 << 20
-        ),
-        name="granules",
-    )(rows)
-
-
 def finish_kernel(
     chips, owners, groups,
-    da_ref, pieces_ref, small_ref, output_ref,
+    da_ref, pieces_ref, small_ref,
     total_ref, sums_ref, small_all_ref,
     da_twin, da_sum, da_in, w_twin, w_sum, w_in, s_twin, s_sum, s_in, s_total,
     stack_ref, shares, shares_in, block_ref,
@@ -1097,7 +1380,9 @@
         pair[0, far].wait_recv()
         s_sum[peer] = small_ref[mine] + s_twin[peer]
         pair[1, far].wait_recv()
-        w_sum[peer] = (pieces_ref[mine] + w_twin[peer]).astype(BF16)
+        w_sum[peer] = (
+            pieces_ref[mine].astype(F32) + w_twin[peer].astype(F32)
+        ).astype(BF16)
     moved = {}
     for far in range(1, chips):
         moved[0, far] = across(0, s_sum, s_in, far)
@@ -1132,10 +1417,6 @@
             stack_ref[which * shard : (which + 1) * shard, group * width : (group + 1) * width] = (
                 total[which * width : (which + 1) * width].T
             )
-    total = output_ref[0].astype(F32)
-    for other in range(1, output_ref.shape[0]):
-        total = total + output_ref[other].astype(F32)
-    stack_ref[3 * shard :, :] = total
     lines = shares.shape[1]
     for owner in range(owners):
         shares[owner] = stack_ref[owner * lines : (owner + 1) * lines, :].astype(BF16)
@@ -1186,12 +1467,12 @@
         copy.wait_send()
 
 
-def finish(da, pieces, small, output_parts, owners, groups, number):
+def finish(da, pieces, small, owners, groups, number):
     context, tokens, width = da.shape
     chips = context // 2
     lines, shard = pieces.shape[1:]
     few = small.shape[1]
-    stack = 4 * shard
+    stack = 3 * shard
     block = (stack // owners, width)
     return pl.pallas_call(
         functools.partial(finish_kernel, chips, owners, groups),
@@ -1200,13 +1481,13 @@
             jax.ShapeDtypeStruct((owners,) + block, BF16),
             jax.ShapeDtypeStruct((owners, few, shard), F32),
         ),
-        in_specs=vmem(4),
+        in_specs=vmem(3),
         out_specs=vmem(3),
         scratch_shapes=[
             pltpu.VMEM((chips, tokens, width), BF16),
             pltpu.VMEM((chips, tokens, width), BF16),
             pltpu.VMEM((chips, tokens, width), BF16),
-            pltpu.VMEM((chips, lines, shard), F32),
+            pltpu.VMEM((chips, lines, shard), BF16),
             pltpu.VMEM((chips, lines, shard), BF16),
             pltpu.VMEM((chips, lines, shard), BF16),
             pltpu.VMEM((chips, few, shard), F32),
@@ -1228,7 +1509,7 @@
             collective_id=number, has_side_effects=True, vmem_limit_bytes=60 << 20
         ),
         name="finish",
-    )(da, pieces, small, output_parts)
+    )(da, pieces, small)
 
 
 def shards(
@@ -1304,18 +1585,14 @@
         return jnp.dot(pick_either, rows, preferred_element_type=F32).astype(BF16).reshape(blocks)
 
     (
-        attn_out, out_t, log_total, query_t, key_heads, key_t, value_heads,
-        a_full, ids, weights_t, output_full, wide_full, grad_arrived,
+        out_t, log_total, query_t, ids, weights_t, key_heads, key_t, value_heads,
+        a_full, mix_granules, output_full, wide_full, grad_arrived, _,
     ) = attn_forward(
         ids_wide, pieces, attn_input, cos_t, sin_t, pick(cotangent_low),
         output_weight, gate_weight, up_weight, heads, head_size, ranks, context, roles, 0,
     )
     kept = (out_t, log_total, query_t, key_heads, key_t, value_heads)
-    granule = TILE // 2
-    shard_granules = token_rows // granule
-    out_blocks = granules(
-        attn_out.reshape(-1, granule, width), ranks, shard_granules, True, 1
-    ).reshape(groups, token_rows, width)
+    out_blocks = mix_granules.reshape(groups, token_rows, width)
     mix_low = jnp.transpose(out_blocks, (1, 0, 2)).reshape(token_rows, model_width)
 
     after_attn = residual + jnp.dot(mix_low, output_full, preferred_element_type=F32)
@@ -1348,15 +1625,14 @@
         values = values.reshape(owners, per_owner, CAP)
         return jnp.pad(values, ((0, 0), (0, 8 - per_owner), (0, 128 - CAP)))
 
-    gates, arrived, grad_arrived, down_full = dispatch(
-        spread(slot_gate), pick(moe_input.astype(BF16)), grad_arrived, down_weight,
-        context, roles, 2,
+    gates, arrived, down_full = dispatch(
+        spread(slot_gate), pick(moe_input.astype(BF16)), down_weight, context, roles, 2
     )
     role = lax.axis_index("context") // 2 // (context // 2 // roles)
     gates = lax.dynamic_index_in_dim(gates, role, 3, keepdims=False)[..., :CAP].reshape(-1, 1)
 
-    expert_out, grad_rows, owner_dot, grad_wide, grad_down = experts(
-        arrived, grad_arrived, gates, wide_full, down_full
+    expert_out, grad_rows, owner_dot, grad_wide, down_parts = experts(
+        arrived, grad_arrived, gates, wide_full, down_full, context, owners, 7
     )
     owner_dot = jnp.pad(
         owner_dot.reshape(roles, 2, owners, 1, CAP), ((0, 0),) * 3 + ((0, 7), (0, 128 - CAP))
@@ -1448,35 +1724,35 @@
         grad_attn_low, output_full, (((1,), (1,)), ((), ())), preferred_element_type=F32
     ).astype(BF16)
     grad_pieces = jnp.transpose(grad_mix_low.reshape(token_rows, groups, width), (1, 0, 2))
-    grad_own = granules(
-        grad_pieces.reshape(-1, granule, width), ranks, shard_granules, False, 4
-    ).reshape(-1, width)
+    grad_own = grad_pieces.reshape(-1, TILE // 2, width)
     grad_output_local = lax.dot_general(
         mix_low, grad_attn_low, (((0,), (0,)), ((), ())), preferred_element_type=F32
     ).astype(BF16)
-    da_part, w_pieces, wide_parts, down_parts, returned, output_parts = attn_backward(
+    da_part, w_pieces, output_sum, wide_parts, returned = attn_backward(
         grad_own, a_full, weights_t, cos_t, sin_t, ids, kept,
-        grad_wide, grad_down, expert_out, grad_output_local,
+        grad_wide, expert_out, grad_output_local,
         heads, head_size, ranks, context, roles, 6,
     )
     returned = returned.reshape(slot_count, model_width)
     same = context // 2 // roles
     wide_parts = wide_parts.reshape(roles, same, 2, 2, shard_width, -1)
-    wide_sum = jnp.sum(wide_parts.astype(F32), axis=1)
-    wide_sum = jnp.transpose(wide_sum, (2, 0, 3, 1, 4)).reshape(2, roles, shard_width, -1)
+
+    def whole(which):
+        total = jnp.sum(wide_parts[:, :, :, which].astype(F32), axis=1)
+        return jnp.concatenate([total[:, 0], total[:, 1]], axis=-1)
+
     down_sum = jnp.sum(
         down_parts.reshape(roles, same, -1, model_width).astype(F32), axis=1
     )
     grad_attn_input, sums, small_all = finish(
-        da_part.reshape(context, token_rows, model_width), w_pieces, small, output_parts,
+        da_part.reshape(context, token_rows, model_width), w_pieces, small,
         owners, groups, 5,
     )
     grad_normed_one = grad_attn_input * attn_gain
     grad_input = grad_after + inv_rms1 * (
         grad_normed_one - normed_one * jnp.mean(grad_normed_one * normed_one, axis=1, keepdims=True)
     )
-    sums = sums.astype(F32).reshape(4, shard_width, model_width)
-    w_sum, output_sum = sums[:3], sums[3]
+    w_sum = sums.astype(F32).reshape(3, shard_width, model_width)
     small_own = jnp.sum(small_all, axis=0)
     grad_attn_gain = jnp.sum(
         w_sum[0] * query_weight.astype(F32)
@@ -1512,8 +1788,8 @@
         grad_prior_weight,
         small_own[expert_count:mixes].reshape(consts, 2, shard_width),
         small_own[mixes : mixes + consts],
-        wide_sum[0],
-        wide_sum[1],
+        whole(0),
+        whole(1),
         down_sum,
     )
 

time: 444 us -> 401 us (0.903)
  Pallas kernels: 369 us -> 331 us
  local copies, waits for them, and re-layouts: 26.6 us -> 17.2 us
    pallas_call x4 -> x2, Pallas kernels: 117 us -> 79.5 us  [the longest x1 42.6 us: experts(): pl.pallas_call(functools.partial(expert_kernel, context, owners), out_sha...]
    squeeze x3 -> x1, local copies, waits for them, and re-layouts: 5.72 us -> 0.34 us  [whole(): return jnp.concatenate([total[:, 0], total[:, 1]], axis=-1)]
    slice x5 -> x2, local copies, waits for them, and re-layouts: 5.5 us -> 0.21 us  [the longest x2 4.08 us: shards(): wide_sum[1]]
    pallas_call x1, Pallas kernels: 84.8 us -> 89.6 us  [attn_forward(): pl.pallas_call(functools.partial(attn_forward_kernel, dims), out_shape=sh...]
    pallas_call x1, Pallas kernels: 57 us -> 52.5 us  [finish(): pl.pallas_call(functools.partial(finish_kernel, chips, owners, groups), o...]
where the time goes in v4:
time: 401 us; the launch traced here: 394 us
  Pallas kernels  331 us (83%)
  other arithmetic  25 us (6%)
  matrix products  18.6 us (5%)
  local copies, waits for them, and re-layouts  17.2 us (4%)
    pallas_call x1, Pallas kernels, attn_forward(): pl.pallas_call(functools.partial(attn_forward_kernel, dims), out_shape=sh...  89.6 us
    pallas_call x1, Pallas kernels, attn_backward(): pl.pallas_call(functools.partial(attn_backward_kernel, dims), out_shape=s...  72.6 us
    pallas_call x1, Pallas kernels, finish(): pl.pallas_call(functools.partial(finish_kernel, chips, owners, groups), o...  52.5 us
    pallas_call x1, Pallas kernels, experts(): pl.pallas_call(functools.partial(expert_kernel, context, owners), out_sha...  42.6 us
    pallas_call x1, Pallas kernels, dispatch(): pl.pallas_call(functools.partial(dispatch_kernel, context, roles, square)...  36.9 us
    pallas_call x1, Pallas kernels, collect(): pl.pallas_call(functools.partial(collect_kernel, context, roles), out_sha...  36.8 us

profile of v4, /device:TPU:0, one launch (start us, length us, event | category | flops | bytes accessed | tf_op | source)
XLA Modules:
  0.0 393.8 jit_solution(12388906915805569133)
XLA Ops:
  0.7 0.9 copy.114
  1.7 1.7 reduce-window.6
  4.1 0.2 reduce_sum.220
  4.4 0.3 slice_reduce_fusion.3
  4.6 1.9 convolution_convert_fusion.2
  6.5 2.3 multiply_sine_fusion
  8.8 0.2 fusion.14
  9.0 1.0 fusion.8.input_ref
  10.3 0.2 copy.135
  10.6 1.0 pad_maximum_fusion.2
  11.6 0.6 broadcast_in_dim.102.ids_ref
  12.2 89.6 %attn_forward.1 = (f32[192,1536]{1,0:T(8,128)}, f32[3,1536]{1,0:T(4,128)}, bf16[192,1536]{1,0:T(8,128)(2,1)}, f32[8,3072]{1,0:T(8,128)}, bf16[576,768]{1,0:T(8,1...) custom-call(f32[8,384]{1,0:T(8,128)} %broadcast_in_dim.102.ids_ref, ...), custom_call_target="tpu_custom_call" | custom-call | flops 92000002048 | tf_op jit(solution)/shard_map/attn_forward/pallas_call | solution.py:593
  101.8 1.5 copy.119
  103.3 2.1 multiply_reduce_fusion.2
  105.4 1.3 fusion.23
  106.7 0.2 fusion.73
  107.0 0.3 slice_reduce_fusion.1
  107.3 0.3 add_reduce_fusion
  107.7 0.6 pad.16.gates_ref
  108.3 1.9 convolution_convert_fusion.1
  110.3 36.9 %dispatch.1 = (f32[2,2,4,8,128]{4,3,2,1,0:T(8,128)}, bf16[2,2,4,96,768]{4,3,2,1,0:T(8,128)(2,1)}, bf16[1024,768]{1,0:T(8,128)(2,1)}) custom-call(f32[4,8,128]{2,1,0:T(8,128)} %pad.16.gates_ref, bf16[4,2,96,768]{3,2,1,0:T(8,128)(2,1)} %bitcast.154, bf16[2,256,768]{2,1,0:T(8,128)(2,1)} %down_ref.1), custom_call_target="tpu_custom_call" | custom-call | tf_op jit(solution)/shard_map/dispatch/pallas_call | solution.py:1175
  147.2 0.9 constant_dynamic-slice_fusion
  148.1 1.6 reshape.225.prob_ref
  149.6 42.6 %experts.1 = (bf16[2,2,4,96,768]{4,3,2,1,0:T(8,128)(2,1)}, bf16[2,2,4,96,768]{4,3,2,1,0:T(8,128)(2,1)}, f32[1536,1]{1,0:T(8,128)}, bf16[2,768,1024]{2,1,0:T(8,128)(2,1)}, bf16[4,256,768]{2,1,0:T(8,128)(2,1)}) custom-call(bf16[2,2,4,96,768]{4,3,2,1,0:T(8,128)(2,1)} %get-tuple-element.50.rows_ref, bf16[2,2,4,96,768]{4,3,2,1,0:T(8,128)(2,1)} %get-tuple-element.51.grad_ref, ...), custom_call_target="tpu_custom_call" | custom-call | flops 42550001664 | tf_op jit(solution)/shard_map/experts/pallas_call | solution.py:974
  192.3 1.4 reduce.16
  193.7 0.7 pad.17.dots_ref
  194.4 36.8 %collect.1 = (f32[4,2,8,128]{3,2,1,0:T(8,128)}, bf16[4,2,96,768]{3,2,1,0:T(8,128)(2,1)}, bf16[4,2,96,768]{3,2,1,0:T(8,128)(2,1)}) custom-call(f32[2,2,4,8,128]{4,3,2,1,0:T(8,128)} %pad.17.dots_ref, bf16[2,2,4,96,768]{4,3,2,1,0:T(8,128)(2,1)} %get-tuple-element.56.grad_ref, bf16[2,2,4,96,768]{4,3,2,1,0:T(8,128)(2,1)} %get-tuple-element.57.out_ref), custom_call_target="tpu_custom_call" | custom-call | tf_op jit(solution)/shard_map/collect/pallas_call | solution.py:1302
  231.2 0.8 slice_reduce_fusion.4
  232.1 0.4 select_reduce_fusion.1
  232.6 0.9 fusion.16
  233.8 0.6 fusion.20
  234.5 1.1 fusion.48
  235.8 1.0 multiply_reduce_fusion
  236.8 0.3 convert_add_fusion
  237.2 1.8 convolution_convert_fusion.output_ref
  239.0 0.7 convolution_convert_fusion.3
  239.7 0.3 copy.126
  240.0 1.2 copy.127
  241.2 72.6 %attn_backward.1 = (bf16[3072,768]{1,0:T(8,128)(2,1)}, bf16[8,576,96]{2,1,0:T(8,128)(2,1)}, f32[96,768]{1,0:T(8,128)}, bf16[8,2,96,1024]{3,2,1,0:T(8,128)(2,1)}, bf16[4,2,96,768]{3,2,1,0:T(8,128)(2,1)}) custom-call(bf16[12,128,192]{2,1,0:T(8,128)(2,1)} %bitcast.158, bf16[3072,768]{1,0:T(8,128)(2,1)} %get-tuple-element.60.a_ref, ...), custom_call_target="tpu_custom_call" | custom-call | flops 69000003584 | tf_op jit(solution)/shard_map/attn_backward/pallas_call | solution.py:833
  313.8 3.1 convert_reduce_fusion.1
  316.9 0.3 slice_bitcast_fusion.1
  317.2 1.2 pad_maximum_fusion.1
  318.5 1.2 pad_maximum_fusion
  319.7 0.6 copy-done.2
  320.3 0.8 fusion.21
  321.3 0.3 copy.128
  321.6 0.8 fusion.63
  322.9 0.7 fusion.47.small_ref
  323.6 52.5 %finish.1 = (f32[384,768]{1,0:T(8,128)}, bf16[4,72,768]{2,1,0:T(8,128)(2,1)}, f32[4,24,96]{2,1,0:T(8,128)}) custom-call(bf16[8,384,768]{2,1,0:T(8,128)(2,1)} %bitcast.148, bf16[8,576,96]{2,1,0:T(8,128)(2,1)} %get-tuple-element.73.pieces_ref, f32[8,24,96]{2,1,0:T(8,128)} %fusion.47.small_ref), custom_call_target="tpu_custom_call" | custom-call | tf_op jit(solution)/shard_map/finish/pallas_call | solution.py:1477
  376.2 1.1 convert.4
  377.4 1.0 add_reduce_fusion.1
  378.4 0.6 dynamic-slice_divide_fusion
  379.0 1.6 fusion.9
  380.7 2.6 fusion.13
  383.3 0.6 fusion.72
  383.9 0.7 slice.147
  384.6 0.6 slice_bitcast_fusion.7
  385.2 0.6 slice.182
  385.8 0.5 slice_bitcast_fusion.10
  386.3 2.6 fusion.4
  388.9 1.5 fusion.7
  390.6 0.6 copy.133
  391.2 1.4 convert_reduce_fusion
  392.6 0.7 copy.162
  (119 shorter events, 3.1 us)
Async XLA Ops:
  0.6 106.1 %copy-start = (f32[12,12]{1,0:T(8,128)S(1)}, f32[12,12]{1,0:T(8,128)}, u32[]{:S(2)}) copy-start(f32[12,12]{1,0:T(8,128)} %param.30) | copy-start | bytes 1732
  0.7 3.9 %copy-start.5 = (bf16[1,384,768]{2,1,0:T(8,128)(2,1)S(1)}, bf16[1,384,768]{2,1,0:T(8,128)(2,1)}, u32[]{:S(2)}) copy-start(bf16[1,384,768]{2,1,0:T(8,128)(2,1)} %param.22) | copy-start | bytes 1769476
  4.6 4.2 %copy-start.6 = (bf16[1,384,768]{2,1,0:T(8,128)(2,1)S(1)}, bf16[1,384,768]{2,1,0:T(8,128)(2,1)}, u32[]{:S(2)}) copy-start(bf16[1,384,768]{2,1,0:T(8,128)(2,1)} %param.18) | copy-start | bytes 1769476
  6.5 2.6 copy-start.21
  6.5 3.6 copy-start.14
  8.8 1.4 copy-start.12
  8.8 1.6 copy-start.10
  9.0 1.2 copy-start.23
  10.1 1.5 copy-start.27
  103.3 2.1 copy-start.26
  103.3 2.1 copy-start.17
  103.3 2.1 copy-start.19
  105.4 131.4 %copy-start.1 = (f32[384,768]{1,0:T(8,128)}, f32[384,768]{1,0:T(8,128)S(1)}, u32[]{:S(2)}) copy-start(f32[384,768]{1,0:T(8,128)S(1)} %get-tuple-element.202) | copy-start | bytes 3538948
  105.4 1.4 copy-start.18
  194.4 38.2 %copy-start.25 = (f32[2,768]{1,0:T(2,128)S(1)}, f32[2,768]{1,0:T(2,128)}, u32[]{:S(2)}) copy-start(f32[2,768]{1,0:T(2,128)} %param.32) | copy-start | bytes 18436
  234.5 1.3 copy-start.28
  237.2 1.8 copy-start.3
  237.2 1.8 copy-start.9
  318.5 1.8 copy-start.2
  376.1 1.2 copy-start.11
  376.1 1.2 copy-start.13
  376.2 1.2 copy-start.15
  377.3 1.1 copy-start.22
  377.3 1.7 copy-start.7
  377.4 1.7 copy-start.24
  378.4 2.2 copy-start.4
  380.7 2.7 copy-start.20
  386.3 2.6 copy-start.29
  388.9 2.4 copy-start.8
  391.2 1.4 copy-start.16
